TPU v7x, 512 devices: a whole 4x8x8 slice. The times are simulated.
512 devices in a mesh: dp: 16 (over z, core), fsdp: 32 (over x, y).
Axes of the slice: x: 4, y: 8, z: 8, core: 2. Of those that a mesh axis runs over, the one named last changes fastest.
Arguments:
- passages: bfloat16 [16, 32, 40, 8, 2048], P('dp', 'fsdp'), may hold values from -6 to 6
- counts: int32 [16, 32], P('dp', 'fsdp'), may hold values from 1 to 40, as said below
- helper_table: int32 [16, 32, 2, 32], P('dp', 'fsdp'), may hold values from -1 to 31, as said below
- norm_gain: float32 [2048], replicated, may hold values from 0.1 to 1.9
- projection: bfloat16 [2048, 2048], P('fsdp'), may hold values from -0.125 to 0.125
- queries: bfloat16 [16, 32, 16, 1024], P('dp', 'fsdp'), may hold values from -140 to 140
- cotangent: bfloat16 [16, 32, 24, 8, 2048], P('dp', 'fsdp'), may hold values from -0.0234375 to 0.0234375
Outputs:
- context: bfloat16 [16, 32, 16, 1024], P('dp', 'fsdp')
- gain_gradient: float32 [2048], P('fsdp')
Inputs may be any that keep to these rules, and one draw needn't show every extreme that they name: `counts`: A question with passages beyond the first 8 has 8 plus that many; some question of every group has 40. `helper_table`: entries at e are -1 exactly when 8 + e is not below the question's count; otherwise row 0 names a device of the same group and row 1 a slot from 0 to 15. No two passages of a group share a device and slot; some device of every group has all 16 slots taken; one question sends at most 1 passages to one device, and some question of every group sends exactly that many to some device.
All inputs are finite; a program needn't handle non-finite values.
Results may differ from a plain program's by a relative error of at most 0.0095.
The roundings to bfloat16 on the way count: a program that leaves them out, or rounds other values in their place, can miss the bound.
Values may be sent and summed in bfloat16 or wider, within the bound.
No kernel may reach another device: no remote copies, remote signals or barrier semaphores. Data moves between devices by JAX's collectives and lax.ppermute only.
A program may use at most 64 MiB of HBM per device.

v0:
```python
import jax
import jax.numpy as jnp
from jax import lax
from jax.sharding import Mesh
from jax.sharding import PartitionSpec as P

D = 2048
HEADS = 32
HEAD_DIM = 32
HW = 1024
DEC = 16
LEN = 8
PMAX = 40
KEEP = 8
HELP = 16
ENC = 24
DP = ("dp_0", "dp_1")


EPSILON = 1e-06


def cut_along(array, dim, peers):
    dims = array.shape
    parts = array.reshape(*dims[:dim], peers, dims[dim] // peers, *dims[dim + 1 :])
    return jnp.moveaxis(parts, dim, 0)


def sent_and_summed(array, axis, dim):
    peers = lax.axis_size(axis)
    parts = lax.all_to_all(cut_along(array, dim, peers), axis, 0, 0, tiled=True)
    return jnp.sum(parts, axis=0)


def by_axis(array, axes):
    for axis in axes:
        array = lax.psum(array, axis)
    return array


def normalize(states):
    values = states.astype(jnp.float32)
    scaling = lax.rsqrt(jnp.mean(values * values, axis=-1, keepdims=True) + EPSILON)
    return values * scaling


def rank_slots(helpers, alive_mask, peer_count, per_peer):
    onehot = (
        (helpers[:, None] == lax.iota(jnp.int32, peer_count)[None, :]) & alive_mask[:, None]
    ).astype(jnp.int32)
    before = jnp.cumsum(onehot, axis=0) - onehot
    ranking = jnp.sum(before * onehot, axis=1)
    target = helpers * per_peer + ranking
    places = lax.iota(jnp.int32, peer_count * per_peer)
    return (places[:, None] == target[None, :]) & alive_mask[None, :]


def shards(passages, counts, helper_table, norm_gain, projection, queries, cotangent):
    peer_count = lax.axis_size("fsdp")
    spare_slots = PMAX - KEEP
    per_peer = -(-spare_slots // peer_count)
    stored = passages.reshape(PMAX, LEN, D)
    passage_count = counts.reshape(())
    table_rows = helper_table.reshape(2, spare_slots)
    alive_mask = table_rows[0] >= 0
    selector = rank_slots(table_rows[0], alive_mask, peer_count, per_peer)
    select_matrix = selector.astype(jnp.bfloat16)
    outgoing = jnp.dot(
        select_matrix,
        stored[KEEP:].reshape(spare_slots, LEN * D),
        preferred_element_type=jnp.float32,
    ).astype(jnp.bfloat16)
    slot_tags = jnp.sum(jnp.where(selector, table_rows[1][None, :] + 1, 0), axis=1) - 1
    arrived, arrived_tags = (
        lax.all_to_all(
            outgoing.reshape(peer_count, per_peer, LEN * D),
            "fsdp",
            split_axis=0,
            concat_axis=0,
            tiled=True,
        ),
        lax.all_to_all(
            slot_tags.reshape(peer_count, per_peer), "fsdp", split_axis=0, concat_axis=0, tiled=True
        ),
    )
    pick_matrix = arrived_tags.reshape(-1)[None, :] == lax.iota(jnp.int32, HELP)[:, None]
    helped = jnp.dot(
        pick_matrix.astype(jnp.bfloat16),
        arrived.reshape(-1, LEN * D),
        preferred_element_type=jnp.float32,
    ).astype(jnp.bfloat16)
    encoded = jnp.concatenate([stored[:KEEP], helped.reshape(HELP, LEN, D)], axis=0)
    normal = normalize(encoded).reshape(ENC * LEN, D)
    scaled = (normal * norm_gain).astype(jnp.bfloat16)
    slot_alive = jnp.concatenate(
        [lax.iota(jnp.int32, KEEP) < passage_count, jnp.any(pick_matrix, axis=1)]
    )
    token_alive = jnp.repeat(slot_alive, LEN).astype(jnp.float32)
    upstream = cotangent.reshape(ENC * LEN, 2 * HW)
    weight_piece = lax.all_gather(projection, "fsdp", axis=0, tiled=True)
    partial_states = jnp.dot(scaled, weight_piece, preferred_element_type=jnp.float32)
    back_piece = lax.dot_general(
        upstream, weight_piece, (((1,), (1,)), ((), ())), preferred_element_type=jnp.float32
    )
    row_terms = jnp.dot(token_alive, normal * back_piece, precision=lax.Precision.HIGHEST)
    state_rows = partial_states.astype(jnp.bfloat16).reshape(ENC, LEN * 2 * HW)
    returning = jnp.dot(
        pick_matrix.T.astype(jnp.bfloat16), state_rows[KEEP:], preferred_element_type=jnp.float32
    ).astype(jnp.bfloat16)
    returned = lax.all_to_all(
        returning.reshape(peer_count, per_peer, LEN * 2 * HW),
        "fsdp",
        split_axis=0,
        concat_axis=0,
        tiled=True,
    )
    remote_states = jnp.dot(
        select_matrix.T, returned.reshape(-1, LEN * 2 * HW), preferred_element_type=jnp.float32
    ).astype(jnp.bfloat16)
    all_states = jnp.concatenate([state_rows[:KEEP], remote_states], axis=0).reshape(
        PMAX * LEN, 2, HEADS, HEAD_DIM
    )
    key_rows = all_states[:, 0]
    value_rows = all_states[:, 1]
    query_rows = queries.reshape(DEC, HEADS, HEAD_DIM)
    scores = jnp.einsum(
        "qhd,thd->hqt", query_rows, key_rows, preferred_element_type=jnp.float32
    ) * HEAD_DIM ** (-0.5)
    token_live = jnp.repeat(lax.iota(jnp.int32, PMAX) < passage_count, LEN)
    scores = jnp.where(token_live[None, None, :], scores, -jnp.inf)
    highest = jnp.max(scores, axis=-1, keepdims=True)
    raised = jnp.exp(scores - highest)
    weights = (raised / jnp.sum(raised, axis=-1, keepdims=True)).astype(jnp.bfloat16)
    context = jnp.einsum("hqt,thd->qhd", weights, value_rows, preferred_element_type=jnp.float32)
    context_out = context.astype(jnp.bfloat16).reshape(1, 1, DEC, HW)
    group_share = sent_and_summed(row_terms, "fsdp", 0)
    gradient = by_axis(group_share, DP)
    return (context_out, gradient)


def solution(mesh):
    split = Mesh(mesh.devices.reshape(8, 2, mesh.shape["fsdp"]), ("dp_0", "dp_1", "fsdp"))
    return jax.shard_map(
        shards,
        mesh=split,
        in_specs=(
            P(DP, "fsdp", None, None, None),
            P(DP, "fsdp"),
            P(DP, "fsdp", None, None),
            P(),
            P("fsdp", None),
            P(DP, "fsdp", None, None),
            P(DP, "fsdp", None, None, None),
        ),
        out_specs=(P(DP, "fsdp", None, None), P("fsdp")),
        check_vma=False,
    )
```

profile of v0, /device:TPU:1, one launch (start us, length us, event | category | flops | bytes accessed | tf_op | source)
XLA Modules:
  0.0 229.6 jit_solution(2594520575006294680)
XLA Ops:
  8.6 0.8 add_bitcast_fusion.1
  10.5 0.7 copy.33
  11.2 10.5 %all-to-all-start = ((s32[32,1,1]{2,1,0:T(1,128)}), s32[32,1,1]{2,1,0:T(1,128)S(1)}, u32[]{:S(2)}, u32[]{:S(2)}) async-start(s32[32,1,1]{2,1,0:T(1,128)} %copy.33), calls=%async_computation | async-start | bytes 32768 | tf_op jit(solution)/shard_map/all_to_all | solution.py:82
  23.3 1.4 reduce.2
  24.7 1.6 reshape.139
  26.3 4.0 %all-to-all-done = s32[32,1,1]{2,1,0:T(1,128)S(1)} async-done(((s32[32,1,1]{2,1,0:T(1,128)}), s32[32,1,1]{2,1,0:T(1,128)S(1)}, u32[]{:S(2)}, u32[]{:S(2)}) %all-to-all-start) | async-done | bytes 160 | tf_op jit(solution)/shard_map/all_to_all | solution.py:82
  30.3 5.4 %all-to-all-start.1 = ((bf16[32,2,8192]{2,1,0:T(2,128)(2,1)}), bf16[32,2,8192]{2,1,0:T(2,128)(2,1)}, u32[]{:S(2)}, u32[]{:S(2)}) async-start(bf16[32,2,8192]{2,1,0:T(2,128)(2,1)} %reshape.139), calls=%async_computation.1 | async-start | bytes 2097152 | tf_op jit(solution)/shard_map/all_to_all | solution.py:75
  37.4 31.5 %all-to-all-done.1 = bf16[32,2,8192]{2,1,0:T(2,128)(2,1)} async-done(((bf16[32,2,8192]{2,1,0:T(2,128)(2,1)}), bf16[32,2,8192]{2,1,0:T(2,128)(2,1)}, u32[]{:S(2)}, u32[]{:S(2)}) %all-to-all-start.1) | async-done | bytes 1048608 | tf_op jit(solution)/shard_map/all_to_all | solution.py:75
  69.0 4.3 %reshape.140 = bf16[32,1,16384]{2,1,0:T(2,128)(2,1)S(1)} reshape(bf16[32,2,8192]{2,1,0:T(2,128)(2,1)} %all-to-all-done.1) | data formatting | bytes 2097152
  73.3 1.2 convolution_convert_fusion.3
  75.1 55.0 %all-gather.2.cloned.1.call-done = bf16[2048,2048]{1,0:T(8,128)(2,1)} async-done(((bf16[64,2048]{1,0:T(8,128)(2,1)}), bf16[2048,2048]{1,0:T(8,128)(2,1)}) %all-gather.2.cloned.1.call-update) | async-done | bytes 8388624 | tf_op jit(solution)/shard_map/all_gather | solution.py:100
  130.1 5.2 %convolution_convert_fusion.4 = bf16[192,2048]{1,0:T(8,128)(2,1)S(1)} fusion(bf16[2048,2048]{1,0:T(8,128)(2,1)} %all-gather.2.cloned.1.call-done, f32[2048]{0:T(1024)S(1)} %copy-done.12, f32[192]{0:T(256)S(1)} %rsqrt.12, bf16[16,8,2048]{2,1,0:T(8,128)(2,1)S(1)} %bitcast.75, bf16[8,8,2048]{2,1,0:T(8,128)(2,1)S(1)} %slice_bitcast_fusion), kind=kOutput, calls=%fused_computation.9 | convolution fusion | flops 1612972032 | bytes 9970432 | tf_op jit(solution)/shard_map/dot_general | solution.py:101
  136.5 7.4 %fusion.3 = f32[2048,192]{0,1:T(8,128)} fusion(bf16[2048,2048]{1,0:T(8,128)(2,1)} %all-gather.2.cloned.1.call-done, bf16[1,1,24,8,2048]{4,3,2,1,0:T(8,128)(2,1)S(1)} %copy-done, f32[192]{0:T(256)S(1)} %rsqrt.12, bf16[16,8,2048]{2,1,0:T(8,128)(2,1)S(1)} %bitcast.76, bf16[8,8,2048]{2,1,0:T(8,128)(2,1)S(1)} %copy-done.4), kind=kOutput, calls=%fused_computation.8 | convolution fusion | flops 1612185600 | bytes 11535104 | tf_op jit(solution)/shard_map/dot_general | solution.py:102
  143.9 1.8 copy.40
  145.8 2.0 convolution_bitcast_fusion
  147.8 5.7 %all-to-all-start.3 = ((f32[32,1,64]{2,1,0:T(1,128)}), f32[32,1,64]{2,1,0:T(1,128)S(1)}, u32[]{:S(2)}, u32[]{:S(2)}) async-start(f32[32,1,64]{2,1,0:T(1,128)} %convolution_bitcast_fusion), calls=%async_computation.3 | async-start | bytes 32768 | tf_op jit(solution)/shard_map/all_to_all | solution.py:31
  153.9 1.4 reduce.3
  155.4 1.6 reshape.141
  157.0 4.9 %all-to-all-done.3 = f32[32,1,64]{2,1,0:T(1,128)S(1)} async-done(((f32[32,1,64]{2,1,0:T(1,128)}), f32[32,1,64]{2,1,0:T(1,128)S(1)}, u32[]{:S(2)}, u32[]{:S(2)}) %all-to-all-start.3) | async-done | bytes 8224 | tf_op jit(solution)/shard_map/all_to_all | solution.py:31
  161.8 4.7 %all-to-all-start.2 = ((bf16[32,2,8192]{2,1,0:T(2,128)(2,1)}), bf16[32,2,8192]{2,1,0:T(2,128)(2,1)}, u32[]{:S(2)}, u32[]{:S(2)}) async-start(bf16[32,2,8192]{2,1,0:T(2,128)(2,1)} %reshape.141), calls=%async_computation.2 | async-start | bytes 2097152 | tf_op jit(solution)/shard_map/all_to_all | solution.py:110
  167.6 15.5 %psum.14 = f32[64]{0:T(128)S(1)} all-reduce(f32[64]{0:T(128)S(1)} %reduce_sum.49), channel_id=1, replica_groups=mesh['dp_0'=8,'dp_1'=2,'fsdp'=32] {'dp_0'}, use_global_device_ids=true, to_apply=%region_8.9 | all-reduce | flops 64 | bytes 512 | tf_op jit(solution)/shard_map/psum | solution.py:37
  183.1 8.1 %psum.15 = f32[64]{0:T(128)} all-reduce(f32[64]{0:T(128)S(1)} %psum.14), channel_id=1, replica_groups=mesh['dp_0'=8,'dp_1'=2,'fsdp'=32] {'dp_1'}, use_global_device_ids=true, to_apply=%region_9.10 | all-reduce | flops 64 | bytes 512 | tf_op jit(solution)/shard_map/psum | solution.py:37
  191.2 4.3 %reshape.142 = bf16[32,1,16384]{2,1,0:T(2,128)(2,1)S(1)} reshape(bf16[32,2,8192]{2,1,0:T(2,128)(2,1)} %all-to-all-done.2) | data formatting | bytes 2097152
  195.5 1.4 convolution_convert_fusion
  197.1 5.4 %reshape.128 = bf16[320,2,32,32]{3,2,1,0:T(8,128)(2,1)} reshape(bf16[40,16384]{1,0:T(8,128)(2,1)S(1)} %pad_maximum_fusion) | data formatting | bytes 2621440 | tf_op jit(solution)/shard_map/reshape | solution.py:120
  202.5 5.0 %fusion.40 = (bf16[320,1,32,32]{3,2,1,0:T(8,128)(2,1)}, bf16[320,1,32,32]{3,2,1,0:T(8,128)(2,1)S(1)}) fusion(bf16[320,2,32,32]{3,2,1,0:T(8,128)(2,1)} %reshape.128), kind=kLoop, calls=%fused_computation.65 | loop fusion | bytes 2621440 | tf_op jit(solution)/shard_map/slice | solution.py:123
  207.4 5.1 %copy.45 = bf16[320,1,32,32]{0,3,2,1:T(8,128)(2,1)} copy(bf16[320,1,32,32]{3,2,1,0:T(8,128)(2,1)} %get-tuple-element.2) | data formatting | bytes 1310720
  212.5 1.4 fusion.11
  213.9 0.9 copy-done.2
  215.1 4.3 %copy.44 = bf16[320,1,32,32]{0,3,2,1:T(8,128)(2,1)} copy(bf16[320,1,32,32]{3,2,1,0:T(8,128)(2,1)S(1)} %get-tuple-element.3) | data formatting | bytes 1310720
  219.4 2.6 %fusion.12 = bf16[16,32,32]{2,0,1:T(8,128)(2,1)S(1)} fusion(bf16[320,1,32,32]{0,3,2,1:T(8,128)(2,1)} %copy.44, f32[32,16]{1,0:T(8,128)S(1)} %fusion.41, f32[32,16,320]{2,1,0:T(8,128)} %copy-done.2), kind=kOutput, calls=%fused_computation.23 | convolution fusion | flops 10994495 | bytes 1345536 | tf_op jit(solution)/shard_map/hqt,thd->qhd/dot_general | solution.py:134
  222.0 0.8 reshape.131
  (65 shorter events, 8.8 us)
Async XLA Ops:
  7.2 129.1 %copy-start = (bf16[1,1,24,8,2048]{4,3,2,1,0:T(8,128)(2,1)S(1)}, bf16[1,1,24,8,2048]{4,3,2,1,0:T(8,128)(2,1)}, u32[]{:S(2)}) copy-start(bf16[1,1,24,8,2048]{4,3,2,1,0:T(8,128)(2,1)} %param.13) | copy-start | bytes 2359300
  7.2 14.5 %slice-start = ((bf16[1,1,40,8,2048]{4,3,2,1,0:T(8,128)(2,1)}), bf16[1,1,32,8,2048]{4,3,2,1,0:T(8,128)(2,1)S(1)}, s32[]{:S(2)}) async-start(bf16[1,1,40,8,2048]{4,3,2,1,0:T(8,128)(2,1)} %param.7), calls=%async_computation.5 | async-start | bytes 2097152 | tf_op jit(solution)/shard_map/slice | solution.py:70
  7.2 122.9 %all-gather.2.cloned.1.call-start = ((), (), s32[]{:S(2)}) async-start(), calls=%async_computation.4 | async-start | bytes 8650752 | tf_op jit(solution)/shard_map/all_gather | solution.py:100
  8.6 13.7 %copy-start.7 = (pred[32]{0:T(512)(128)(4,1)}, pred[32]{0:T(512)(128)(4,1)S(1)}, u32[]{:S(2)}) copy-start(pred[32]{0:T(512)(128)(4,1)S(1)} %broadcast_compare_fusion) | copy-start | bytes 100
  10.4 11.9 %copy-start.9 = (s32[32]{0:T(128)}, s32[32]{0:T(128)S(1)}, u32[]{:S(2)}) copy-start(s32[32]{0:T(128)S(1)} %fusion.39) | copy-start | bytes 388
  11.2 19.1 %all-to-all-start = ((s32[32,1,1]{2,1,0:T(1,128)}), s32[32,1,1]{2,1,0:T(1,128)S(1)}, u32[]{:S(2)}, u32[]{:S(2)}) async-start(s32[32,1,1]{2,1,0:T(1,128)} %copy.33), calls=%async_computation | async-start | bytes 32768 | tf_op jit(solution)/shard_map/all_to_all | solution.py:82
  24.7 11.6 %copy-start.1 = (bf16[1,1,40,8,2048]{4,3,2,1,0:T(8,128)(2,1)S(1)}, bf16[1,1,40,8,2048]{4,3,2,1,0:T(8,128)(2,1)}, u32[]{:S(2)}) copy-start(bf16[1,1,40,8,2048]{4,3,2,1,0:T(8,128)(2,1)} %param.7) | copy-start | bytes 3932164
  30.3 38.7 %all-to-all-start.1 = ((bf16[32,2,8192]{2,1,0:T(2,128)(2,1)}), bf16[32,2,8192]{2,1,0:T(2,128)(2,1)}, u32[]{:S(2)}, u32[]{:S(2)}) async-start(bf16[32,2,8192]{2,1,0:T(2,128)(2,1)} %reshape.139), calls=%async_computation.1 | async-start | bytes 2097152 | tf_op jit(solution)/shard_map/all_to_all | solution.py:75
  36.4 93.8 %copy-start.3 = (bf16[8,8,2048]{2,1,0:T(8,128)(2,1)}, bf16[8,8,2048]{2,1,0:T(8,128)(2,1)S(1)}, u32[]{:S(2)}) copy-start(bf16[8,8,2048]{2,1,0:T(8,128)(2,1)S(1)} %slice_bitcast_fusion) | copy-start | bytes 786436
  73.3 56.8 %copy-start.12 = (f32[2048]{0:T(1024)S(1)}, f32[2048]{0:T(1024)}, u32[]{:S(2)}) copy-start(f32[2048]{0:T(1024)} %param.10) | copy-start | bytes 24580
  135.3 0.9 copy-start.5
  135.4 1.1 copy-start.4
  147.8 14.1 %all-to-all-start.3 = ((f32[32,1,64]{2,1,0:T(1,128)}), f32[32,1,64]{2,1,0:T(1,128)S(1)}, u32[]{:S(2)}, u32[]{:S(2)}) async-start(f32[32,1,64]{2,1,0:T(1,128)} %convolution_bitcast_fusion), calls=%async_computation.3 | async-start | bytes 32768 | tf_op jit(solution)/shard_map/all_to_all | solution.py:31
  155.4 11.9 %copy-start.6 = (bf16[1,1,16,1024]{3,2,1,0:T(8,128)(2,1)S(1)}, bf16[1,1,16,1024]{3,2,1,0:T(8,128)(2,1)}, u32[]{:S(2)}) copy-start(bf16[1,1,16,1024]{3,2,1,0:T(8,128)(2,1)} %param.12) | copy-start | bytes 98308
  155.4 12.0 %slice-start.1 = ((bf16[192,2048]{1,0:T(8,128)(2,1)}), bf16[64,2048]{1,0:T(8,128)(2,1)S(1)}, s32[]{:S(2)}) async-start(bf16[192,2048]{1,0:T(8,128)(2,1)} %copy-done.5), calls=%async_computation.6 | async-start | bytes 524288 | tf_op jit(solution)/shard_map/slice | solution.py:120
  161.8 29.3 %all-to-all-start.2 = ((bf16[32,2,8192]{2,1,0:T(2,128)(2,1)}), bf16[32,2,8192]{2,1,0:T(2,128)(2,1)}, u32[]{:S(2)}, u32[]{:S(2)}) async-start(bf16[32,2,8192]{2,1,0:T(2,128)(2,1)} %reshape.141), calls=%async_computation.2 | async-start | bytes 2097152 | tf_op jit(solution)/shard_map/all_to_all | solution.py:110
  167.4 28.1 %copy-start.8 = (pred[32]{0:T(512)(128)(4,1)S(1)}, pred[32]{0:T(512)(128)(4,1)}, u32[]{:S(2)}) copy-start(pred[32]{0:T(512)(128)(4,1)} %copy-done.7) | copy-start | bytes 100
  167.4 28.1 %copy-start.10 = (s32[32]{0:T(128)S(1)}, s32[32]{0:T(128)}, u32[]{:S(2)}) copy-start(s32[32]{0:T(128)} %copy-done.9) | copy-start | bytes 388
  207.4 5.1 %copy-start.11 = (pred[320]{0:T(512)(128)(4,1)S(1)}, pred[320]{0:T(512)(128)(4,1)}, u32[]{:S(2)}) copy-start(pred[320]{0:T(512)(128)(4,1)} %broadcast_in_dim.42) | copy-start | bytes 964
  213.9 0.9 copy-start.2
Sparse Core Ops, SparseCore 0:
  11.2 118.8 all-gather.1
where the time goes:
time: 234 us; the launch traced here: 230 us
  waiting for transfers between devices  96.1 us (41%)
  local copies, waits for them, and re-layouts  39.6 us (17%)
  starting transfers between devices  26.2 us (11%)
  blocking collectives  23.6 us (10%)
  matrix products  22.2 us (9%)
  between operations  15 us (6%)
  other arithmetic  6.97 us (3%)
    all_gather x1, waiting for transfers between devices, shards(): weight_piece = lax.all_gather(projection, 'fsdp', axis=0, tiled=True)  55 us
    all_to_all x1, waiting for transfers between devices, shards(): lax.all_to_all(outgoing.reshape(peer_count, per_peer, LEN * D), 'fsdp', s...  31.5 us
    unnamed x34, local copies, waits for them, and re-layouts  23.8 us
    psum x2, blocking collectives, by_axis(): array = lax.psum(array, axis)  23.6 us
    all_to_all x1, starting transfers between devices, shards(): lax.all_to_all(slot_tags.reshape(peer_count, per_peer), 'fsdp', split_axi...  10.5 us
    dot_general x1, matrix products, shards(): lax.dot_general(upstream, weight_piece, (((1,), (1,)), ((), ())), preferr...  7.43 us
    all_to_all x1, starting transfers between devices, sent_and_summed(): parts = lax.all_to_all(cut_along(array, dim, peers), axis, 0, 0, tiled=True)  5.67 us
    reshape x1, local copies, waits for them, and re-layouts, shards(): jnp.concatenate([state_rows[:KEEP], remote_states], axis=0)  5.41 us
  transfers between devices with their start and end apart: 5, of which 4 were waited for; matrix products, arithmetic and copies ran while one was open for 9% of the time, Pallas kernels for 0%

commit v1 on v0

v1 whole, which is shorter than its diff:
```python
import jax
import jax.numpy as jnp
from jax import lax
from jax.experimental import pallas as pl
from jax.experimental.pallas import tpu as pltpu
from jax.sharding import Mesh
from jax.sharding import PartitionSpec as P

D = 2048
HEADS = 32
HEAD_DIM = 32
HW = 1024
DEC = 16
LEN = 8
PMAX = 40
KEEP = 8
HELP = 16
ENC = 24
TOK = PMAX * LEN
OWN = KEEP * LEN
AID = HELP * LEN
G = 4
COLS = HW // G
GH = HEADS // G
QROW = ENC * LEN
CROW = QROW + DEC
EROWS = CROW + 16
WIDE = D + 128
EPSILON = 1e-06
GROUP = ("zl", "core")
DP = ("zh", "zl", "core")
FSDP = ("x", "y")

VM = pl.BlockSpec(memory_space=pltpu.VMEM)
SM = pl.BlockSpec(memory_space=pltpu.SMEM)


def params():
    return pltpu.CompilerParams(vmem_limit_bytes=48 * 1024 * 1024)


def pack_body(table, passages, out):
    for s in range(32):
        out[s, :, D:] = jnp.full((LEN, WIDE - D), -1.0, jnp.bfloat16)
    for e in range(PMAX - KEEP):
        peer = table[0, e]

        @pl.when(peer >= 0)
        def _():
            slot = table[1, e].astype(jnp.float32)
            out[peer, :, :D] = passages[KEEP + e]
            out[peer, :, D:] = jnp.full((LEN, WIDE - D), slot, jnp.float32).astype(jnp.bfloat16)


def pack(table, passages):
    return pl.pallas_call(
        pack_body,
        out_shape=jax.ShapeDtypeStruct((32, LEN, WIDE), jnp.bfloat16),
        in_specs=[SM, VM],
        out_specs=VM,
        compiler_params=params(),
        name="pack",
    )(table, passages)


def prep_body(count, cot, queries, out):
    for g in range(G):
        lo, hi = g * COLS, (g + 1) * COLS
        out[g, :QROW, :COLS] = cot[:, lo:hi]
        out[g, :QROW, COLS:] = cot[:, HW + lo : HW + hi]
        out[g, QROW:CROW, :COLS] = queries[:, lo:hi]
        out[g, QROW:CROW, COLS:] = queries[:, lo:hi]
        out[g, CROW:, :] = jnp.full((EROWS - CROW, 2 * COLS), count[0].astype(jnp.float32), jnp.float32).astype(
            jnp.bfloat16
        )


def prep(count, cot, queries):
    return pl.pallas_call(
        prep_body,
        out_shape=jax.ShapeDtypeStruct((G, EROWS, 2 * COLS), jnp.bfloat16),
        in_specs=[SM, VM, VM],
        out_specs=VM,
        compiler_params=params(),
        name="prep",
    )(count, cot, queries)


def unpack_body(tags, arrived, out):
    out[...] = jnp.zeros(out.shape, out.dtype)
    for s in range(32):
        tag = tags[s]

        @pl.when(tag >= 0)
        def _():
            out[tag] = arrived[s, :, :D]


def unpack(tags, arrived):
    return pl.pallas_call(
        unpack_body,
        out_shape=jax.ShapeDtypeStruct((HELP, LEN, D), jnp.bfloat16),
        in_specs=[SM, VM],
        out_specs=VM,
        compiler_params=params(),
        name="unpack",
    )(tags, arrived)


def normal_of(values):
    return values * lax.rsqrt(jnp.mean(values * values, axis=-1, keepdims=True) + EPSILON)


def normals_body(member, e, x0, x1, x2, x3, h0, h1, h2, h3, out):
    for r, (x, h) in enumerate(((x0, h0), (x1, h1), (x2, h2), (x3, h3))):
        src = member[0] ^ r
        live = e[src, CROW : CROW + 8, :128].astype(jnp.float32)[0:1, 0:1]
        spot = (lax.broadcasted_iota(jnp.int32, (OWN, 1), 0) // LEN).astype(jnp.float32)
        normal = normal_of(x[...].astype(jnp.float32))
        out[src, :OWN, :] = jnp.where(spot < live, normal, 0.0)
        out[src, OWN:, :] = normal_of(h[...].astype(jnp.float32))


def normals(member, e, xs, hs):
    return pl.pallas_call(
        normals_body,
        out_shape=jax.ShapeDtypeStruct((G, QROW, D), jnp.float32),
        grid=(1,),
        in_specs=[SM, pl.BlockSpec((G, EROWS, 2 * COLS), lambda i: (0, 0, 0))]
        + [pl.BlockSpec((OWN, D), lambda i: (0, 0))] * G
        + [pl.BlockSpec((AID, D), lambda i: (0, 0))] * G,
        out_specs=pl.BlockSpec((G, QROW, D), lambda i: (0, 0, 0)),
        compiler_params=params(),
        name="normals",
    )(member, e, *xs, *hs)


def grad_body(e, normal, weight, out):
    cot = e[:, :QROW, :].reshape(G * QROW, 2 * COLS)
    back = lax.dot_general(cot, weight[...], (((1,), (1,)), ((), ())), preferred_element_type=jnp.float32)
    block = normal.shape[-1]
    out[...] = jnp.sum(normal[...].reshape(G * QROW, block) * back, axis=0, keepdims=True)


def grad(e, normal, weight):
    block = 512
    return pl.pallas_call(
        grad_body,
        out_shape=jax.ShapeDtypeStruct((1, D), jnp.float32),
        grid=(D // block,),
        in_specs=[
            pl.BlockSpec((G, EROWS, 2 * COLS), lambda i: (0, 0, 0)),
            pl.BlockSpec((G, QROW, block), lambda i: (0, 0, i)),
            pl.BlockSpec((block, 2 * COLS), lambda i: (i, 0)),
        ],
        out_specs=pl.BlockSpec((1, block), lambda i: (0, i)),
        compiler_params=params(),
        name="gain_grad",
    )(e, normal, weight)


def attend_body(member, e, gain, weight, x0, x1, x2, x3, out):
    rows = GH * DEC
    row_head = lax.broadcasted_iota(jnp.int32, (rows, COLS), 0) // DEC
    col_head = lax.broadcasted_iota(jnp.int32, (rows, COLS), 1) // HEAD_DIM
    same = row_head == col_head
    spot = (lax.broadcasted_iota(jnp.int32, (1, TOK), 1) // LEN).astype(jnp.float32)
    for r, x in enumerate((x0, x1, x2, x3)):
        src = member[0] ^ r
        scaled = (normal_of(x[...].astype(jnp.float32)) * gain[...]).astype(jnp.bfloat16)
        states = jnp.dot(scaled, weight[...], preferred_element_type=jnp.float32).astype(jnp.bfloat16)
        query = e[src, QROW:CROW, :COLS].astype(jnp.float32)
        spread = jnp.where(same, jnp.concatenate([query] * GH, axis=0), 0.0).astype(jnp.bfloat16)
        scores = lax.dot_general(
            spread, states[:, :COLS], (((1,), (1,)), ((), ())), preferred_element_type=jnp.float32
        ) * HEAD_DIM ** (-0.5)
        count = e[src, CROW : CROW + 8, :TOK].astype(jnp.float32)[0:1, :]
        scores = jnp.where(spot < count, scores, -jnp.inf)
        raised = jnp.exp(scores - jnp.max(scores, axis=-1, keepdims=True))
        weights = (raised / jnp.sum(raised, axis=-1, keepdims=True)).astype(jnp.bfloat16)
        mixed = jnp.dot(weights, states[:, COLS:], preferred_element_type=jnp.float32)
        mixed = jnp.where(same, mixed, 0.0).reshape(GH, DEC, COLS)
        out[src] = jnp.sum(mixed, axis=0).astype(jnp.bfloat16)


def attend(member, e, gain, weight, xs):
    return pl.pallas_call(
        attend_body,
        out_shape=jax.ShapeDtypeStruct((G, DEC, COLS), jnp.bfloat16),
        in_specs=[SM, VM, VM, VM, VM, VM, VM, VM],
        out_specs=VM,
        compiler_params=params(),
        name="attend",
    )(member, e, gain, weight, *xs)


def exchange(array, axes):
    return lax.all_to_all(array, axes, 0, 0, tiled=True)


def spread_to(array, axis):
    return exchange(jnp.broadcast_to(array[None], (lax.axis_size(axis), *array.shape)), axis)


def swap(array, axis):
    return lax.ppermute(array, axis, [(0, 1), (1, 0)])


def shards(passages, counts, helper_table, norm_gain, projection, queries, cotangent):
    member = (lax.axis_index("zl") * 2 + lax.axis_index("core")).astype(jnp.int32)
    stored = passages.reshape(PMAX, LEN, D)
    x_own = passages.reshape(TOK, D)
    member_ref = member.reshape(1)

    x_z = swap(x_own, "zl")
    x_c = swap(x_own, "core")
    x_cz = swap(x_z, "core")
    xs = (x_own, x_c, x_z, x_cz)

    outgoing = pack(helper_table.reshape(2, PMAX - KEEP), stored)
    arrived = exchange(outgoing, FSDP)
    e = exchange(prep(counts.reshape(1), cotangent.reshape(QROW, D), queries.reshape(DEC, HW)), GROUP)

    tags = arrived[:, 0, D].astype(jnp.int32)
    h_own = unpack(tags, arrived).reshape(AID, D)
    h_z = swap(h_own, "zl")
    h_c = swap(h_own, "core")
    h_cz = swap(h_z, "core")
    normal = normals(member_ref, e, xs, (h_own, h_c, h_z, h_cz))

    mine = lax.dynamic_index_in_dim(projection.reshape(64, 2, G, COLS), member, 2, keepdims=False).reshape(
        64, 2 * COLS
    )
    by_y = spread_to(mine, "y").reshape(512, 2 * COLS)
    weight = spread_to(by_y, "x").reshape(D, 2 * COLS)

    row_terms = grad(e, normal, weight)
    parts = exchange(row_terms.reshape(32, 1, 64), FSDP)
    share = jnp.sum(parts, axis=0)
    gathered = exchange(jnp.broadcast_to(share[None], (16, 1, 64)), DP)
    gradient = jnp.sum(gathered, axis=0).reshape(64)

    mixed = attend(member_ref, e, norm_gain.reshape(1, D), weight, xs)
    context = exchange(mixed, GROUP)
    context_out = jnp.transpose(context, (1, 0, 2)).reshape(1, 1, DEC, HW)
    return (context_out, gradient)


def solution(mesh):
    split = Mesh(mesh.devices.reshape(4, 2, 2, 4, 8), ("zh", "zl", "core", "x", "y"))
    return jax.shard_map(
        shards,
        mesh=split,
        in_specs=(
            P(DP, FSDP, None, None, None),
            P(DP, FSDP),
            P(DP, FSDP, None, None),
            P(),
            P(FSDP, None),
            P(DP, FSDP, None, None),
            P(DP, FSDP, None, None, None),
        ),
        out_specs=(P(DP, FSDP, None, None), P(FSDP)),
        check_vma=False,
    )
```

time: 234 us -> 170 us (0.73); the launches traced: 230 us -> 169 us
  starting transfers between devices: 26.2 us -> 63.4 us
  waiting for transfers between devices: 96.1 us -> 67.5 us
  local copies, waits for them, and re-layouts: 39.6 us -> 11.6 us
  blocking collectives: 23.6 us -> 0 us
  Pallas kernels: 0 us -> 22.7 us
  matrix products: 22.2 us -> 0 us
  between operations: 15 us -> 1.52 us
  other arithmetic: 6.97 us -> 2.75 us
    all_gather x1 -> x0, waiting for transfers between devices: 55 us -> none  [shards(): weight_piece = lax.all_gather(projection, 'fsdp', axis=0, tiled=True)]
    psum x2 -> x0, blocking collectives: 23.6 us -> none  [by_axis(): array = lax.psum(array, axis)]
    pallas_call x0 -> x6, Pallas kernels: none -> 22.7 us  [the longest x1 7.49 us: attend(): pl.pallas_call(attend_body, out_shape=jax.ShapeDtypeStruct((G, DEC, COLS)...]
    dot_general x9 -> x0, matrix products: 22.2 us -> none  [the longest x1 7.43 us: shards(): lax.dot_general(upstream, weight_piece, (((1,), (1,)), ((), ())), preferr...]
    ppermute x0 -> x6, starting transfers between devices: none -> 19.2 us  [swap(): return lax.ppermute(array, axis, [(0, 1), (1, 0)])]
    unnamed x34 -> x23, local copies, waits for them, and re-layouts: 23.8 us -> 5.05 us
    all_to_all x4 -> x7, starting transfers between devices: 26.2 us -> 44.2 us  [exchange(): return lax.all_to_all(array, axes, 0, 0, tiled=True)]
    all_to_all x4 -> x7, waiting for transfers between devices: 40.4 us -> 56.1 us  [exchange(): return lax.all_to_all(array, axes, 0, 0, tiled=True)]
  transfers between devices with their start and end apart: 5 -> 13, of which waited for: 4 -> 7; matrix products, arithmetic and copies ran while one was open for 9% -> 2% of each run, Pallas kernels for 0% -> 10%
where the time goes in v1:
time: 170 us; the launch traced here: 169 us
  waiting for transfers between devices  67.5 us (40%)
  starting transfers between devices  63.4 us (37%)
  Pallas kernels  22.7 us (13%)
  local copies, waits for them, and re-layouts  11.6 us (7%)
  other arithmetic  2.75 us (2%)
    all_to_all x7, waiting for transfers between devices, exchange(): return lax.all_to_all(array, axes, 0, 0, tiled=True)  56.1 us
    all_to_all x7, starting transfers between devices, exchange(): return lax.all_to_all(array, axes, 0, 0, tiled=True)  44.2 us
    ppermute x6, starting transfers between devices, swap(): return lax.ppermute(array, axis, [(0, 1), (1, 0)])  19.2 us
    ppermute x6, waiting for transfers between devices, swap(): return lax.ppermute(array, axis, [(0, 1), (1, 0)])  11.4 us
    pallas_call x1, Pallas kernels, attend(): pl.pallas_call(attend_body, out_shape=jax.ShapeDtypeStruct((G, DEC, COLS)...  7.49 us
    pallas_call x1, Pallas kernels, grad(): pl.pallas_call(grad_body, out_shape=jax.ShapeDtypeStruct((1, D), jnp.floa...  5.59 us
    pallas_call x1, Pallas kernels, normals(): pl.pallas_call(normals_body, out_shape=jax.ShapeDtypeStruct((G, QROW, D),...  5.11 us
    unnamed x23, local copies, waits for them, and re-layouts  5.05 us
  transfers between devices with their start and end apart: 13, of which 7 were waited for; matrix products, arithmetic and copies ran while one was open for 2% of the time, Pallas kernels for 10%

profile of v1, /device:TPU:1, one launch (start us, length us, event | category | flops | bytes accessed | tf_op | source)
XLA Modules:
  0.0 169.4 jit_solution(15671832193849808576)
XLA Ops:
  0.7 1.2 reshape.61
  3.2 7.6 %all-to-all-start.1 = ((bf16[8,64,512]{2,1,0:T(8,128)(2,1)}), bf16[8,64,512]{2,1,0:T(8,128)(2,1)S(1)}, u32[]{:S(2)}, u32[]{:S(2)}) async-start(bf16[8,64,512]{2,1,0:T(8,128)(2,1)} %broadcast_in_dim.21), calls=%async_computation.1 | async-start | bytes 1048576 | tf_op jit(solution)/shard_map/all_to_all | solution.py:198
  11.5 1.0 prep.1
  12.5 13.3 %all-to-all-done.1 = bf16[8,64,512]{2,1,0:T(8,128)(2,1)S(1)} async-done(((bf16[8,64,512]{2,1,0:T(8,128)(2,1)}), bf16[8,64,512]{2,1,0:T(8,128)(2,1)S(1)}, u32[]{:S(2)}, u32[]{:S(2)}) %all-to-all-start.1) | async-done | bytes 524320 | tf_op jit(solution)/shard_map/all_to_all | solution.py:198
  25.8 7.1 %all-to-all-start = ((bf16[4,224,512]{2,1,0:T(8,128)(2,1)}), bf16[4,224,512]{2,1,0:T(8,128)(2,1)S(1)}, u32[]{:S(2)}, u32[]{:S(2)}) async-start(bf16[4,224,512]{2,1,0:T(8,128)(2,1)} %prep.1), calls=%async_computation | async-start | bytes 1835008 | tf_op jit(solution)/shard_map/all_to_all | solution.py:198
  32.9 2.7 %pack.1 = bf16[32,8,2176]{2,1,0:T(8,128)(2,1)} custom-call(s32[2,32]{1,0:T(2,128)S(1)} %bitcast.25, bf16[40,8,2048]{2,1,0:T(8,128)(2,1)} %bitcast.10.passages), custom_call_target="tpu_custom_call" | custom-call | tf_op jit(solution)/shard_map/pack/pallas_call | solution.py:56
  35.6 9.4 %all-to-all-done.e = bf16[4,224,512]{2,1,0:T(8,128)(2,1)S(1)} async-done(((bf16[4,224,512]{2,1,0:T(8,128)(2,1)}), bf16[4,224,512]{2,1,0:T(8,128)(2,1)S(1)}, u32[]{:S(2)}, u32[]{:S(2)}) %all-to-all-start) | async-done | bytes 917536 | tf_op jit(solution)/shard_map/all_to_all | solution.py:198
  44.9 4.4 %all-to-all-start.4 = ((bf16[32,8,2176]{2,1,0:T(8,128)(2,1)}), bf16[32,8,2176]{2,1,0:T(8,128)(2,1)S(1)}, u32[]{:S(2)}, u32[]{:S(2)}) async-start(bf16[32,8,2176]{2,1,0:T(8,128)(2,1)} %pack.1), calls=%async_computation.4 | async-start | bytes 2228224 | tf_op jit(solution)/shard_map/all_to_all | solution.py:198
  49.4 2.4 %collective-permute-start.1 = (bf16[320,2048]{1,0:T(8,128)(2,1)}, bf16[320,2048]{1,0:T(8,128)(2,1)}, u32[]{:S(2)}, u32[]{:S(2)}) collective-permute-start(bf16[320,2048]{1,0:T(8,128)(2,1)} %bitcast.7.x0), channel_id=1, source_target_pairs={{0,64},{64,0},{1,65},{65,1},{2,66},{66,2},{3,67},{67,3},{4,68},{68... | collective-permute-start | bytes 3932168 | tf_op jit(solution)/shard_map/ppermute | solution.py:206
  51.8 24.0 %all-to-all-done.4.arrived = bf16[32,8,2176]{2,1,0:T(8,128)(2,1)S(1)} async-done(((bf16[32,8,2176]{2,1,0:T(8,128)(2,1)}), bf16[32,8,2176]{2,1,0:T(8,128)(2,1)S(1)}, u32[]{:S(2)}, u32[]{:S(2)}) %all-to-all-start.4) | async-done | bytes 1114144 | tf_op jit(solution)/shard_map/all_to_all | solution.py:198
  75.8 1.6 broadcast_in_dim.23
  77.5 3.6 %all-to-all-start.2 = ((bf16[4,512,512]{2,1,0:T(8,128)(2,1)}), bf16[4,512,512]{2,1,0:T(8,128)(2,1)S(1)}, u32[]{:S(2)}, u32[]{:S(2)}) async-start(bf16[4,512,512]{2,1,0:T(8,128)(2,1)} %broadcast_in_dim.23), calls=%async_computation.2 | async-start | bytes 4194304 | tf_op jit(solution)/shard_map/all_to_all | solution.py:198
  81.1 6.6 %collective-permute-start = (bf16[320,2048]{1,0:T(8,128)(2,1)}, bf16[320,2048]{1,0:T(8,128)(2,1)S(1)}, u32[]{:S(2)}, u32[]{:S(2)}) collective-permute-start(bf16[320,2048]{1,0:T(8,128)(2,1)} %bitcast.7.x0), channel_id=1, source_target_pairs={{0,32},{32,0},{1,33},{33,1},{2,34},{34,2},{3,35},{35,3},{4,36},{36... | collective-permute-start | bytes 3932168 | tf_op jit(solution)/shard_map/ppermute | solution.py:206
  87.7 1.9 %collective-permute-start.2 = (bf16[320,2048]{1,0:T(8,128)(2,1)}, bf16[320,2048]{1,0:T(8,128)(2,1)S(1)}, u32[]{:S(2)}, u32[]{:S(2)}) collective-permute-start(bf16[320,2048]{1,0:T(8,128)(2,1)} %collective-permute-done.1.x2), channel_id=1, source_target_pairs={{0,32},{32,0},{1,33},{33,1},{2,34},{34,2},{3,35},{35,3},{4,36},{36... | collective-permute-start | bytes 3932168 | tf_op jit(solution)/shard_map/ppermute | solution.py:206
  89.6 1.5 fusion.tags
  91.1 1.2 copy-done.6
  93.2 2.3 %collective-permute-start.4 = (bf16[128,2048]{1,0:T(8,128)(2,1)S(1)}, bf16[128,2048]{1,0:T(8,128)(2,1)S(1)}, u32[]{:S(2)}, u32[]{:S(2)}) collective-permute-start(bf16[128,2048]{1,0:T(8,128)(2,1)S(1)} %bitcast.19), channel_id=1, source_target_pairs={{0,64},{64,0},{1,65},{65,1},{2,66},{66,2},{3,67},{67,3},{4,68},{68... | collective-permute-start | bytes 1572872 | tf_op jit(solution)/shard_map/ppermute | solution.py:206
  95.5 2.7 %collective-permute-start.3 = (bf16[128,2048]{1,0:T(8,128)(2,1)S(1)}, bf16[128,2048]{1,0:T(8,128)(2,1)S(1)}, u32[]{:S(2)}, u32[]{:S(2)}) collective-permute-start(bf16[128,2048]{1,0:T(8,128)(2,1)S(1)} %bitcast.20), channel_id=1, source_target_pairs={{0,32},{32,0},{1,33},{33,1},{2,34},{34,2},{3,35},{35,3},{4,36},{36... | collective-permute-start | bytes 1572872 | tf_op jit(solution)/shard_map/ppermute | solution.py:206
  98.2 9.9 %collective-permute-done.4.h2 = bf16[128,2048]{1,0:T(8,128)(2,1)S(1)} collective-permute-done((bf16[128,2048]{1,0:T(8,128)(2,1)S(1)}, bf16[128,2048]{1,0:T(8,128)(2,1)S(1)}, u32[]{:S(2)}, u32[]{:S(2)}) %collective-permute-start.4) | collective-permute-done | bytes 524320 | tf_op jit(solution)/shard_map/ppermute | solution.py:206
  108.1 3.3 %collective-permute-start.5 = (bf16[128,2048]{1,0:T(8,128)(2,1)S(1)}, bf16[128,2048]{1,0:T(8,128)(2,1)S(1)}, u32[]{:S(2)}, u32[]{:S(2)}) collective-permute-start(bf16[128,2048]{1,0:T(8,128)(2,1)S(1)} %collective-permute-done.4.h2), channel_id=1, source_target_pairs={{0,32},{32,0},{1,33},{33,1},{2,34},{34,2},{3,35},{35,3},{4,36},{36... | collective-permute-start | bytes 1572872 | tf_op jit(solution)/shard_map/ppermute | solution.py:206
  111.4 1.5 collective-permute-done.5.h3
  112.9 5.1 %normals.1.normal = f32[4,192,2048]{2,1,0:T(8,128)} custom-call(s32[1]{0:T(128)} %bitcast.member, bf16[4,224,512]{2,1,0:T(8,128)(2,1)S(1)} %all-to-all-done.e, bf16[320,2048]{1,0:T(8,128)(2,1)} %bitcast.7.x0, bf16[320,2048]{1,0:T(8,128)(2,1)S(1)} %collective-permute-done.x1, bf16[320,2048]{1,0:T(8,128)(2,1)} %collective-permute-done.1.x2, ...), custom_call_target="tpu_custom_call" | custom-call | tf_op jit(solution)/shard_map/normals/pallas_call | solution.py:125
  118.0 1.1 copy-done.1
  119.1 5.6 %gain_grad.1 = f32[1,2048]{1,0:T(1,128)S(1)} custom-call(bf16[4,224,512]{2,1,0:T(8,128)(2,1)S(1)} %all-to-all-done.e, f32[4,192,2048]{2,1,0:T(8,128)} %normals.1.normal, bf16[2048,512]{1,0:T(8,128)(2,1)S(1)} %bitcast.17), custom_call_target="tpu_custom_call" | custom-call | tf_op jit(solution)/shard_map/gain_grad/pallas_call | solution.py:147
  126.5 6.6 %all-to-all-start.5 = ((f32[32,1,64]{2,1,0:T(1,128)}), f32[32,1,64]{2,1,0:T(1,128)S(1)}, u32[]{:S(2)}, u32[]{:S(2)}) async-start(f32[32,1,64]{2,1,0:T(1,128)} %bitcast.12), calls=%async_computation.5 | async-start | bytes 32768 | tf_op jit(solution)/shard_map/all_to_all | solution.py:198
  133.1 1.3 copy-done.2
  134.4 1.3 copy-done.4
  135.8 7.5 %attend.1 = bf16[4,16,256]{2,1,0:T(8,128)(2,1)} custom-call(s32[1]{0:T(128)} %bitcast.member, bf16[4,224,512]{2,1,0:T(8,128)(2,1)S(1)} %all-to-all-done.e, f32[1,2048]{1,0:T(1,128)S(1)} %bitcast.24, bf16[2048,512]{1,0:T(8,128)(2,1)} %bitcast.18, bf16[320,2048]{1,0:T(8,128)(2,1)} %bitcast.7.x0, bf16[320,2048]{1,0:T(8,128)(2,1)S(1)} %copy-done.2, ...), custom_call_target="tpu_custom_call" | custom-call | tf_op jit(solution)/shard_map/attend/pallas_call | solution.py:187
  143.3 3.9 %all-to-all-start.3 = ((bf16[4,16,256]{2,1,0:T(8,128)(2,1)}), bf16[4,16,256]{2,1,0:T(8,128)(2,1)S(1)}, u32[]{:S(2)}, u32[]{:S(2)}) async-start(bf16[4,16,256]{2,1,0:T(8,128)(2,1)} %attend.1), calls=%async_computation.3 | async-start | bytes 65536 | tf_op jit(solution)/shard_map/all_to_all | solution.py:198
  147.2 3.1 %all-to-all-done.3 = bf16[4,16,256]{2,1,0:T(8,128)(2,1)S(1)} async-done(((bf16[4,16,256]{2,1,0:T(8,128)(2,1)}), bf16[4,16,256]{2,1,0:T(8,128)(2,1)S(1)}, u32[]{:S(2)}, u32[]{:S(2)}) %all-to-all-start.3) | async-done | bytes 32800 | tf_op jit(solution)/shard_map/all_to_all | solution.py:198
  150.9 10.9 %all-to-all-start.6 = ((f32[16,1,64]{2,1,0:T(1,128)}), f32[16,1,64]{2,1,0:T(1,128)S(1)}, u32[]{:S(2)}, u32[]{:S(2)}) async-start(f32[16,1,64]{2,1,0:T(1,128)} %broadcast_in_dim.24), calls=%async_computation.6 | async-start | bytes 16384 | tf_op jit(solution)/shard_map/all_to_all | solution.py:198
  162.5 6.4 %all-to-all-done.6 = f32[16,1,64]{2,1,0:T(1,128)S(1)} async-done(((f32[16,1,64]{2,1,0:T(1,128)}), f32[16,1,64]{2,1,0:T(1,128)S(1)}, u32[]{:S(2)}, u32[]{:S(2)}) %all-to-all-start.6) | async-done | bytes 4128 | tf_op jit(solution)/shard_map/all_to_all | solution.py:198
  (36 shorter events, 5.9 us)
Async XLA Ops:
  0.6 10.8 %copy-start.7 = (bf16[1,1,24,8,2048]{4,3,2,1,0:T(8,128)(2,1)S(1)}, bf16[1,1,24,8,2048]{4,3,2,1,0:T(8,128)(2,1)}, u32[]{:S(2)}) copy-start(bf16[1,1,24,8,2048]{4,3,2,1,0:T(8,128)(2,1)} %param.13) | copy-start | bytes 2359300
  0.6 10.8 %copy-start.8 = (bf16[1,1,16,1024]{3,2,1,0:T(8,128)(2,1)S(1)}, bf16[1,1,16,1024]{3,2,1,0:T(8,128)(2,1)}, u32[]{:S(2)}) copy-start(bf16[1,1,16,1024]{3,2,1,0:T(8,128)(2,1)} %param.12) | copy-start | bytes 98308
  3.2 22.6 %all-to-all-start.1 = ((bf16[8,64,512]{2,1,0:T(8,128)(2,1)}), bf16[8,64,512]{2,1,0:T(8,128)(2,1)S(1)}, u32[]{:S(2)}, u32[]{:S(2)}) async-start(bf16[8,64,512]{2,1,0:T(8,128)(2,1)} %broadcast_in_dim.21), calls=%async_computation.1 | async-start | bytes 1048576 | tf_op jit(solution)/shard_map/all_to_all | solution.py:198
  12.5 20.4 %copy-start.10 = (s32[1,1,2,32]{3,2,1,0:T(2,128)S(1)}, s32[1,1,2,32]{3,2,1,0:T(2,128)}, u32[]{:S(2)}) copy-start(s32[1,1,2,32]{3,2,1,0:T(2,128)} %param.9) | copy-start | bytes 772
  25.8 19.2 %all-to-all-start = ((bf16[4,224,512]{2,1,0:T(8,128)(2,1)}), bf16[4,224,512]{2,1,0:T(8,128)(2,1)S(1)}, u32[]{:S(2)}, u32[]{:S(2)}) async-start(bf16[4,224,512]{2,1,0:T(8,128)(2,1)} %prep.1), calls=%async_computation | async-start | bytes 1835008 | tf_op jit(solution)/shard_map/all_to_all | solution.py:198
  44.9 30.8 %all-to-all-start.4 = ((bf16[32,8,2176]{2,1,0:T(8,128)(2,1)}), bf16[32,8,2176]{2,1,0:T(8,128)(2,1)S(1)}, u32[]{:S(2)}, u32[]{:S(2)}) async-start(bf16[32,8,2176]{2,1,0:T(8,128)(2,1)} %pack.1), calls=%async_computation.4 | async-start | bytes 2228224 | tf_op jit(solution)/shard_map/all_to_all | solution.py:198
  49.4 38.3 %collective-permute-start.1 = (bf16[320,2048]{1,0:T(8,128)(2,1)}, bf16[320,2048]{1,0:T(8,128)(2,1)}, u32[]{:S(2)}, u32[]{:S(2)}) collective-permute-start(bf16[320,2048]{1,0:T(8,128)(2,1)} %bitcast.7.x0), channel_id=1, source_target_pairs={{0,64},{64,0},{1,65},{65,1},{2,66},{66,2},{3,67},{67,3},{4,68},{68... | collective-permute-start | bytes 3932168 | tf_op jit(solution)/shard_map/ppermute | solution.py:206
  75.8 1.7 %copy-start.5 = (bf16[32,8,2176]{2,1,0:T(8,128)(2,1)}, bf16[32,8,2176]{2,1,0:T(8,128)(2,1)S(1)}, u32[]{:S(2)}) copy-start(bf16[32,8,2176]{2,1,0:T(8,128)(2,1)S(1)} %all-to-all-done.4.arrived) | copy-start | bytes 3342340
  77.5 41.6 %all-to-all-start.2 = ((bf16[4,512,512]{2,1,0:T(8,128)(2,1)}), bf16[4,512,512]{2,1,0:T(8,128)(2,1)S(1)}, u32[]{:S(2)}, u32[]{:S(2)}) async-start(bf16[4,512,512]{2,1,0:T(8,128)(2,1)} %broadcast_in_dim.23), calls=%async_computation.2 | async-start | bytes 4194304 | tf_op jit(solution)/shard_map/all_to_all | solution.py:198
  81.1 30.3 %collective-permute-start = (bf16[320,2048]{1,0:T(8,128)(2,1)}, bf16[320,2048]{1,0:T(8,128)(2,1)S(1)}, u32[]{:S(2)}, u32[]{:S(2)}) collective-permute-start(bf16[320,2048]{1,0:T(8,128)(2,1)} %bitcast.7.x0), channel_id=1, source_target_pairs={{0,32},{32,0},{1,33},{33,1},{2,34},{34,2},{3,35},{35,3},{4,36},{36... | collective-permute-start | bytes 3932168 | tf_op jit(solution)/shard_map/ppermute | solution.py:206
  87.7 23.7 %collective-permute-start.2 = (bf16[320,2048]{1,0:T(8,128)(2,1)}, bf16[320,2048]{1,0:T(8,128)(2,1)S(1)}, u32[]{:S(2)}, u32[]{:S(2)}) collective-permute-start(bf16[320,2048]{1,0:T(8,128)(2,1)} %collective-permute-done.1.x2), channel_id=1, source_target_pairs={{0,32},{32,0},{1,33},{33,1},{2,34},{34,2},{3,35},{35,3},{4,36},{36... | collective-permute-start | bytes 3932168 | tf_op jit(solution)/shard_map/ppermute | solution.py:206
  91.1 1.3 copy-start.6
  93.2 14.9 %collective-permute-start.4 = (bf16[128,2048]{1,0:T(8,128)(2,1)S(1)}, bf16[128,2048]{1,0:T(8,128)(2,1)S(1)}, u32[]{:S(2)}, u32[]{:S(2)}) collective-permute-start(bf16[128,2048]{1,0:T(8,128)(2,1)S(1)} %bitcast.19), channel_id=1, source_target_pairs={{0,64},{64,0},{1,65},{65,1},{2,66},{66,2},{3,67},{67,3},{4,68},{68... | collective-permute-start | bytes 1572872 | tf_op jit(solution)/shard_map/ppermute | solution.py:206
  95.5 15.9 %collective-permute-start.3 = (bf16[128,2048]{1,0:T(8,128)(2,1)S(1)}, bf16[128,2048]{1,0:T(8,128)(2,1)S(1)}, u32[]{:S(2)}, u32[]{:S(2)}) collective-permute-start(bf16[128,2048]{1,0:T(8,128)(2,1)S(1)} %bitcast.20), channel_id=1, source_target_pairs={{0,32},{32,0},{1,33},{33,1},{2,34},{34,2},{3,35},{35,3},{4,36},{36... | collective-permute-start | bytes 1572872 | tf_op jit(solution)/shard_map/ppermute | solution.py:206
  108.1 4.8 %collective-permute-start.5 = (bf16[128,2048]{1,0:T(8,128)(2,1)S(1)}, bf16[128,2048]{1,0:T(8,128)(2,1)S(1)}, u32[]{:S(2)}, u32[]{:S(2)}) collective-permute-start(bf16[128,2048]{1,0:T(8,128)(2,1)S(1)} %collective-permute-done.4.h2), channel_id=1, source_target_pairs={{0,32},{32,0},{1,33},{33,1},{2,34},{34,2},{3,35},{35,3},{4,36},{36... | collective-permute-start | bytes 1572872 | tf_op jit(solution)/shard_map/ppermute | solution.py:206
  111.4 1.5 copy-start.3
  118.0 1.1 copy-start.1
  119.1 5.6 %copy-start = (bf16[4,512,512]{2,1,0:T(8,128)(2,1)}, bf16[4,512,512]{2,1,0:T(8,128)(2,1)S(1)}, u32[]{:S(2)}) copy-start(bf16[4,512,512]{2,1,0:T(8,128)(2,1)S(1)} %all-to-all-done.2) | copy-start | bytes 6291460
  119.1 14.1 %copy-start.9 = (f32[2048]{0:T(1024)S(1)}, f32[2048]{0:T(1024)}, u32[]{:S(2)}) copy-start(f32[2048]{0:T(1024)} %param.10) | copy-start | bytes 24580
  126.5 16.7 %all-to-all-start.5 = ((f32[32,1,64]{2,1,0:T(1,128)}), f32[32,1,64]{2,1,0:T(1,128)S(1)}, u32[]{:S(2)}, u32[]{:S(2)}) async-start(f32[32,1,64]{2,1,0:T(1,128)} %bitcast.12), calls=%async_computation.5 | async-start | bytes 32768 | tf_op jit(solution)/shard_map/all_to_all | solution.py:198
  133.1 1.3 copy-start.2
  134.4 1.3 copy-start.4
  143.3 7.1 %all-to-all-start.3 = ((bf16[4,16,256]{2,1,0:T(8,128)(2,1)}), bf16[4,16,256]{2,1,0:T(8,128)(2,1)S(1)}, u32[]{:S(2)}, u32[]{:S(2)}) async-start(bf16[4,16,256]{2,1,0:T(8,128)(2,1)} %attend.1), calls=%async_computation.3 | async-start | bytes 65536 | tf_op jit(solution)/shard_map/all_to_all | solution.py:198
  150.9 18.0 %all-to-all-start.6 = ((f32[16,1,64]{2,1,0:T(1,128)}), f32[16,1,64]{2,1,0:T(1,128)S(1)}, u32[]{:S(2)}, u32[]{:S(2)}) async-start(f32[16,1,64]{2,1,0:T(1,128)} %broadcast_in_dim.24), calls=%async_computation.6 | async-start | bytes 16384 | tf_op jit(solution)/shard_map/all_to_all | solution.py:198

commit v2 on v1

v2 whole, which is shorter than its diff:
```python
import jax
import jax.numpy as jnp
from jax import lax
from jax.experimental import pallas as pl
from jax.experimental.pallas import tpu as pltpu
from jax.sharding import Mesh
from jax.sharding import PartitionSpec as P

D = 2048
HEADS = 32
HEAD_DIM = 32
HW = 1024
DEC = 16
LEN = 8
PMAX = 40
KEEP = 8
HELP = 16
ENC = 24
TOK = PMAX * LEN
OWN = KEEP * LEN
AID = HELP * LEN
G = 4
COLS = HW // G
GH = HEADS // G
CROW = TOK + ENC * LEN // 2
QROW = CROW
MROWS = QROW + DEC
WIDE = D + 128
EPSILON = 1e-06
GROUP = ("zl", "core")
DP = ("zh", "zl", "core")
FSDP = ("x", "y")

VM = pl.BlockSpec(memory_space=pltpu.VMEM)
SM = pl.BlockSpec(memory_space=pltpu.SMEM)


def params():
    return pltpu.CompilerParams(vmem_limit_bytes=48 * 1024 * 1024)


def pack_body(table, passages, out):
    for s in range(32):
        out[s, :, D:] = jnp.full((LEN, WIDE - D), -1.0, jnp.bfloat16)
    for e in range(PMAX - KEEP):
        peer = table[0, e]

        @pl.when(peer >= 0)
        def _():
            slot = table[1, e].astype(jnp.float32)
            out[peer, :, :D] = passages[KEEP + e]
            out[peer, :, D:] = jnp.full((LEN, WIDE - D), slot, jnp.float32).astype(jnp.bfloat16)


def pack(table, passages):
    return pl.pallas_call(
        pack_body,
        out_shape=jax.ShapeDtypeStruct((32, LEN, WIDE), jnp.bfloat16),
        in_specs=[SM, VM],
        out_specs=VM,
        compiler_params=params(),
        name="pack",
    )(table, passages)


def prep_body(place, count, passages, cot, queries, near, far):
    half = ENC * LEN // 2
    for out, flip in ((near, 0), (far, 1)):
        out[:TOK, :] = passages[...]
        for z in range(2):

            @pl.when(place[0] == z)
            def _():
                for c in range(2):
                    lo = (2 * (z ^ flip) + c) * COLS
                    for part in range(2):
                        at = (2 * c + part) * 2 * COLS
                        rows = slice(part * half, (part + 1) * half)
                        out[TOK:CROW, at : at + COLS] = cot[rows, lo : lo + COLS]
                        out[TOK:CROW, at + COLS : at + 2 * COLS] = cot[rows, HW + lo : HW + lo + COLS]
                    out[QROW:, c * COLS : (c + 1) * COLS] = queries[:, lo : lo + COLS]

        out[QROW:, 2 * COLS :] = jnp.full((DEC, D - 2 * COLS), count[0].astype(jnp.float32), jnp.float32).astype(
            jnp.bfloat16
        )


def prep(place, count, passages, cot, queries):
    message = jax.ShapeDtypeStruct((MROWS, D), jnp.bfloat16)
    return pl.pallas_call(
        prep_body,
        out_shape=(message, message),
        in_specs=[SM, SM, VM, VM, VM],
        out_specs=(VM, VM),
        compiler_params=params(),
        name="prep",
    )(place, count, passages, cot, queries)


def columns_body(member, projection, out):
    for g in range(G):

        @pl.when(member[0] == g)
        def _():
            lo = g * COLS
            for peer in range(8):
                out[peer, :, :COLS] = projection[:, lo : lo + COLS]
                out[peer, :, COLS:] = projection[:, HW + lo : HW + lo + COLS]


def columns(member, projection):
    return pl.pallas_call(
        columns_body,
        out_shape=jax.ShapeDtypeStruct((8, 64, 2 * COLS), jnp.bfloat16),
        in_specs=[SM, VM],
        out_specs=VM,
        compiler_params=params(),
        name="columns",
    )(member, projection)


def unpack_body(tags, arrived, out):
    out[...] = jnp.zeros(out.shape, out.dtype)
    for s in range(32):
        tag = tags[s]

        @pl.when(tag >= 0)
        def _():
            out[tag] = arrived[s, :, :D]


def unpack(tags, arrived):
    return pl.pallas_call(
        unpack_body,
        out_shape=jax.ShapeDtypeStruct((HELP, LEN, D), jnp.bfloat16),
        in_specs=[SM, VM],
        out_specs=VM,
        compiler_params=params(),
        name="unpack",
    )(tags, arrived)


def inverse_rms(values):
    return lax.rsqrt(jnp.mean(values * values, axis=-1, keepdims=True) + EPSILON)


def scale_body(message, gain, out):
    values = message[...].astype(jnp.float32)
    out[...] = (values * inverse_rms(values) * gain[...]).astype(jnp.bfloat16)


def scale(message, gain):
    return pl.pallas_call(
        scale_body,
        out_shape=jax.ShapeDtypeStruct((TOK, D), jnp.bfloat16),
        grid=(1,),
        in_specs=[pl.BlockSpec((TOK, D), lambda i: (0, 0)), pl.BlockSpec((1, D), lambda i: (0, 0))],
        out_specs=pl.BlockSpec((TOK, D), lambda i: (0, 0)),
        compiler_params=params(),
        name="scale",
    )(message, gain)


def outer_body(place, m0, m1, m2, m3, h0, h1, h2, h3, out, rows, high, low):
    spot = (lax.broadcasted_iota(jnp.int32, (OWN, 1), 0) // LEN).astype(jnp.float32)
    for r, (message, aid) in enumerate(((m0, h0), (m1, h1), (m2, h2), (m3, h3))):
        at = r * ENC * LEN
        own = message[:OWN, :]
        helped = aid[...]
        rows[at : at + OWN, :] = own
        rows[at + OWN : at + ENC * LEN, :] = helped
        count = message[QROW : QROW + DEC, 2 * COLS : 2 * COLS + 128].astype(jnp.float32)[0:1, 0:1]
        own_scale = jnp.where(spot < count, inverse_rms(own.astype(jnp.float32)), 0.0)
        scales = jnp.concatenate([own_scale, inverse_rms(helped.astype(jnp.float32))], axis=0)
        for c in range(2):

            @pl.when(place[1] == c)
            def _():
                left = 4 * c * COLS
                cot = jnp.concatenate(
                    [
                        message[TOK:CROW, left : left + 2 * COLS],
                        message[TOK:CROW, left + 2 * COLS : left + 4 * COLS],
                    ],
                    axis=0,
                )
                product = cot.astype(jnp.float32) * scales
                top = product.astype(jnp.bfloat16)
                high[at : at + ENC * LEN, :] = top
                low[at : at + ENC * LEN, :] = (product - top.astype(jnp.float32)).astype(jnp.bfloat16)

    over_tokens = (((0,), (0,)), ((), ()))
    block = 512
    for d in range(0, D, block):
        x = rows[:, d : d + block]
        out[d : d + block, :] = lax.dot_general(
            x, high[...], over_tokens, preferred_element_type=jnp.float32
        ) + lax.dot_general(x, low[...], over_tokens, preferred_element_type=jnp.float32)


def outer(place, messages, hs):
    return pl.pallas_call(
        outer_body,
        out_shape=jax.ShapeDtypeStruct((D, 2 * COLS), jnp.float32),
        in_specs=[SM] + [VM] * (2 * G),
        out_specs=VM,
        scratch_shapes=[
            pltpu.VMEM((G * ENC * LEN, D), jnp.bfloat16),
            pltpu.VMEM((G * ENC * LEN, 2 * COLS), jnp.bfloat16),
            pltpu.VMEM((G * ENC * LEN, 2 * COLS), jnp.bfloat16),
        ],
        compiler_params=params(),
        name="outer",
    )(place, *messages, *hs)


def grad_body(weight, products, out):
    out[...] = jnp.sum((weight[...].astype(jnp.float32) * products[...]).reshape(32, 64, 2 * COLS), axis=-1)


def grad(weight, products):
    return pl.pallas_call(
        grad_body,
        out_shape=jax.ShapeDtypeStruct((32, 64), jnp.float32),
        in_specs=[VM, VM],
        out_specs=VM,
        compiler_params=params(),
        name="gain_grad",
    )(weight, products)


def attend_body(place, weight, m0, m1, m2, m3, s0, s1, s2, s3, out):
    rows = GH * DEC
    row_head = lax.broadcasted_iota(jnp.int32, (rows, COLS), 0) // DEC
    col_head = lax.broadcasted_iota(jnp.int32, (rows, COLS), 1) // HEAD_DIM
    same = row_head == col_head
    spot = (lax.broadcasted_iota(jnp.int32, (1, TOK), 1) // LEN).astype(jnp.float32)
    upper = place[1] == 1
    for r, (message, scaled) in enumerate(((m0, s0), (m1, s1), (m2, s2), (m3, s3))):
        states = jnp.dot(scaled[...], weight[...], preferred_element_type=jnp.float32).astype(jnp.bfloat16)
        query = jnp.where(
            upper,
            message[:, COLS : 2 * COLS].astype(jnp.float32),
            message[:, :COLS].astype(jnp.float32),
        )
        spread = jnp.where(same, jnp.concatenate([query] * GH, axis=0), 0.0).astype(jnp.bfloat16)
        scores = lax.dot_general(
            spread, states[:, :COLS], (((1,), (1,)), ((), ())), preferred_element_type=jnp.float32
        ) * HEAD_DIM ** (-0.5)
        count = message[:, 2 * COLS : 2 * COLS + TOK].astype(jnp.float32)[0:1, :]
        scores = jnp.where(spot < count, scores, -jnp.inf)
        raised = jnp.exp(scores - jnp.max(scores, axis=-1, keepdims=True))
        weights = (raised / jnp.sum(raised, axis=-1, keepdims=True)).astype(jnp.bfloat16)
        mixed = jnp.dot(weights, states[:, COLS:], preferred_element_type=jnp.float32)
        mixed = jnp.where(same, mixed, 0.0).reshape(GH, DEC, COLS)
        out[(2 * place[0] + place[1]) ^ r] = jnp.sum(mixed, axis=0).astype(jnp.bfloat16)


def attend(place, weight, messages, scaled):
    last = pl.BlockSpec((DEC, D), lambda i: (QROW // DEC, 0))
    return pl.pallas_call(
        attend_body,
        out_shape=jax.ShapeDtypeStruct((G, DEC, COLS), jnp.bfloat16),
        grid=(1,),
        in_specs=[SM, pl.BlockSpec((D, 2 * COLS), lambda i: (0, 0))]
        + [last] * G
        + [pl.BlockSpec((TOK, D), lambda i: (0, 0))] * G,
        out_specs=pl.BlockSpec((G, DEC, COLS), lambda i: (0, 0, 0)),
        compiler_params=params(),
        name="attend",
    )(place, weight, *messages, *scaled)


def exchange(array, axes):
    return lax.all_to_all(array, axes, 0, 0, tiled=True)


def spread_to(array, axis):
    return exchange(jnp.broadcast_to(array[None], (lax.axis_size(axis), *array.shape)), axis)


def swap(array, axis):
    return lax.ppermute(array, axis, [(0, 1), (1, 0)])


def forward(passages, counts, helper_table, norm_gain, projection, queries, cotangent):
    zl, core = lax.axis_index("zl").astype(jnp.int32), lax.axis_index("core").astype(jnp.int32)
    place = jnp.stack([zl, core])
    member = (zl * 2 + core).reshape(1)
    gain = norm_gain.reshape(1, D)

    near, far = prep(
        place, counts.reshape(1), passages.reshape(TOK, D), cotangent.reshape(ENC * LEN, D), queries.reshape(DEC, HW)
    )
    m_z = swap(far, "zl")
    m_c = swap(near, "core")
    m_cz = swap(m_z, "core")
    messages = (near, m_c, m_z, m_cz)

    outgoing = pack(helper_table.reshape(2, PMAX - KEEP), passages.reshape(PMAX, LEN, D))
    arrived = exchange(outgoing, FSDP)
    s_0, s_1 = scale(near, gain), scale(m_c, gain)
    tags = arrived[:, 0, D].astype(jnp.int32)
    h_own = unpack(tags, arrived).reshape(AID, D)
    h_z = swap(h_own, "zl")
    h_c = swap(h_own, "core")
    h_cz = swap(h_z, "core")

    mine = columns(member, projection)
    mine, s_0, s_1, _ = lax.optimization_barrier((mine, s_0, s_1, h_own))
    by_y = exchange(mine, "y").reshape(512, 2 * COLS)
    weight = spread_to(by_y, "x").reshape(D, 2 * COLS)
    s_2, s_3 = scale(m_z, gain), scale(m_cz, gain)
    products = outer(place, messages, (h_own, h_c, h_z, h_cz))
    weight, s_2, s_3, products = lax.optimization_barrier((weight, s_2, s_3, products))
    scaled = (s_0, s_1, s_2, s_3)

    row_terms = grad(weight, products)
    parts = exchange(row_terms.reshape(32, 1, 64), FSDP)
    share = jnp.sum(parts, axis=0)
    gathered = exchange(jnp.broadcast_to(share[None], (16, 1, 64)), DP)
    gradient = jnp.sum(gathered, axis=0).reshape(64)

    context = exchange(attend(place, weight, messages, scaled), GROUP)
    context_out = jnp.transpose(context, (1, 0, 2)).reshape(1, 1, DEC, HW)
    return (context_out, gradient)


def solution(mesh):
    split = Mesh(mesh.devices.reshape(4, 2, 2, 4, 8), ("zh", "zl", "core", "x", "y"))
    return jax.shard_map(
        forward,
        mesh=split,
        in_specs=(
            P(DP, FSDP, None, None, None),
            P(DP, FSDP),
            P(DP, FSDP, None, None),
            P(),
            P(FSDP, None),
            P(DP, FSDP, None, None),
            P(DP, FSDP, None, None, None),
        ),
        out_specs=(P(DP, FSDP, None, None), P(FSDP)),
        check_vma=False,
    )
```

time: 170 us -> 158 us (0.929)
  waiting for transfers between devices: 67.5 us -> 33.2 us
  blocking collectives: 0 us -> 17.7 us
  Pallas kernels: 22.7 us -> 30.4 us
  starting transfers between devices: 63.4 us -> 57.1 us
  local copies, waits for them, and re-layouts: 11.6 us -> 14.9 us
    all_to_all x7 -> x5, waiting for transfers between devices: 56.1 us -> 13.2 us  [exchange(): return lax.all_to_all(array, axes, 0, 0, tiled=True)]
    all_to_all x0 -> x1, blocking collectives: none -> 17.7 us  [exchange(): return lax.all_to_all(array, axes, 0, 0, tiled=True)]
    pallas_call x3 -> x8, Pallas kernels: 11.7 us -> 20.8 us  [the longest x1 9.03 us: outer(): pl.pallas_call(outer_body, out_shape=jax.ShapeDtypeStruct((D, 2 * COLS),...]
    all_to_all x7 -> x5, starting transfers between devices: 44.2 us -> 35.5 us  [exchange(): return lax.all_to_all(array, axes, 0, 0, tiled=True)]
    ppermute x6, waiting for transfers between devices: 11.4 us -> 19.9 us  [swap(): return lax.ppermute(array, axis, [(0, 1), (1, 0)])]
    unnamed x23 -> x44, local copies, waits for them, and re-layouts: 5.05 us -> 12.1 us
    ppermute x6, starting transfers between devices: 19.2 us -> 21.6 us  [swap(): return lax.ppermute(array, axis, [(0, 1), (1, 0)])]
    reshape x3 -> x1, local copies, waits for them, and re-layouts: 2.51 us -> 0.63 us  [forward(): context_out = jnp.transpose(context, (1, 0, 2)).reshape(1, 1, DEC, HW)]
  transfers between devices with their start and end apart: 13 -> 11, of which waited for: 7 -> 4; matrix products, arithmetic and copies ran while one was open for 2% -> 2% of each run, Pallas kernels for 10% -> 16%
where the time goes in v2:
time: 158 us; the launch traced here: 157 us
  starting transfers between devices  57.1 us (36%)
  waiting for transfers between devices  33.2 us (21%)
  Pallas kernels  30.4 us (19%)
  blocking collectives  17.7 us (11%)
  local copies, waits for them, and re-layouts  14.9 us (9%)
  other arithmetic  2.15 us (1%)
    all_to_all x5, starting transfers between devices, exchange(): return lax.all_to_all(array, axes, 0, 0, tiled=True)  35.5 us
    ppermute x6, starting transfers between devices, swap(): return lax.ppermute(array, axis, [(0, 1), (1, 0)])  21.6 us
    ppermute x6, waiting for transfers between devices, swap(): return lax.ppermute(array, axis, [(0, 1), (1, 0)])  19.9 us
    all_to_all x1, blocking collectives, exchange(): return lax.all_to_all(array, axes, 0, 0, tiled=True)  17.7 us
    all_to_all x5, waiting for transfers between devices, exchange(): return lax.all_to_all(array, axes, 0, 0, tiled=True)  13.2 us
    unnamed x44, local copies, waits for them, and re-layouts  12.1 us
    pallas_call x1, Pallas kernels, outer(): pl.pallas_call(outer_body, out_shape=jax.ShapeDtypeStruct((D, 2 * COLS),...  9.03 us
    pallas_call x1, Pallas kernels, attend(): pl.pallas_call(attend_body, out_shape=jax.ShapeDtypeStruct((G, DEC, COLS)...  6.24 us
  transfers between devices with their start and end apart: 11, of which 4 were waited for; matrix products, arithmetic and copies ran while one was open for 2% of the time, Pallas kernels for 16%

profile of v2, /device:TPU:1, one launch (start us, length us, event | category | flops | bytes accessed | tf_op | source)
XLA Modules:
  0.0 156.9 jit_solution(15425201886662983149)
XLA Ops:
  0.6 1.3 copy-done.5
  2.6 1.8 %pack.1 = bf16[32,8,2176]{2,1,0:T(8,128)(2,1)} custom-call(s32[2,32]{1,0:T(2,128)S(1)} %bitcast.33, bf16[40,8,2048]{2,1,0:T(8,128)(2,1)S(1)} %bitcast.21), custom_call_target="tpu_custom_call" | custom-call | tf_op jit(solution)/shard_map/pack/pallas_call | solution.py:56
  4.4 10.7 %all-to-all-start = ((bf16[32,8,2176]{2,1,0:T(8,128)(2,1)}), bf16[32,8,2176]{2,1,0:T(8,128)(2,1)}, u32[]{:S(2)}, u32[]{:S(2)}) async-start(bf16[32,8,2176]{2,1,0:T(8,128)(2,1)} %pack.1), calls=%async_computation | async-start | bytes 2228224 | tf_op jit(solution)/shard_map/all_to_all | solution.py:275
  15.9 1.1 copy-done.17
  17.1 2.0 %prep.1 = (bf16[432,2048]{1,0:T(8,128)(2,1)S(1)}, bf16[432,2048]{1,0:T(8,128)(2,1)}) custom-call(s32[2]{0:T(128)S(1)} %pad_add_fusion.place, s32[1]{0:T(128)} %bitcast.18.count, bf16[320,2048]{1,0:T(8,128)(2,1)S(1)} %bitcast.22, bf16[192,2048]{1,0:T(8,128)(2,1)S(1)} %bitcast.26, bf16[16,1024]{1,0:T(8,128)(2,1)S(1)} %bitcast.32), custom_call_target="tpu_custom_call" | custom-call | tf_op jit(solution)/shard_map/prep/pallas_call | solution.py:90
  19.1 2.9 %collective-permute-start = (bf16[432,2048]{1,0:T(8,128)(2,1)S(1)}, bf16[432,2048]{1,0:T(8,128)(2,1)S(1)}, u32[]{:S(2)}, u32[]{:S(2)}) collective-permute-start(bf16[432,2048]{1,0:T(8,128)(2,1)S(1)} %get-tuple-element.11.message.m0), channel_id=1, source_target_pairs={{0,32},{32,0},{1,33},{33,1},{2,34},{34,2},{3,35},{35,3},{4,36},{36... | collective-permute-start | bytes 5308424 | tf_op jit(solution)/shard_map/ppermute | solution.py:283
  22.0 4.0 %collective-permute-start.1 = (bf16[432,2048]{1,0:T(8,128)(2,1)}, bf16[432,2048]{1,0:T(8,128)(2,1)}, u32[]{:S(2)}, u32[]{:S(2)}) collective-permute-start(bf16[432,2048]{1,0:T(8,128)(2,1)} %get-tuple-element.13), channel_id=1, source_target_pairs={{0,64},{64,0},{1,65},{65,1},{2,66},{66,2},{3,67},{67,3},{4,68},{68... | collective-permute-start | bytes 5308424 | tf_op jit(solution)/shard_map/ppermute | solution.py:283
  29.9 1.1 copy-done.9
  31.0 10.6 %all-to-all-done.arrived = bf16[32,8,2176]{2,1,0:T(8,128)(2,1)} async-done(((bf16[32,8,2176]{2,1,0:T(8,128)(2,1)}), bf16[32,8,2176]{2,1,0:T(8,128)(2,1)}, u32[]{:S(2)}, u32[]{:S(2)}) %all-to-all-start) | async-done | bytes 1114144 | tf_op jit(solution)/shard_map/all_to_all | solution.py:275
  41.6 1.5 fusion.tags
  43.1 1.6 unpack.1
  45.5 6.0 %all-to-all-start.1 = ((bf16[8,64,512]{2,1,0:T(8,128)(2,1)}), bf16[8,64,512]{2,1,0:T(8,128)(2,1)S(1)}, u32[]{:S(2)}, u32[]{:S(2)}) async-start(bf16[8,64,512]{2,1,0:T(8,128)(2,1)} %columns.1), calls=%async_computation.1 | async-start | bytes 1048576 | tf_op jit(solution)/shard_map/all_to_all | solution.py:275
  51.4 13.8 %collective-permute-done.1.message.m2 = bf16[432,2048]{1,0:T(8,128)(2,1)} collective-permute-done((bf16[432,2048]{1,0:T(8,128)(2,1)}, bf16[432,2048]{1,0:T(8,128)(2,1)}, u32[]{:S(2)}, u32[]{:S(2)}) %collective-permute-start.1) | collective-permute-done | bytes 1769504 | tf_op jit(solution)/shard_map/ppermute | solution.py:283
  65.3 2.5 %collective-permute-start.2 = (bf16[432,2048]{1,0:T(8,128)(2,1)}, bf16[432,2048]{1,0:T(8,128)(2,1)}, u32[]{:S(2)}, u32[]{:S(2)}) collective-permute-start(bf16[432,2048]{1,0:T(8,128)(2,1)} %collective-permute-done.1.message.m2), channel_id=1, source_target_pairs={{0,32},{32,0},{1,33},{33,1},{2,34},{34,2},{3,35},{35,3},{4,36},{36... | collective-permute-start | bytes 5308424 | tf_op jit(solution)/shard_map/ppermute | solution.py:283
  67.8 1.5 broadcast_in_dim.14
  69.3 4.4 %all-to-all-start.2 = ((bf16[4,512,512]{2,1,0:T(8,128)(2,1)}), bf16[4,512,512]{2,1,0:T(8,128)(2,1)S(1)}, u32[]{:S(2)}, u32[]{:S(2)}) async-start(bf16[4,512,512]{2,1,0:T(8,128)(2,1)} %broadcast_in_dim.14), calls=%async_computation.2 | async-start | bytes 4194304 | tf_op jit(solution)/shard_map/all_to_all | solution.py:275
  73.7 3.6 %collective-permute-start.4 = (bf16[128,2048]{1,0:T(8,128)(2,1)S(1)}, bf16[128,2048]{1,0:T(8,128)(2,1)S(1)}, u32[]{:S(2)}, u32[]{:S(2)}) collective-permute-start(bf16[128,2048]{1,0:T(8,128)(2,1)S(1)} %bitcast.23), channel_id=1, source_target_pairs={{0,64},{64,0},{1,65},{65,1},{2,66},{66,2},{3,67},{67,3},{4,68},{68... | collective-permute-start | bytes 1572872 | tf_op jit(solution)/shard_map/ppermute | solution.py:283
  77.2 4.2 %collective-permute-start.3 = (bf16[128,2048]{1,0:T(8,128)(2,1)S(1)}, bf16[128,2048]{1,0:T(8,128)(2,1)S(1)}, u32[]{:S(2)}, u32[]{:S(2)}) collective-permute-start(bf16[128,2048]{1,0:T(8,128)(2,1)S(1)} %bitcast.24), channel_id=1, source_target_pairs={{0,32},{32,0},{1,33},{33,1},{2,34},{34,2},{3,35},{35,3},{4,36},{36... | collective-permute-start | bytes 1572872 | tf_op jit(solution)/shard_map/ppermute | solution.py:283
  81.4 6.1 %collective-permute-done.4.h2 = bf16[128,2048]{1,0:T(8,128)(2,1)S(1)} collective-permute-done((bf16[128,2048]{1,0:T(8,128)(2,1)S(1)}, bf16[128,2048]{1,0:T(8,128)(2,1)S(1)}, u32[]{:S(2)}, u32[]{:S(2)}) %collective-permute-start.4) | collective-permute-done | bytes 524320 | tf_op jit(solution)/shard_map/ppermute | solution.py:283
  87.5 4.5 %collective-permute-start.5 = (bf16[128,2048]{1,0:T(8,128)(2,1)S(1)}, bf16[128,2048]{1,0:T(8,128)(2,1)S(1)}, u32[]{:S(2)}, u32[]{:S(2)}) collective-permute-start(bf16[128,2048]{1,0:T(8,128)(2,1)S(1)} %collective-permute-done.4.h2), channel_id=1, source_target_pairs={{0,32},{32,0},{1,33},{33,1},{2,34},{34,2},{3,35},{35,3},{4,36},{36... | collective-permute-start | bytes 1572872 | tf_op jit(solution)/shard_map/ppermute | solution.py:283
  92.0 1.9 %scale.6.s2 = bf16[320,2048]{1,0:T(8,128)(2,1)S(1)} custom-call(bf16[432,2048]{1,0:T(8,128)(2,1)} %collective-permute-done.1.message.m2, f32[1,2048]{1,0:T(1,128)S(1)} %bitcast.29), custom_call_target="tpu_custom_call" | custom-call | tf_op jit(solution)/shard_map/scale/pallas_call | solution.py:153
  94.0 2.3 %scale.7.s3 = bf16[320,2048]{1,0:T(8,128)(2,1)S(1)} custom-call(bf16[432,2048]{1,0:T(8,128)(2,1)} %collective-permute-done.2.message.m3, f32[1,2048]{1,0:T(1,128)S(1)} %bitcast.30), custom_call_target="tpu_custom_call" | custom-call | tf_op jit(solution)/shard_map/scale/pallas_call | solution.py:153
  97.5 9.0 %outer.1.products = f32[2048,512]{1,0:T(8,128)} custom-call(s32[2]{0:T(128)S(1)} %pad_add_fusion.place, bf16[432,2048]{1,0:T(8,128)(2,1)S(1)} %copy-done.2, bf16[432,2048]{1,0:T(8,128)(2,1)S(1)} %copy-done.4, bf16[432,2048]{1,0:T(8,128)(2,1)} %collective-permute-done.1.message.m2, bf16[432,2048]{1,0:T(8,128)(2,1)} %collective-permute-done.2.message.m3, ...), custom_call_target="tpu_custom_call" | custom-call | tf_op jit(solution)/shard_map/outer/pallas_call | solution.py:202
  106.5 3.6 %gain_grad.1 = f32[32,64]{1,0:T(8,128)S(1)} custom-call(bf16[2048,512]{1,0:T(8,128)(2,1)S(1)} %bitcast.19, f32[2048,512]{1,0:T(8,128)} %outer.1.products), custom_call_target="tpu_custom_call" | custom-call | tf_op jit(solution)/shard_map/gain_grad/pallas_call | solution.py:222
  110.1 17.7 %all_to_all.30 = f32[32,1,64]{2,1,0:T(1,128)S(1)} all-to-all(f32[32,1,64]{2,1,0:T(1,128)S(1)} %bitcast.31), channel_id=1, replica_groups=mesh['zh'=4,'zl'=2,'core'=2,'x'=4,'y'=8] {'x','y'}, dimensions={0} | all-to-all | bytes 16384 | tf_op jit(solution)/shard_map/all_to_all | solution.py:275
  128.4 11.1 %all-to-all-start.5 = ((f32[16,1,64]{2,1,0:T(1,128)}), f32[16,1,64]{2,1,0:T(1,128)S(1)}, u32[]{:S(2)}, u32[]{:S(2)}) async-start(f32[16,1,64]{2,1,0:T(1,128)} %broadcast_in_dim.15), calls=%async_computation.5 | async-start | bytes 16384 | tf_op jit(solution)/shard_map/all_to_all | solution.py:275
  139.6 1.3 copy-done.10
  140.9 1.3 copy-done.12
  142.2 1.3 copy-done.14
  143.5 6.2 %attend.1 = bf16[4,16,256]{2,1,0:T(8,128)(2,1)} custom-call(s32[2]{0:T(128)S(1)} %pad_add_fusion.place, bf16[2048,512]{1,0:T(8,128)(2,1)} %bitcast.20, bf16[432,2048]{1,0:T(8,128)(2,1)} %copy-done.1, bf16[432,2048]{1,0:T(8,128)(2,1)} %copy-done.3, bf16[432,2048]{1,0:T(8,128)(2,1)} %collective-permute-done.1.message.m2, ...), custom_call_target="tpu_custom_call" | custom-call | tf_op jit(solution)/shard_map/attend/pallas_call | solution.py:261
  149.8 3.3 %all-to-all-start.3 = ((bf16[4,16,256]{2,1,0:T(8,128)(2,1)}), bf16[4,16,256]{2,1,0:T(8,128)(2,1)S(1)}, u32[]{:S(2)}, u32[]{:S(2)}) async-start(bf16[4,16,256]{2,1,0:T(8,128)(2,1)} %attend.1), calls=%async_computation.3 | async-start | bytes 65536 | tf_op jit(solution)/shard_map/all_to_all | solution.py:275
  153.6 2.6 %all-to-all-done.3 = bf16[4,16,256]{2,1,0:T(8,128)(2,1)S(1)} async-done(((bf16[4,16,256]{2,1,0:T(8,128)(2,1)}), bf16[4,16,256]{2,1,0:T(8,128)(2,1)S(1)}, u32[]{:S(2)}, u32[]{:S(2)}) %all-to-all-start.3) | async-done | bytes 32800 | tf_op jit(solution)/shard_map/all_to_all | solution.py:275
  (54 shorter events, 8.4 us)
Async XLA Ops:
  0.6 1.3 copy-start.5
  2.6 13.3 %copy-start.6 = (bf16[1,1,40,8,2048]{4,3,2,1,0:T(8,128)(2,1)S(1)}, bf16[1,1,40,8,2048]{4,3,2,1,0:T(8,128)(2,1)}, u32[]{:S(2)}) copy-start(bf16[1,1,40,8,2048]{4,3,2,1,0:T(8,128)(2,1)} %param.7) | copy-start | bytes 3932164
  2.6 13.3 %copy-start.20 = (bf16[1,1,16,1024]{3,2,1,0:T(8,128)(2,1)S(1)}, bf16[1,1,16,1024]{3,2,1,0:T(8,128)(2,1)}, u32[]{:S(2)}) copy-start(bf16[1,1,16,1024]{3,2,1,0:T(8,128)(2,1)} %param.12) | copy-start | bytes 98308
  4.4 21.6 %copy-start.19 = (f32[2048]{0:T(1024)S(1)}, f32[2048]{0:T(1024)}, u32[]{:S(2)}) copy-start(f32[2048]{0:T(1024)} %param.10) | copy-start | bytes 24580
  4.4 37.2 %all-to-all-start = ((bf16[32,8,2176]{2,1,0:T(8,128)(2,1)}), bf16[32,8,2176]{2,1,0:T(8,128)(2,1)}, u32[]{:S(2)}, u32[]{:S(2)}) async-start(bf16[32,8,2176]{2,1,0:T(8,128)(2,1)} %pack.1), calls=%async_computation | async-start | bytes 2228224 | tf_op jit(solution)/shard_map/all_to_all | solution.py:275
  15.9 1.1 copy-start.17
  19.1 10.3 %copy-start.1 = (bf16[432,2048]{1,0:T(8,128)(2,1)}, bf16[432,2048]{1,0:T(8,128)(2,1)S(1)}, u32[]{:S(2)}) copy-start(bf16[432,2048]{1,0:T(8,128)(2,1)S(1)} %get-tuple-element.11.message.m0) | copy-start | bytes 5308420
  19.1 10.3 %collective-permute-start = (bf16[432,2048]{1,0:T(8,128)(2,1)S(1)}, bf16[432,2048]{1,0:T(8,128)(2,1)S(1)}, u32[]{:S(2)}, u32[]{:S(2)}) collective-permute-start(bf16[432,2048]{1,0:T(8,128)(2,1)S(1)} %get-tuple-element.11.message.m0), channel_id=1, source_target_pairs={{0,32},{32,0},{1,33},{33,1},{2,34},{34,2},{3,35},{35,3},{4,36},{36... | collective-permute-start | bytes 5308424 | tf_op jit(solution)/shard_map/ppermute | solution.py:283
  22.0 43.3 %collective-permute-start.1 = (bf16[432,2048]{1,0:T(8,128)(2,1)}, bf16[432,2048]{1,0:T(8,128)(2,1)}, u32[]{:S(2)}, u32[]{:S(2)}) collective-permute-start(bf16[432,2048]{1,0:T(8,128)(2,1)} %get-tuple-element.13), channel_id=1, source_target_pairs={{0,64},{64,0},{1,65},{65,1},{2,66},{66,2},{3,67},{67,3},{4,68},{68... | collective-permute-start | bytes 5308424 | tf_op jit(solution)/shard_map/ppermute | solution.py:283
  26.5 1.1 copy-start.7
  27.6 0.9 copy-start.18
  29.4 15.3 %copy-start.3 = (bf16[432,2048]{1,0:T(8,128)(2,1)}, bf16[432,2048]{1,0:T(8,128)(2,1)S(1)}, u32[]{:S(2)}) copy-start(bf16[432,2048]{1,0:T(8,128)(2,1)S(1)} %collective-permute-done.message.m1) | copy-start | bytes 5308420
  29.9 1.1 copy-start.9
  44.7 0.8 copy-start.15
  45.5 22.3 %all-to-all-start.1 = ((bf16[8,64,512]{2,1,0:T(8,128)(2,1)}), bf16[8,64,512]{2,1,0:T(8,128)(2,1)S(1)}, u32[]{:S(2)}, u32[]{:S(2)}) async-start(bf16[8,64,512]{2,1,0:T(8,128)(2,1)} %columns.1), calls=%async_computation.1 | async-start | bytes 1048576 | tf_op jit(solution)/shard_map/all_to_all | solution.py:275
  65.3 28.7 %collective-permute-start.2 = (bf16[432,2048]{1,0:T(8,128)(2,1)}, bf16[432,2048]{1,0:T(8,128)(2,1)}, u32[]{:S(2)}, u32[]{:S(2)}) collective-permute-start(bf16[432,2048]{1,0:T(8,128)(2,1)} %collective-permute-done.1.message.m2), channel_id=1, source_target_pairs={{0,32},{32,0},{1,33},{33,1},{2,34},{34,2},{3,35},{35,3},{4,36},{36... | collective-permute-start | bytes 5308424 | tf_op jit(solution)/shard_map/ppermute | solution.py:283
  69.3 4.4 %copy-start.16 = (bf16[16,8,2048]{2,1,0:T(8,128)(2,1)S(1)}, bf16[16,8,2048]{2,1,0:T(8,128)(2,1)}, u32[]{:S(2)}) copy-start(bf16[16,8,2048]{2,1,0:T(8,128)(2,1)} %copy-done.15) | copy-start | bytes 1572868
  69.3 37.2 %all-to-all-start.2 = ((bf16[4,512,512]{2,1,0:T(8,128)(2,1)}), bf16[4,512,512]{2,1,0:T(8,128)(2,1)S(1)}, u32[]{:S(2)}, u32[]{:S(2)}) async-start(bf16[4,512,512]{2,1,0:T(8,128)(2,1)} %broadcast_in_dim.14), calls=%async_computation.2 | async-start | bytes 4194304 | tf_op jit(solution)/shard_map/all_to_all | solution.py:275
  73.7 13.9 %collective-permute-start.4 = (bf16[128,2048]{1,0:T(8,128)(2,1)S(1)}, bf16[128,2048]{1,0:T(8,128)(2,1)S(1)}, u32[]{:S(2)}, u32[]{:S(2)}) collective-permute-start(bf16[128,2048]{1,0:T(8,128)(2,1)S(1)} %bitcast.23), channel_id=1, source_target_pairs={{0,64},{64,0},{1,65},{65,1},{2,66},{66,2},{3,67},{67,3},{4,68},{68... | collective-permute-start | bytes 1572872 | tf_op jit(solution)/shard_map/ppermute | solution.py:283
  77.2 20.2 %collective-permute-start.3 = (bf16[128,2048]{1,0:T(8,128)(2,1)S(1)}, bf16[128,2048]{1,0:T(8,128)(2,1)S(1)}, u32[]{:S(2)}, u32[]{:S(2)}) collective-permute-start(bf16[128,2048]{1,0:T(8,128)(2,1)S(1)} %bitcast.24), channel_id=1, source_target_pairs={{0,32},{32,0},{1,33},{33,1},{2,34},{34,2},{3,35},{35,3},{4,36},{36... | collective-permute-start | bytes 1572872 | tf_op jit(solution)/shard_map/ppermute | solution.py:283
  87.5 9.9 %collective-permute-start.5 = (bf16[128,2048]{1,0:T(8,128)(2,1)S(1)}, bf16[128,2048]{1,0:T(8,128)(2,1)S(1)}, u32[]{:S(2)}, u32[]{:S(2)}) collective-permute-start(bf16[128,2048]{1,0:T(8,128)(2,1)S(1)} %collective-permute-done.4.h2), channel_id=1, source_target_pairs={{0,32},{32,0},{1,33},{33,1},{2,34},{34,2},{3,35},{35,3},{4,36},{36... | collective-permute-start | bytes 1572872 | tf_op jit(solution)/shard_map/ppermute | solution.py:283
  92.0 5.4 %copy-start.4 = (bf16[432,2048]{1,0:T(8,128)(2,1)S(1)}, bf16[432,2048]{1,0:T(8,128)(2,1)}, u32[]{:S(2)}) copy-start(bf16[432,2048]{1,0:T(8,128)(2,1)} %copy-done.3) | copy-start | bytes 5308420
  94.0 3.5 %copy-start.11 = (bf16[320,2048]{1,0:T(8,128)(2,1)}, bf16[320,2048]{1,0:T(8,128)(2,1)S(1)}, u32[]{:S(2)}) copy-start(bf16[320,2048]{1,0:T(8,128)(2,1)S(1)} %scale.6.s2) | copy-start | bytes 3932164
  94.0 3.5 %copy-start.2 = (bf16[432,2048]{1,0:T(8,128)(2,1)S(1)}, bf16[432,2048]{1,0:T(8,128)(2,1)}, u32[]{:S(2)}) copy-start(bf16[432,2048]{1,0:T(8,128)(2,1)} %copy-done.1) | copy-start | bytes 5308420
  96.3 1.1 copy-start.13
  106.5 3.6 %copy-start = (bf16[4,512,512]{2,1,0:T(8,128)(2,1)}, bf16[4,512,512]{2,1,0:T(8,128)(2,1)S(1)}, u32[]{:S(2)}) copy-start(bf16[4,512,512]{2,1,0:T(8,128)(2,1)S(1)} %all-to-all-done.2) | copy-start | bytes 6291460
  106.5 33.1 %copy-start.8 = (bf16[320,2048]{1,0:T(8,128)(2,1)S(1)}, bf16[320,2048]{1,0:T(8,128)(2,1)}, u32[]{:S(2)}) copy-start(bf16[320,2048]{1,0:T(8,128)(2,1)} %copy-done.7) | copy-start | bytes 3932164
  128.4 21.3 %all-to-all-start.5 = ((f32[16,1,64]{2,1,0:T(1,128)}), f32[16,1,64]{2,1,0:T(1,128)S(1)}, u32[]{:S(2)}, u32[]{:S(2)}) async-start(f32[16,1,64]{2,1,0:T(1,128)} %broadcast_in_dim.15), calls=%async_computation.5 | async-start | bytes 16384 | tf_op jit(solution)/shard_map/all_to_all | solution.py:275
  139.6 1.3 copy-start.10
  140.9 1.3 copy-start.12
  142.2 1.3 copy-start.14
  149.8 6.5 %all-to-all-start.3 = ((bf16[4,16,256]{2,1,0:T(8,128)(2,1)}), bf16[4,16,256]{2,1,0:T(8,128)(2,1)S(1)}, u32[]{:S(2)}, u32[]{:S(2)}) async-start(bf16[4,16,256]{2,1,0:T(8,128)(2,1)} %attend.1), calls=%async_computation.3 | async-start | bytes 65536 | tf_op jit(solution)/shard_map/all_to_all | solution.py:275
  (1 other events, 0.7 us)

commit v3 on v2

--- a/solution.py
+++ b/solution.py
@@ -27,19 +27,35 @@
 MROWS = QROW + DEC
 WIDE = D + 128
 EPSILON = 1e-06
+CHUNKS = 4
 GROUP = ("zl", "core")
 DP = ("zh", "zl", "core")
 FSDP = ("x", "y")
 
 VM = pl.BlockSpec(memory_space=pltpu.VMEM)
 SM = pl.BlockSpec(memory_space=pltpu.SMEM)
+HB = pl.BlockSpec(memory_space=pltpu.HBM)
+
+
+def in_hbm(array):
+    return pltpu.with_memory_space_constraint(array, pltpu.HBM)
 
 
 def params():
-    return pltpu.CompilerParams(vmem_limit_bytes=48 * 1024 * 1024)
-
-
-def pack_body(table, passages, out):
+    return pltpu.CompilerParams(vmem_limit_bytes=24 * 1024 * 1024)
+
+
+def pack_body(table, passages, out, arrivals):
+    def copy(e):
+        peer = jnp.maximum(table[0, e], 0)
+        return pltpu.make_async_copy(passages.at[KEEP + e], out.at[peer, :, pl.ds(0, D)], arrivals.at[e])
+
+    for e in range(PMAX - KEEP):
+
+        @pl.when(table[0, e] >= 0)
+        def _():
+            copy(e).start()
+
     for s in range(32):
         out[s, :, D:] = jnp.full((LEN, WIDE - D), -1.0, jnp.bfloat16)
     for e in range(PMAX - KEEP):
@@ -48,19 +64,25 @@
         @pl.when(peer >= 0)
         def _():
             slot = table[1, e].astype(jnp.float32)
-            out[peer, :, :D] = passages[KEEP + e]
             out[peer, :, D:] = jnp.full((LEN, WIDE - D), slot, jnp.float32).astype(jnp.bfloat16)
+
+    for e in range(PMAX - KEEP):
+
+        @pl.when(table[0, e] >= 0)
+        def _():
+            copy(e).wait()
 
 
 def pack(table, passages):
     return pl.pallas_call(
         pack_body,
         out_shape=jax.ShapeDtypeStruct((32, LEN, WIDE), jnp.bfloat16),
-        in_specs=[SM, VM],
+        in_specs=[SM, HB],
         out_specs=VM,
+        scratch_shapes=[pltpu.SemaphoreType.DMA((PMAX - KEEP,))],
         compiler_params=params(),
         name="pack",
-    )(table, passages)
+    )(table, in_hbm(passages))
 
 
 def prep_body(place, count, passages, cot, queries, near, far):
@@ -144,34 +166,27 @@
     return lax.rsqrt(jnp.mean(values * values, axis=-1, keepdims=True) + EPSILON)
 
 
-def scale_body(message, gain, out):
-    values = message[...].astype(jnp.float32)
-    out[...] = (values * inverse_rms(values) * gain[...]).astype(jnp.bfloat16)
-
-
-def scale(message, gain):
-    return pl.pallas_call(
-        scale_body,
-        out_shape=jax.ShapeDtypeStruct((TOK, D), jnp.bfloat16),
-        grid=(1,),
-        in_specs=[pl.BlockSpec((TOK, D), lambda i: (0, 0)), pl.BlockSpec((1, D), lambda i: (0, 0))],
-        out_specs=pl.BlockSpec((TOK, D), lambda i: (0, 0)),
-        compiler_params=params(),
-        name="scale",
-    )(message, gain)
-
-
-def outer_body(place, m0, m1, m2, m3, h0, h1, h2, h3, out, rows, high, low):
+def outer_body(place, m0, m1, m2, m3, h0, h1, h2, h3, out, rows, tails, high, low, total, arrivals, leaving):
+    messages = (m0, m1, m2, m3)
+    size = ENC * LEN
+    copies = []
+    for r, message in enumerate(messages):
+        own = pltpu.make_async_copy(message.at[pl.ds(0, OWN)], rows.at[pl.ds(r * size, OWN)], arrivals.at[r, 0])
+        tail = pltpu.make_async_copy(message.at[pl.ds(TOK, MROWS - TOK)], tails.at[r], arrivals.at[r, 1])
+        own.start()
+        tail.start()
+        copies.append((own, tail))
     spot = (lax.broadcasted_iota(jnp.int32, (OWN, 1), 0) // LEN).astype(jnp.float32)
-    for r, (message, aid) in enumerate(((m0, h0), (m1, h1), (m2, h2), (m3, h3))):
-        at = r * ENC * LEN
-        own = message[:OWN, :]
+    for r, aid in enumerate((h0, h1, h2, h3)):
+        at = r * size
         helped = aid[...]
-        rows[at : at + OWN, :] = own
-        rows[at + OWN : at + ENC * LEN, :] = helped
-        count = message[QROW : QROW + DEC, 2 * COLS : 2 * COLS + 128].astype(jnp.float32)[0:1, 0:1]
-        own_scale = jnp.where(spot < count, inverse_rms(own.astype(jnp.float32)), 0.0)
-        scales = jnp.concatenate([own_scale, inverse_rms(helped.astype(jnp.float32))], axis=0)
+        rows[at + OWN : at + size, :] = helped
+        helped_scale = inverse_rms(helped.astype(jnp.float32))
+        for copy in copies[r]:
+            copy.wait()
+        count = tails[r, QROW - TOK :, 2 * COLS : 2 * COLS + 128].astype(jnp.float32)[0:1, 0:1]
+        own_scale = jnp.where(spot < count, inverse_rms(rows[at : at + OWN, :].astype(jnp.float32)), 0.0)
+        scales = jnp.concatenate([own_scale, helped_scale], axis=0)
         for c in range(2):
 
             @pl.when(place[1] == c)
@@ -179,96 +194,152 @@
                 left = 4 * c * COLS
                 cot = jnp.concatenate(
                     [
-                        message[TOK:CROW, left : left + 2 * COLS],
-                        message[TOK:CROW, left + 2 * COLS : left + 4 * COLS],
+                        tails[r, : CROW - TOK, left : left + 2 * COLS],
+                        tails[r, : CROW - TOK, left + 2 * COLS : left + 4 * COLS],
                     ],
                     axis=0,
                 )
                 product = cot.astype(jnp.float32) * scales
                 top = product.astype(jnp.bfloat16)
-                high[at : at + ENC * LEN, :] = top
-                low[at : at + ENC * LEN, :] = (product - top.astype(jnp.float32)).astype(jnp.bfloat16)
+                high[at : at + size, :] = top
+                low[at : at + size, :] = (product - top.astype(jnp.float32)).astype(jnp.bfloat16)
 
     over_tokens = (((0,), (0,)), ((), ()))
-    block = 512
-    for d in range(0, D, block):
+    block = D // CHUNKS
+    sent = []
+    for i in range(CHUNKS):
+        d = i * block
         x = rows[:, d : d + block]
-        out[d : d + block, :] = lax.dot_general(
+        total[d : d + block, :] = lax.dot_general(
             x, high[...], over_tokens, preferred_element_type=jnp.float32
         ) + lax.dot_general(x, low[...], over_tokens, preferred_element_type=jnp.float32)
+        leave = pltpu.make_async_copy(total.at[pl.ds(d, block)], out.at[pl.ds(d, block)], leaving.at[i])
+        leave.start()
+        sent.append(leave)
+    for leave in sent:
+        leave.wait()
 
 
 def outer(place, messages, hs):
     return pl.pallas_call(
         outer_body,
-        out_shape=jax.ShapeDtypeStruct((D, 2 * COLS), jnp.float32),
-        in_specs=[SM] + [VM] * (2 * G),
-        out_specs=VM,
+        out_shape=pltpu.HBM((D, 2 * COLS), jnp.float32),
+        in_specs=[SM] + [HB] * G + [VM] * G,
+        out_specs=HB,
         scratch_shapes=[
             pltpu.VMEM((G * ENC * LEN, D), jnp.bfloat16),
+            pltpu.VMEM((G, MROWS - TOK, D), jnp.bfloat16),
             pltpu.VMEM((G * ENC * LEN, 2 * COLS), jnp.bfloat16),
             pltpu.VMEM((G * ENC * LEN, 2 * COLS), jnp.bfloat16),
+            pltpu.VMEM((D, 2 * COLS), jnp.float32),
+            pltpu.SemaphoreType.DMA((G, 2)),
+            pltpu.SemaphoreType.DMA((CHUNKS,)),
         ],
         compiler_params=params(),
-        name="outer",
-    )(place, *messages, *hs)
-
-
-def grad_body(weight, products, out):
-    out[...] = jnp.sum((weight[...].astype(jnp.float32) * products[...]).reshape(32, 64, 2 * COLS), axis=-1)
+        name="outer_product",
+    )(place, *map(in_hbm, messages), *hs)
+
+
+def grad_body(weight, products, out, held, arrivals):
+    block = D // CHUNKS
+    copies = []
+    for i in range(CHUNKS):
+        span = pl.ds(i * block, block)
+        copy = pltpu.make_async_copy(products.at[span], held.at[span], arrivals.at[i])
+        copy.start()
+        copies.append(copy)
+    for i in range(CHUNKS):
+        copies[i].wait()
+        at = slice(i * block, (i + 1) * block)
+        terms = weight[at, :].astype(jnp.float32) * held[at, :]
+        out[i * block // 64 : (i + 1) * block // 64, :] = jnp.sum(terms.reshape(block // 64, 64, 2 * COLS), axis=-1)
 
 
 def grad(weight, products):
     return pl.pallas_call(
         grad_body,
         out_shape=jax.ShapeDtypeStruct((32, 64), jnp.float32),
-        in_specs=[VM, VM],
+        in_specs=[VM, HB],
         out_specs=VM,
+        scratch_shapes=[pltpu.VMEM((D, 2 * COLS), jnp.float32), pltpu.SemaphoreType.DMA((CHUNKS,))],
         compiler_params=params(),
         name="gain_grad",
-    )(weight, products)
-
-
-def attend_body(place, weight, m0, m1, m2, m3, s0, s1, s2, s3, out):
+    )(weight, in_hbm(products))
+
+
+def attend_body(place, gain, weight, m0, m1, m2, m3, o0, o1, o2, o3, tokens, asked, arrivals):
+    copies = []
+    for r, message in enumerate((m0, m1, m2, m3)):
+        x = pltpu.make_async_copy(message.at[pl.ds(0, TOK)], tokens.at[r], arrivals.at[r, 0])
+        q = pltpu.make_async_copy(message.at[pl.ds(QROW, DEC)], asked.at[r], arrivals.at[r, 1])
+        x.start()
+        q.start()
+        copies.append((x, q))
     rows = GH * DEC
     row_head = lax.broadcasted_iota(jnp.int32, (rows, COLS), 0) // DEC
     col_head = lax.broadcasted_iota(jnp.int32, (rows, COLS), 1) // HEAD_DIM
     same = row_head == col_head
     spot = (lax.broadcasted_iota(jnp.int32, (1, TOK), 1) // LEN).astype(jnp.float32)
     upper = place[1] == 1
-    for r, (message, scaled) in enumerate(((m0, s0), (m1, s1), (m2, s2), (m3, s3))):
-        states = jnp.dot(scaled[...], weight[...], preferred_element_type=jnp.float32).astype(jnp.bfloat16)
+    for r, out in enumerate((o0, o1, o2, o3)):
+        for copy in copies[r]:
+            copy.wait()
+        values = tokens[r].astype(jnp.float32)
+        scaled = (values * inverse_rms(values) * gain[...]).astype(jnp.bfloat16)
+        states = jnp.dot(scaled, weight[...], preferred_element_type=jnp.float32).astype(jnp.bfloat16)
         query = jnp.where(
             upper,
-            message[:, COLS : 2 * COLS].astype(jnp.float32),
-            message[:, :COLS].astype(jnp.float32),
+            asked[r, :, COLS : 2 * COLS].astype(jnp.float32),
+            asked[r, :, :COLS].astype(jnp.float32),
         )
         spread = jnp.where(same, jnp.concatenate([query] * GH, axis=0), 0.0).astype(jnp.bfloat16)
         scores = lax.dot_general(
             spread, states[:, :COLS], (((1,), (1,)), ((), ())), preferred_element_type=jnp.float32
         ) * HEAD_DIM ** (-0.5)
-        count = message[:, 2 * COLS : 2 * COLS + TOK].astype(jnp.float32)[0:1, :]
+        count = asked[r, :, 2 * COLS : 2 * COLS + TOK].astype(jnp.float32)[0:1, :]
         scores = jnp.where(spot < count, scores, -jnp.inf)
         raised = jnp.exp(scores - jnp.max(scores, axis=-1, keepdims=True))
         weights = (raised / jnp.sum(raised, axis=-1, keepdims=True)).astype(jnp.bfloat16)
         mixed = jnp.dot(weights, states[:, COLS:], preferred_element_type=jnp.float32)
         mixed = jnp.where(same, mixed, 0.0).reshape(GH, DEC, COLS)
-        out[(2 * place[0] + place[1]) ^ r] = jnp.sum(mixed, axis=0).astype(jnp.bfloat16)
-
-
-def attend(place, weight, messages, scaled):
-    last = pl.BlockSpec((DEC, D), lambda i: (QROW // DEC, 0))
+        out[...] = jnp.sum(mixed, axis=0).astype(jnp.bfloat16)
+
+
+def attend(place, gain, weight, messages):
     return pl.pallas_call(
         attend_body,
-        out_shape=jax.ShapeDtypeStruct((G, DEC, COLS), jnp.bfloat16),
-        grid=(1,),
-        in_specs=[SM, pl.BlockSpec((D, 2 * COLS), lambda i: (0, 0))]
-        + [last] * G
-        + [pl.BlockSpec((TOK, D), lambda i: (0, 0))] * G,
-        out_specs=pl.BlockSpec((G, DEC, COLS), lambda i: (0, 0, 0)),
+        out_shape=tuple(jax.ShapeDtypeStruct((DEC, COLS), jnp.bfloat16) for _ in range(G)),
+        in_specs=[SM, VM, VM] + [HB] * G,
+        out_specs=(VM,) * G,
+        scratch_shapes=[
+            pltpu.VMEM((G, TOK, D), jnp.bfloat16),
+            pltpu.VMEM((G, DEC, D), jnp.bfloat16),
+            pltpu.SemaphoreType.DMA((G, 2)),
+        ],
         compiler_params=params(),
         name="attend",
-    )(place, weight, *messages, *scaled)
+    )(place, gain, weight, *map(in_hbm, messages))
+
+
+def assemble_body(member, p0, p1, p2, p3, out):
+    parts = (p0, p1, p2, p3)
+    for g in range(G):
+
+        @pl.when(member[0] == g)
+        def _():
+            for j in range(G):
+                out[:, j * COLS : (j + 1) * COLS] = parts[j ^ g][...]
+
+
+def assemble(member, parts):
+    return pl.pallas_call(
+        assemble_body,
+        out_shape=jax.ShapeDtypeStruct((DEC, HW), jnp.bfloat16),
+        in_specs=[SM] + [VM] * G,
+        out_specs=VM,
+        compiler_params=params(),
+        name="assemble",
+    )(member, *parts)
 
 
 def exchange(array, axes):
@@ -299,21 +370,17 @@
 
     outgoing = pack(helper_table.reshape(2, PMAX - KEEP), passages.reshape(PMAX, LEN, D))
     arrived = exchange(outgoing, FSDP)
-    s_0, s_1 = scale(near, gain), scale(m_c, gain)
+    mine = columns(member, projection)
+    mine, arrived = lax.optimization_barrier((mine, arrived))
+    by_y = exchange(mine, "y").reshape(512, 2 * COLS)
+
     tags = arrived[:, 0, D].astype(jnp.int32)
     h_own = unpack(tags, arrived).reshape(AID, D)
     h_z = swap(h_own, "zl")
     h_c = swap(h_own, "core")
     h_cz = swap(h_z, "core")
-
-    mine = columns(member, projection)
-    mine, s_0, s_1, _ = lax.optimization_barrier((mine, s_0, s_1, h_own))
-    by_y = exchange(mine, "y").reshape(512, 2 * COLS)
     weight = spread_to(by_y, "x").reshape(D, 2 * COLS)
-    s_2, s_3 = scale(m_z, gain), scale(m_cz, gain)
     products = outer(place, messages, (h_own, h_c, h_z, h_cz))
-    weight, s_2, s_3, products = lax.optimization_barrier((weight, s_2, s_3, products))
-    scaled = (s_0, s_1, s_2, s_3)
 
     row_terms = grad(weight, products)
     parts = exchange(row_terms.reshape(32, 1, 64), FSDP)
@@ -321,8 +388,11 @@
     gathered = exchange(jnp.broadcast_to(share[None], (16, 1, 64)), DP)
     gradient = jnp.sum(gathered, axis=0).reshape(64)
 
-    context = exchange(attend(place, weight, messages, scaled), GROUP)
-    context_out = jnp.transpose(context, (1, 0, 2)).reshape(1, 1, DEC, HW)
+    mixed = attend(place, gain, weight, messages)
+    from_core = swap(mixed[1], "core")
+    from_z = swap(mixed[2], "zl")
+    from_both = lax.ppermute(mixed[3], GROUP, [(i, i ^ 3) for i in range(G)])
+    context_out = assemble(member, (mixed[0], from_core, from_z, from_both)).reshape(1, 1, DEC, HW)
     return (context_out, gradient)
 
 

time: 158 us -> 147 us (0.930)
  blocking collectives: 17.7 us -> 0 us
  starting transfers between devices: 57.1 us -> 72.3 us
  local copies, waits for them, and re-layouts: 14.9 us -> 2.82 us
  waiting for transfers between devices: 33.2 us -> 41.4 us
  Pallas kernels: 30.4 us -> 26.7 us
    all_to_all x1 -> x0, blocking collectives: 17.7 us -> none  [exchange(): return lax.all_to_all(array, axes, 0, 0, tiled=True)]
    unnamed x44 -> x12, local copies, waits for them, and re-layouts: 12.1 us -> 0.7 us
    all_to_all x5, waiting for transfers between devices: 13.2 us -> 24.4 us  [exchange(): return lax.all_to_all(array, axes, 0, 0, tiled=True)]
    ppermute x6 -> x8, starting transfers between devices: 21.6 us -> 30.3 us  [swap(): return lax.ppermute(array, axis, [(0, 1), (1, 0)])]
    all_to_all x5, starting transfers between devices: 35.5 us -> 40 us  [exchange(): return lax.all_to_all(array, axes, 0, 0, tiled=True)]
    pallas_call x6 -> x3, Pallas kernels: 20.6 us -> 17 us  [the longest x1 8.42 us: attend(): pl.pallas_call(attend_body, out_shape=tuple((jax.ShapeDtypeStruct((DEC, C...]
    ppermute x6 -> x8, waiting for transfers between devices: 19.9 us -> 17 us  [swap(): return lax.ppermute(array, axis, [(0, 1), (1, 0)])]
    ppermute x0 -> x1, starting transfers between devices: none -> 2.09 us  [forward(): from_both = lax.ppermute(mixed[3], GROUP, [(i, i ^ 3) for i in range(G)])]
  transfers between devices with their start and end apart: 11 -> 14, of which waited for: 4 -> 5; matrix products, arithmetic and copies ran while one was open for 2% -> 2% of each run, Pallas kernels for 16% -> 15%
where the time goes in v3:
time: 147 us; the launch traced here: 146 us
  starting transfers between devices  72.3 us (49%)
  waiting for transfers between devices  41.4 us (28%)
  Pallas kernels  26.7 us (18%)
  local copies, waits for them, and re-layouts  2.82 us (2%)
  between operations  1.53 us (1%)
    all_to_all x5, starting transfers between devices, exchange(): return lax.all_to_all(array, axes, 0, 0, tiled=True)  40 us
    ppermute x8, starting transfers between devices, swap(): return lax.ppermute(array, axis, [(0, 1), (1, 0)])  30.3 us
    all_to_all x5, waiting for transfers between devices, exchange(): return lax.all_to_all(array, axes, 0, 0, tiled=True)  24.4 us
    ppermute x8, waiting for transfers between devices, swap(): return lax.ppermute(array, axis, [(0, 1), (1, 0)])  17 us
    pallas_call x1, Pallas kernels, attend(): pl.pallas_call(attend_body, out_shape=tuple((jax.ShapeDtypeStruct((DEC, C...  8.42 us
    pallas_call x1, Pallas kernels, outer(): pl.pallas_call(outer_body, out_shape=pltpu.HBM((D, 2 * COLS), jnp.float32...  7.97 us
    pallas_call x1, Pallas kernels, grad(): pl.pallas_call(grad_body, out_shape=jax.ShapeDtypeStruct((32, 64), jnp.fl...  3.01 us
  transfers between devices with their start and end apart: 14, of which 5 were waited for; matrix products, arithmetic and copies ran while one was open for 2% of the time, Pallas kernels for 15%

profile of v3, /device:TPU:1, one launch (start us, length us, event | category | flops | bytes accessed | tf_op | source)
XLA Modules:
  0.0 146.1 jit_solution(17622013183017787070)
XLA Ops:
  0.6 0.7 copy-done.5
  1.3 2.4 %pack.1 = bf16[32,8,2176]{2,1,0:T(8,128)(2,1)} custom-call(s32[2,32]{1,0:T(2,128)S(1)} %bitcast.29, bf16[40,8,2048]{2,1,0:T(8,128)(2,1)} %bitcast.21), custom_call_target="tpu_custom_call" | custom-call | tf_op jit(solution)/shard_map/pack/pallas_call | solution.py:77
  3.7 11.0 %all-to-all-start = ((bf16[32,8,2176]{2,1,0:T(8,128)(2,1)}), bf16[32,8,2176]{2,1,0:T(8,128)(2,1)S(1)}, u32[]{:S(2)}, u32[]{:S(2)}) async-start(bf16[32,8,2176]{2,1,0:T(8,128)(2,1)} %pack.1), calls=%async_computation | async-start | bytes 2228224 | tf_op jit(solution)/shard_map/all_to_all | solution.py:346
  15.5 2.6 %prep.1 = (bf16[432,2048]{1,0:T(8,128)(2,1)}, bf16[432,2048]{1,0:T(8,128)(2,1)}) custom-call(s32[2]{0:T(128)S(1)} %pad_add_fusion.place, s32[1]{0:T(128)} %bitcast.18.count, bf16[320,2048]{1,0:T(8,128)(2,1)S(1)} %bitcast.22, bf16[192,2048]{1,0:T(8,128)(2,1)S(1)} %bitcast.26, bf16[16,1024]{1,0:T(8,128)(2,1)S(1)} %bitcast.27), custom_call_target="tpu_custom_call" | custom-call | tf_op jit(solution)/shard_map/prep/pallas_call | solution.py:112
  18.1 4.2 %collective-permute-start.1 = (bf16[432,2048]{1,0:T(8,128)(2,1)}, bf16[432,2048]{1,0:T(8,128)(2,1)}, u32[]{:S(2)}, u32[]{:S(2)}) collective-permute-start(bf16[432,2048]{1,0:T(8,128)(2,1)} %get-tuple-element.12), channel_id=1, source_target_pairs={{0,64},{64,0},{1,65},{65,1},{2,66},{66,2},{3,67},{67,3},{4,68},{68... | collective-permute-start | bytes 5308424 | tf_op jit(solution)/shard_map/ppermute | solution.py:354
  22.4 0.9 columns.1
  23.2 18.0 %all-to-all-done.arrived = bf16[32,8,2176]{2,1,0:T(8,128)(2,1)S(1)} async-done(((bf16[32,8,2176]{2,1,0:T(8,128)(2,1)}), bf16[32,8,2176]{2,1,0:T(8,128)(2,1)S(1)}, u32[]{:S(2)}, u32[]{:S(2)}) %all-to-all-start) | async-done | bytes 1114144 | tf_op jit(solution)/shard_map/all_to_all | solution.py:346
  41.2 5.4 %all-to-all-start.1 = ((bf16[8,64,512]{2,1,0:T(8,128)(2,1)}), bf16[8,64,512]{2,1,0:T(8,128)(2,1)S(1)}, u32[]{:S(2)}, u32[]{:S(2)}) async-start(bf16[8,64,512]{2,1,0:T(8,128)(2,1)} %columns.1), calls=%async_computation.1 | async-start | bytes 1048576 | tf_op jit(solution)/shard_map/all_to_all | solution.py:346
  46.6 4.7 %collective-permute-start = (bf16[432,2048]{1,0:T(8,128)(2,1)}, bf16[432,2048]{1,0:T(8,128)(2,1)}, u32[]{:S(2)}, u32[]{:S(2)}) collective-permute-start(bf16[432,2048]{1,0:T(8,128)(2,1)} %get-tuple-element.11.m0), channel_id=1, source_target_pairs={{0,32},{32,0},{1,33},{33,1},{2,34},{34,2},{3,35},{35,3},{4,36},{36... | collective-permute-start | bytes 5308424 | tf_op jit(solution)/shard_map/ppermute | solution.py:354
  51.3 9.4 %collective-permute-done.1.m2 = bf16[432,2048]{1,0:T(8,128)(2,1)} collective-permute-done((bf16[432,2048]{1,0:T(8,128)(2,1)}, bf16[432,2048]{1,0:T(8,128)(2,1)}, u32[]{:S(2)}, u32[]{:S(2)}) %collective-permute-start.1) | collective-permute-done | bytes 1769504 | tf_op jit(solution)/shard_map/ppermute | solution.py:354
  60.7 3.4 %collective-permute-start.2 = (bf16[432,2048]{1,0:T(8,128)(2,1)}, bf16[432,2048]{1,0:T(8,128)(2,1)}, u32[]{:S(2)}, u32[]{:S(2)}) collective-permute-start(bf16[432,2048]{1,0:T(8,128)(2,1)} %collective-permute-done.1.m2), channel_id=1, source_target_pairs={{0,32},{32,0},{1,33},{33,1},{2,34},{34,2},{3,35},{35,3},{4,36},{36... | collective-permute-start | bytes 5308424 | tf_op jit(solution)/shard_map/ppermute | solution.py:354
  64.1 1.5 %broadcast_in_dim.14 = bf16[4,512,512]{2,1,0:T(8,128)(2,1)} broadcast(bf16[512,512]{1,0:T(8,128)(2,1)S(1)} %bitcast.30), dimensions={1,2} | broadcast | bytes 2621440 | tf_op jit(solution)/shard_map/broadcast_in_dim | solution.py:350
  65.7 4.0 %all-to-all-start.2 = ((bf16[4,512,512]{2,1,0:T(8,128)(2,1)}), bf16[4,512,512]{2,1,0:T(8,128)(2,1)S(1)}, u32[]{:S(2)}, u32[]{:S(2)}) async-start(bf16[4,512,512]{2,1,0:T(8,128)(2,1)} %broadcast_in_dim.14), calls=%async_computation.2 | async-start | bytes 4194304 | tf_op jit(solution)/shard_map/all_to_all | solution.py:346
  69.7 0.7 convert_reduce_fusion.tags
  70.3 0.8 unpack.1
  71.2 3.4 %collective-permute-start.7 = (bf16[128,2048]{1,0:T(8,128)(2,1)S(1)}, bf16[128,2048]{1,0:T(8,128)(2,1)S(1)}, u32[]{:S(2)}, u32[]{:S(2)}) collective-permute-start(bf16[128,2048]{1,0:T(8,128)(2,1)S(1)} %bitcast.23), channel_id=1, source_target_pairs={{0,64},{64,0},{1,65},{65,1},{2,66},{66,2},{3,67},{67,3},{4,68},{68... | collective-permute-start | bytes 1572872 | tf_op jit(solution)/shard_map/ppermute | solution.py:354
  74.5 4.2 %collective-permute-start.6 = (bf16[128,2048]{1,0:T(8,128)(2,1)S(1)}, bf16[128,2048]{1,0:T(8,128)(2,1)S(1)}, u32[]{:S(2)}, u32[]{:S(2)}) collective-permute-start(bf16[128,2048]{1,0:T(8,128)(2,1)S(1)} %bitcast.24), channel_id=1, source_target_pairs={{0,32},{32,0},{1,33},{33,1},{2,34},{34,2},{3,35},{35,3},{4,36},{36... | collective-permute-start | bytes 1572872 | tf_op jit(solution)/shard_map/ppermute | solution.py:354
  78.7 6.1 %collective-permute-done.7.h2 = bf16[128,2048]{1,0:T(8,128)(2,1)S(1)} collective-permute-done((bf16[128,2048]{1,0:T(8,128)(2,1)S(1)}, bf16[128,2048]{1,0:T(8,128)(2,1)S(1)}, u32[]{:S(2)}, u32[]{:S(2)}) %collective-permute-start.7) | collective-permute-done | bytes 524320 | tf_op jit(solution)/shard_map/ppermute | solution.py:354
  84.8 4.5 %collective-permute-start.8 = (bf16[128,2048]{1,0:T(8,128)(2,1)S(1)}, bf16[128,2048]{1,0:T(8,128)(2,1)S(1)}, u32[]{:S(2)}, u32[]{:S(2)}) collective-permute-start(bf16[128,2048]{1,0:T(8,128)(2,1)S(1)} %collective-permute-done.7.h2), channel_id=1, source_target_pairs={{0,32},{32,0},{1,33},{33,1},{2,34},{34,2},{3,35},{35,3},{4,36},{36... | collective-permute-start | bytes 1572872 | tf_op jit(solution)/shard_map/ppermute | solution.py:354
  89.3 1.5 %collective-permute-done.8.h3 = bf16[128,2048]{1,0:T(8,128)(2,1)S(1)} collective-permute-done((bf16[128,2048]{1,0:T(8,128)(2,1)S(1)}, bf16[128,2048]{1,0:T(8,128)(2,1)S(1)}, u32[]{:S(2)}, u32[]{:S(2)}) %collective-permute-start.8) | collective-permute-done | bytes 524320 | tf_op jit(solution)/shard_map/ppermute | solution.py:354
  90.8 8.0 %outer_product.1.products = f32[2048,512]{1,0:T(8,128)} custom-call(s32[2]{0:T(128)S(1)} %pad_add_fusion.place, bf16[432,2048]{1,0:T(8,128)(2,1)} %get-tuple-element.11.m0, bf16[432,2048]{1,0:T(8,128)(2,1)} %collective-permute-done.m1, bf16[432,2048]{1,0:T(8,128)(2,1)} %collective-permute-done.1.m2, bf16[432,2048]{1,0:T(8,128)(2,1)} %collective-permute-done.2.m3, ...), custom_call_target="tpu_custom_call" | custom-call | tf_op jit(solution)/shard_map/outer_product/pallas_call | solution.py:224
  98.8 3.0 %gain_grad.1 = f32[32,64]{1,0:T(8,128)} custom-call(bf16[2048,512]{1,0:T(8,128)(2,1)S(1)} %bitcast.19, f32[2048,512]{1,0:T(8,128)} %outer_product.1.products), custom_call_target="tpu_custom_call" | custom-call | tf_op jit(solution)/shard_map/gain_grad/pallas_call | solution.py:259
  101.8 9.6 %all-to-all-start.3 = ((f32[32,1,64]{2,1,0:T(1,128)}), f32[32,1,64]{2,1,0:T(1,128)S(1)}, u32[]{:S(2)}, u32[]{:S(2)}) async-start(f32[32,1,64]{2,1,0:T(1,128)} %bitcast.15), calls=%async_computation.3 | async-start | bytes 32768 | tf_op jit(solution)/shard_map/all_to_all | solution.py:346
  111.5 8.4 %attend.1 = (bf16[16,256]{1,0:T(8,128)(2,1)S(1)}, bf16[16,256]{1,0:T(8,128)(2,1)S(1)}, bf16[16,256]{1,0:T(8,128)(2,1)S(1)}, bf16[16,256]{1,0:T(8,128)(2,1)S(1)}) custom-call(s32[2]{0:T(128)S(1)} %pad_add_fusion.place, f32[1,2048]{1,0:T(1,128)S(1)} %bitcast.28, bf16[2048,512]{1,0:T(8,128)(2,1)S(1)} %bitcast.20, bf16[432,2048]{1,0:T(8,128)(2,1)} %get-tuple-element.11.m0, ...), custom_call_target="tpu_custom_call" | custom-call | tf_op jit(solution)/shard_map/attend/pallas_call | solution.py:309
  119.9 2.6 %collective-permute-start.3 = (bf16[16,256]{1,0:T(8,128)(2,1)S(1)}, bf16[16,256]{1,0:T(8,128)(2,1)S(1)}, u32[]{:S(2)}, u32[]{:S(2)}) collective-permute-start(bf16[16,256]{1,0:T(8,128)(2,1)S(1)} %get-tuple-element.14), channel_id=1, source_target_pairs={{0,32},{32,0},{1,33},{33,1},{2,34},{34,2},{3,35},{35,3},{4,36},{36... | collective-permute-start | bytes 24584 | tf_op jit(solution)/shard_map/ppermute | solution.py:354
  122.5 3.4 %collective-permute-start.4 = (bf16[16,256]{1,0:T(8,128)(2,1)S(1)}, bf16[16,256]{1,0:T(8,128)(2,1)S(1)}, u32[]{:S(2)}, u32[]{:S(2)}) collective-permute-start(bf16[16,256]{1,0:T(8,128)(2,1)S(1)} %get-tuple-element.15), channel_id=1, source_target_pairs={{0,64},{64,0},{1,65},{65,1},{2,66},{66,2},{3,67},{67,3},{4,68},{68... | collective-permute-start | bytes 24584 | tf_op jit(solution)/shard_map/ppermute | solution.py:354
  125.9 2.1 %collective-permute-start.5 = (bf16[16,256]{1,0:T(8,128)(2,1)S(1)}, bf16[16,256]{1,0:T(8,128)(2,1)S(1)}, u32[]{:S(2)}, u32[]{:S(2)}) collective-permute-start(bf16[16,256]{1,0:T(8,128)(2,1)S(1)} %get-tuple-element.16), channel_id=1, source_target_pairs={{0,96},{32,64},{64,32},{96,0},{1,97},{33,65},{65,33},{97,1},{2,98}... | collective-permute-start | bytes 24584 | tf_op jit(solution)/shard_map/ppermute | solution.py:394
  128.0 0.6 broadcast_in_dim.15
  128.6 9.9 %all-to-all-start.4 = ((f32[16,1,64]{2,1,0:T(1,128)}), f32[16,1,64]{2,1,0:T(1,128)S(1)}, u32[]{:S(2)}, u32[]{:S(2)}) async-start(f32[16,1,64]{2,1,0:T(1,128)} %broadcast_in_dim.15), calls=%async_computation.4 | async-start | bytes 16384 | tf_op jit(solution)/shard_map/all_to_all | solution.py:346
  138.5 0.7 assemble.1
  139.2 6.4 %all-to-all-done.4 = f32[16,1,64]{2,1,0:T(1,128)S(1)} async-done(((f32[16,1,64]{2,1,0:T(1,128)}), f32[16,1,64]{2,1,0:T(1,128)S(1)}, u32[]{:S(2)}, u32[]{:S(2)}) %all-to-all-start.4) | async-done | bytes 4128 | tf_op jit(solution)/shard_map/all_to_all | solution.py:346
  145.6 0.5 reduce_sum.19
  (22 shorter events, 0.2 us)
Async XLA Ops:
  0.6 0.7 copy-start.5
  1.3 14.2 %copy-start = (bf16[1,1,40,8,2048]{4,3,2,1,0:T(8,128)(2,1)S(1)}, bf16[1,1,40,8,2048]{4,3,2,1,0:T(8,128)(2,1)}, u32[]{:S(2)}) copy-start(bf16[1,1,40,8,2048]{4,3,2,1,0:T(8,128)(2,1)} %param.7) | copy-start | bytes 3932164
  1.3 14.2 %copy-start.1 = (bf16[1,1,24,8,2048]{4,3,2,1,0:T(8,128)(2,1)S(1)}, bf16[1,1,24,8,2048]{4,3,2,1,0:T(8,128)(2,1)}, u32[]{:S(2)}) copy-start(bf16[1,1,24,8,2048]{4,3,2,1,0:T(8,128)(2,1)} %param.13) | copy-start | bytes 2359300
  1.3 14.2 %copy-start.3 = (bf16[1,1,16,1024]{3,2,1,0:T(8,128)(2,1)S(1)}, bf16[1,1,16,1024]{3,2,1,0:T(8,128)(2,1)}, u32[]{:S(2)}) copy-start(bf16[1,1,16,1024]{3,2,1,0:T(8,128)(2,1)} %param.12) | copy-start | bytes 98308
  3.7 18.7 %copy-start.2 = (bf16[64,2048]{1,0:T(8,128)(2,1)S(1)}, bf16[64,2048]{1,0:T(8,128)(2,1)}, u32[]{:S(2)}) copy-start(bf16[64,2048]{1,0:T(8,128)(2,1)} %projection.1) | copy-start | bytes 786436
  3.7 37.5 %all-to-all-start = ((bf16[32,8,2176]{2,1,0:T(8,128)(2,1)}), bf16[32,8,2176]{2,1,0:T(8,128)(2,1)S(1)}, u32[]{:S(2)}, u32[]{:S(2)}) async-start(bf16[32,8,2176]{2,1,0:T(8,128)(2,1)} %pack.1), calls=%async_computation | async-start | bytes 2228224 | tf_op jit(solution)/shard_map/all_to_all | solution.py:346
  18.1 42.6 %collective-permute-start.1 = (bf16[432,2048]{1,0:T(8,128)(2,1)}, bf16[432,2048]{1,0:T(8,128)(2,1)}, u32[]{:S(2)}, u32[]{:S(2)}) collective-permute-start(bf16[432,2048]{1,0:T(8,128)(2,1)} %get-tuple-element.12), channel_id=1, source_target_pairs={{0,64},{64,0},{1,65},{65,1},{2,66},{66,2},{3,67},{67,3},{4,68},{68... | collective-permute-start | bytes 5308424 | tf_op jit(solution)/shard_map/ppermute | solution.py:354
  41.2 22.9 %all-to-all-start.1 = ((bf16[8,64,512]{2,1,0:T(8,128)(2,1)}), bf16[8,64,512]{2,1,0:T(8,128)(2,1)S(1)}, u32[]{:S(2)}, u32[]{:S(2)}) async-start(bf16[8,64,512]{2,1,0:T(8,128)(2,1)} %columns.1), calls=%async_computation.1 | async-start | bytes 1048576 | tf_op jit(solution)/shard_map/all_to_all | solution.py:346
  46.6 42.7 %collective-permute-start = (bf16[432,2048]{1,0:T(8,128)(2,1)}, bf16[432,2048]{1,0:T(8,128)(2,1)}, u32[]{:S(2)}, u32[]{:S(2)}) collective-permute-start(bf16[432,2048]{1,0:T(8,128)(2,1)} %get-tuple-element.11.m0), channel_id=1, source_target_pairs={{0,32},{32,0},{1,33},{33,1},{2,34},{34,2},{3,35},{35,3},{4,36},{36... | collective-permute-start | bytes 5308424 | tf_op jit(solution)/shard_map/ppermute | solution.py:354
  60.7 30.1 %collective-permute-start.2 = (bf16[432,2048]{1,0:T(8,128)(2,1)}, bf16[432,2048]{1,0:T(8,128)(2,1)}, u32[]{:S(2)}, u32[]{:S(2)}) collective-permute-start(bf16[432,2048]{1,0:T(8,128)(2,1)} %collective-permute-done.1.m2), channel_id=1, source_target_pairs={{0,32},{32,0},{1,33},{33,1},{2,34},{34,2},{3,35},{35,3},{4,36},{36... | collective-permute-start | bytes 5308424 | tf_op jit(solution)/shard_map/ppermute | solution.py:354
  65.7 33.2 %all-to-all-start.2 = ((bf16[4,512,512]{2,1,0:T(8,128)(2,1)}), bf16[4,512,512]{2,1,0:T(8,128)(2,1)S(1)}, u32[]{:S(2)}, u32[]{:S(2)}) async-start(bf16[4,512,512]{2,1,0:T(8,128)(2,1)} %broadcast_in_dim.14), calls=%async_computation.2 | async-start | bytes 4194304 | tf_op jit(solution)/shard_map/all_to_all | solution.py:346
  71.2 13.7 %collective-permute-start.7 = (bf16[128,2048]{1,0:T(8,128)(2,1)S(1)}, bf16[128,2048]{1,0:T(8,128)(2,1)S(1)}, u32[]{:S(2)}, u32[]{:S(2)}) collective-permute-start(bf16[128,2048]{1,0:T(8,128)(2,1)S(1)} %bitcast.23), channel_id=1, source_target_pairs={{0,64},{64,0},{1,65},{65,1},{2,66},{66,2},{3,67},{67,3},{4,68},{68... | collective-permute-start | bytes 1572872 | tf_op jit(solution)/shard_map/ppermute | solution.py:354
  74.5 14.8 %collective-permute-start.6 = (bf16[128,2048]{1,0:T(8,128)(2,1)S(1)}, bf16[128,2048]{1,0:T(8,128)(2,1)S(1)}, u32[]{:S(2)}, u32[]{:S(2)}) collective-permute-start(bf16[128,2048]{1,0:T(8,128)(2,1)S(1)} %bitcast.24), channel_id=1, source_target_pairs={{0,32},{32,0},{1,33},{33,1},{2,34},{34,2},{3,35},{35,3},{4,36},{36... | collective-permute-start | bytes 1572872 | tf_op jit(solution)/shard_map/ppermute | solution.py:354
  84.8 6.0 %collective-permute-start.8 = (bf16[128,2048]{1,0:T(8,128)(2,1)S(1)}, bf16[128,2048]{1,0:T(8,128)(2,1)S(1)}, u32[]{:S(2)}, u32[]{:S(2)}) collective-permute-start(bf16[128,2048]{1,0:T(8,128)(2,1)S(1)} %collective-permute-done.7.h2), channel_id=1, source_target_pairs={{0,32},{32,0},{1,33},{33,1},{2,34},{34,2},{3,35},{35,3},{4,36},{36... | collective-permute-start | bytes 1572872 | tf_op jit(solution)/shard_map/ppermute | solution.py:354
  98.8 12.7 %copy-start.4 = (f32[2048]{0:T(1024)S(1)}, f32[2048]{0:T(1024)}, u32[]{:S(2)}) copy-start(f32[2048]{0:T(1024)} %param.10) | copy-start | bytes 24580
  101.8 26.1 %all-to-all-start.3 = ((f32[32,1,64]{2,1,0:T(1,128)}), f32[32,1,64]{2,1,0:T(1,128)S(1)}, u32[]{:S(2)}, u32[]{:S(2)}) async-start(f32[32,1,64]{2,1,0:T(1,128)} %bitcast.15), calls=%async_computation.3 | async-start | bytes 32768 | tf_op jit(solution)/shard_map/all_to_all | solution.py:346
  119.9 18.6 %collective-permute-start.3 = (bf16[16,256]{1,0:T(8,128)(2,1)S(1)}, bf16[16,256]{1,0:T(8,128)(2,1)S(1)}, u32[]{:S(2)}, u32[]{:S(2)}) collective-permute-start(bf16[16,256]{1,0:T(8,128)(2,1)S(1)} %get-tuple-element.14), channel_id=1, source_target_pairs={{0,32},{32,0},{1,33},{33,1},{2,34},{34,2},{3,35},{35,3},{4,36},{36... | collective-permute-start | bytes 24584 | tf_op jit(solution)/shard_map/ppermute | solution.py:354
  122.5 16.0 %collective-permute-start.4 = (bf16[16,256]{1,0:T(8,128)(2,1)S(1)}, bf16[16,256]{1,0:T(8,128)(2,1)S(1)}, u32[]{:S(2)}, u32[]{:S(2)}) collective-permute-start(bf16[16,256]{1,0:T(8,128)(2,1)S(1)} %get-tuple-element.15), channel_id=1, source_target_pairs={{0,64},{64,0},{1,65},{65,1},{2,66},{66,2},{3,67},{67,3},{4,68},{68... | collective-permute-start | bytes 24584 | tf_op jit(solution)/shard_map/ppermute | solution.py:354
  125.9 12.6 %collective-permute-start.5 = (bf16[16,256]{1,0:T(8,128)(2,1)S(1)}, bf16[16,256]{1,0:T(8,128)(2,1)S(1)}, u32[]{:S(2)}, u32[]{:S(2)}) collective-permute-start(bf16[16,256]{1,0:T(8,128)(2,1)S(1)} %get-tuple-element.16), channel_id=1, source_target_pairs={{0,96},{32,64},{64,32},{96,0},{1,97},{33,65},{65,33},{97,1},{2,98}... | collective-permute-start | bytes 24584 | tf_op jit(solution)/shard_map/ppermute | solution.py:394
  128.6 16.9 %all-to-all-start.4 = ((f32[16,1,64]{2,1,0:T(1,128)}), f32[16,1,64]{2,1,0:T(1,128)S(1)}, u32[]{:S(2)}, u32[]{:S(2)}) async-start(f32[16,1,64]{2,1,0:T(1,128)} %broadcast_in_dim.15), calls=%async_computation.4 | async-start | bytes 16384 | tf_op jit(solution)/shard_map/all_to_all | solution.py:346

commit v4 on v3

--- a/solution.py
+++ b/solution.py
@@ -27,7 +27,7 @@
 MROWS = QROW + DEC
 WIDE = D + 128
 EPSILON = 1e-06
-CHUNKS = 4
+BLOCK = 512
 GROUP = ("zl", "core")
 DP = ("zh", "zl", "core")
 FSDP = ("x", "y")
@@ -166,105 +166,90 @@
     return lax.rsqrt(jnp.mean(values * values, axis=-1, keepdims=True) + EPSILON)
 
 
-def outer_body(place, m0, m1, m2, m3, h0, h1, h2, h3, out, rows, tails, high, low, total, arrivals, leaving):
-    messages = (m0, m1, m2, m3)
+def block_rows(ring, step):
+    return pl.ds(pl.multiple_of(((ring[0] + step) % 4) * BLOCK, BLOCK), BLOCK)
+
+
+def weight_body(ring, own, left, right, top, bottom, out):
+    half = BLOCK // 2
+    out[block_rows(ring, 0), :] = own[...]
+    out[block_rows(ring, 3), :] = left[...]
+    out[block_rows(ring, 1), :] = right[...]
+    far = pl.multiple_of(((ring[0] + 2) % 4) * BLOCK, BLOCK)
+    out[pl.ds(far, half), :] = top[...]
+    out[pl.ds(pl.multiple_of(far + half, half), half), :] = bottom[...]
+
+
+def join_weight(ring, pieces):
+    return pl.pallas_call(
+        weight_body,
+        out_shape=jax.ShapeDtypeStruct((D, 2 * COLS), jnp.bfloat16),
+        in_specs=[SM] + [VM] * 5,
+        out_specs=VM,
+        compiler_params=params(),
+        name="join_weight",
+    )(ring, *pieces)
+
+
+def grad_body(place, weight, m0, m1, h0, h1, *refs):
+    *base, out, normal, tails, cots, own, row, arrivals = refs
     size = ENC * LEN
     copies = []
-    for r, message in enumerate(messages):
-        own = pltpu.make_async_copy(message.at[pl.ds(0, OWN)], rows.at[pl.ds(r * size, OWN)], arrivals.at[r, 0])
+    for r, message in enumerate((m0, m1)):
+        head = pltpu.make_async_copy(message.at[pl.ds(0, OWN)], own.at[r], arrivals.at[r, 0])
         tail = pltpu.make_async_copy(message.at[pl.ds(TOK, MROWS - TOK)], tails.at[r], arrivals.at[r, 1])
-        own.start()
+        head.start()
         tail.start()
-        copies.append((own, tail))
+        copies.append((head, tail))
     spot = (lax.broadcasted_iota(jnp.int32, (OWN, 1), 0) // LEN).astype(jnp.float32)
-    for r, aid in enumerate((h0, h1, h2, h3)):
+    for r, aid in enumerate((h0, h1)):
         at = r * size
-        helped = aid[...]
-        rows[at + OWN : at + size, :] = helped
-        helped_scale = inverse_rms(helped.astype(jnp.float32))
+        helped = aid[...].astype(jnp.float32)
+        normal[at + OWN : at + size, :] = helped * inverse_rms(helped)
         for copy in copies[r]:
             copy.wait()
         count = tails[r, QROW - TOK :, 2 * COLS : 2 * COLS + 128].astype(jnp.float32)[0:1, 0:1]
-        own_scale = jnp.where(spot < count, inverse_rms(rows[at : at + OWN, :].astype(jnp.float32)), 0.0)
-        scales = jnp.concatenate([own_scale, helped_scale], axis=0)
+        values = own[r].astype(jnp.float32)
+        normal[at : at + OWN, :] = values * jnp.where(spot < count, inverse_rms(values), 0.0)
         for c in range(2):
 
             @pl.when(place[1] == c)
             def _():
                 left = 4 * c * COLS
-                cot = jnp.concatenate(
-                    [
-                        tails[r, : CROW - TOK, left : left + 2 * COLS],
-                        tails[r, : CROW - TOK, left + 2 * COLS : left + 4 * COLS],
-                    ],
-                    axis=0,
-                )
-                product = cot.astype(jnp.float32) * scales
-                top = product.astype(jnp.bfloat16)
-                high[at : at + size, :] = top
-                low[at : at + size, :] = (product - top.astype(jnp.float32)).astype(jnp.bfloat16)
-
-    over_tokens = (((0,), (0,)), ((), ()))
-    block = D // CHUNKS
-    sent = []
-    for i in range(CHUNKS):
-        d = i * block
-        x = rows[:, d : d + block]
-        total[d : d + block, :] = lax.dot_general(
-            x, high[...], over_tokens, preferred_element_type=jnp.float32
-        ) + lax.dot_general(x, low[...], over_tokens, preferred_element_type=jnp.float32)
-        leave = pltpu.make_async_copy(total.at[pl.ds(d, block)], out.at[pl.ds(d, block)], leaving.at[i])
-        leave.start()
-        sent.append(leave)
-    for leave in sent:
-        leave.wait()
-
-
-def outer(place, messages, hs):
-    return pl.pallas_call(
-        outer_body,
-        out_shape=pltpu.HBM((D, 2 * COLS), jnp.float32),
-        in_specs=[SM] + [HB] * G + [VM] * G,
-        out_specs=HB,
-        scratch_shapes=[
-            pltpu.VMEM((G * ENC * LEN, D), jnp.bfloat16),
-            pltpu.VMEM((G, MROWS - TOK, D), jnp.bfloat16),
-            pltpu.VMEM((G * ENC * LEN, 2 * COLS), jnp.bfloat16),
-            pltpu.VMEM((G * ENC * LEN, 2 * COLS), jnp.bfloat16),
-            pltpu.VMEM((D, 2 * COLS), jnp.float32),
-            pltpu.SemaphoreType.DMA((G, 2)),
-            pltpu.SemaphoreType.DMA((CHUNKS,)),
-        ],
-        compiler_params=params(),
-        name="outer_product",
-    )(place, *map(in_hbm, messages), *hs)
-
-
-def grad_body(weight, products, out, held, arrivals):
-    block = D // CHUNKS
-    copies = []
-    for i in range(CHUNKS):
-        span = pl.ds(i * block, block)
-        copy = pltpu.make_async_copy(products.at[span], held.at[span], arrivals.at[i])
-        copy.start()
-        copies.append(copy)
-    for i in range(CHUNKS):
-        copies[i].wait()
-        at = slice(i * block, (i + 1) * block)
-        terms = weight[at, :].astype(jnp.float32) * held[at, :]
-        out[i * block // 64 : (i + 1) * block // 64, :] = jnp.sum(terms.reshape(block // 64, 64, 2 * COLS), axis=-1)
-
-
-def grad(weight, products):
+                half = size // 2
+                cots[at : at + half, :] = tails[r, :half, left : left + 2 * COLS]
+                cots[at + half : at + size, :] = tails[r, :half, left + 2 * COLS : left + 4 * COLS]
+
+    for d in range(0, D, BLOCK):
+        back = lax.dot_general(
+            cots[...], weight[d : d + BLOCK, :], (((1,), (1,)), ((), ())), preferred_element_type=jnp.float32
+        )
+        row[:, d : d + BLOCK] = jnp.sum(normal[:, d : d + BLOCK] * back, axis=0, keepdims=True)
+    for f in range(32):
+        terms = row[:, f * 64 : (f + 1) * 64]
+        if base:
+            terms = terms + base[0][f : f + 1, :]
+        out[f : f + 1, :] = terms
+
+
+def grad(place, weight, messages, hs, base=None):
+    extra = () if base is None else (base,)
     return pl.pallas_call(
         grad_body,
         out_shape=jax.ShapeDtypeStruct((32, 64), jnp.float32),
-        in_specs=[VM, HB],
-        out_specs=VM,
-        scratch_shapes=[pltpu.VMEM((D, 2 * COLS), jnp.float32), pltpu.SemaphoreType.DMA((CHUNKS,))],
+        in_specs=[SM, VM] + [HB] * 2 + [VM] * (2 + len(extra)),
+        out_specs=VM,
+        scratch_shapes=[
+            pltpu.VMEM((2 * ENC * LEN, D), jnp.float32),
+            pltpu.VMEM((2, MROWS - TOK, D), jnp.bfloat16),
+            pltpu.VMEM((2 * ENC * LEN, 2 * COLS), jnp.bfloat16),
+            pltpu.VMEM((2, OWN, D), jnp.bfloat16),
+            pltpu.VMEM((1, D), jnp.float32),
+            pltpu.SemaphoreType.DMA((2, 2)),
+        ],
         compiler_params=params(),
         name="gain_grad",
-    )(weight, in_hbm(products))
+    )(place, weight, *map(in_hbm, messages), *hs, *extra)
 
 
 def attend_body(place, gain, weight, m0, m1, m2, m3, o0, o1, o2, o3, tokens, asked, arrivals):
@@ -346,12 +331,12 @@
     return lax.all_to_all(array, axes, 0, 0, tiled=True)
 
 
-def spread_to(array, axis):
-    return exchange(jnp.broadcast_to(array[None], (lax.axis_size(axis), *array.shape)), axis)
-
-
 def swap(array, axis):
     return lax.ppermute(array, axis, [(0, 1), (1, 0)])
+
+
+def turn(array, step):
+    return lax.ppermute(array, "x", [(i, (i + step) % 4) for i in range(4)])
 
 
 def forward(passages, counts, helper_table, norm_gain, projection, queries, cotangent):
@@ -360,8 +345,17 @@
     member = (zl * 2 + core).reshape(1)
     gain = norm_gain.reshape(1, D)
 
+    ring = lax.axis_index("x").astype(jnp.int32).reshape(1)
+
+    mine = columns(member, projection)
+    by_y = exchange(mine, "y").reshape(BLOCK, 2 * COLS)
+
     near, far = prep(
-        place, counts.reshape(1), passages.reshape(TOK, D), cotangent.reshape(ENC * LEN, D), queries.reshape(DEC, HW)
+        place,
+        counts.reshape(1),
+        passages.reshape(TOK, D),
+        cotangent.reshape(ENC * LEN, D),
+        queries.reshape(DEC, HW),
     )
     m_z = swap(far, "zl")
     m_c = swap(near, "core")
@@ -370,29 +364,31 @@
 
     outgoing = pack(helper_table.reshape(2, PMAX - KEEP), passages.reshape(PMAX, LEN, D))
     arrived = exchange(outgoing, FSDP)
-    mine = columns(member, projection)
-    mine, arrived = lax.optimization_barrier((mine, arrived))
-    by_y = exchange(mine, "y").reshape(512, 2 * COLS)
+
+    left = turn(by_y, 1)
+    right = turn(by_y, 3)
+    top = turn(left[: BLOCK // 2], 1)
+    bottom = turn(right[BLOCK // 2 :], 3)
+    weight = join_weight(ring, (by_y, left, right, top, bottom))
 
     tags = arrived[:, 0, D].astype(jnp.int32)
     h_own = unpack(tags, arrived).reshape(AID, D)
     h_z = swap(h_own, "zl")
     h_c = swap(h_own, "core")
     h_cz = swap(h_z, "core")
-    weight = spread_to(by_y, "x").reshape(D, 2 * COLS)
-    products = outer(place, messages, (h_own, h_c, h_z, h_cz))
-
-    row_terms = grad(weight, products)
-    parts = exchange(row_terms.reshape(32, 1, 64), FSDP)
-    share = jnp.sum(parts, axis=0)
-    gathered = exchange(jnp.broadcast_to(share[None], (16, 1, 64)), DP)
-    gradient = jnp.sum(gathered, axis=0).reshape(64)
 
     mixed = attend(place, gain, weight, messages)
     from_core = swap(mixed[1], "core")
     from_z = swap(mixed[2], "zl")
     from_both = lax.ppermute(mixed[3], GROUP, [(i, i ^ 3) for i in range(G)])
     context_out = assemble(member, (mixed[0], from_core, from_z, from_both)).reshape(1, 1, DEC, HW)
+
+    row_terms = grad(place, weight, (near, m_c), (h_own, h_c))
+    row_terms = grad(place, weight, (m_z, m_cz), (h_z, h_cz), row_terms)
+    parts = exchange(row_terms.reshape(32, 1, 64), FSDP)
+    share = jnp.sum(parts, axis=0)
+    gathered = exchange(jnp.broadcast_to(share[None], (16, 1, 64)), DP)
+    gradient = jnp.sum(gathered, axis=0).reshape(64)
     return (context_out, gradient)
 
 

time: 147 us -> 156 us (1.061)
  starting transfers between devices: 72.3 us -> 76.3 us
  local copies, waits for them, and re-layouts: 2.82 us -> 6.49 us
  waiting for transfers between devices: 41.4 us -> 43.2 us
    all_to_all x5 -> x4, waiting for transfers between devices: 24.4 us -> 10.4 us  [exchange(): return lax.all_to_all(array, axes, 0, 0, tiled=True)]
    ppermute x0 -> x4, starting transfers between devices: none -> 11.7 us  [turn(): return lax.ppermute(array, 'x', [(i, (i + step) % 4) for i in range(4)])]
    ppermute x0 -> x4, waiting for transfers between devices: none -> 10.8 us  [turn(): return lax.ppermute(array, 'x', [(i, (i + step) % 4) for i in range(4)])]
    pallas_call x1, Pallas kernels: 7.97 us -> 1.18 us  [join_weight(): pl.pallas_call(weight_body, out_shape=jax.ShapeDtypeStruct((D, 2 * COLS),...]
    pallas_call x1 -> x2, Pallas kernels: 3.01 us -> 8.81 us  [grad(): pl.pallas_call(grad_body, out_shape=jax.ShapeDtypeStruct((32, 64), jnp.fl...]
    ppermute x8, waiting for transfers between devices: 17 us -> 22 us  [swap(): return lax.ppermute(array, axis, [(0, 1), (1, 0)])]
    all_to_all x5 -> x4, starting transfers between devices: 40 us -> 35.3 us  [exchange(): return lax.all_to_all(array, axes, 0, 0, tiled=True)]
    unnamed x12 -> x20, local copies, waits for them, and re-layouts: 0.7 us -> 4.89 us
  transfers between devices with their start and end apart: 14 -> 17, of which waited for: 5 -> 6; matrix products, arithmetic and copies ran while one was open for 2% -> 2% of each run, Pallas kernels for 15% -> 13%
where the time goes in v4:
time: 156 us; the launch traced here: 155 us
  starting transfers between devices  76.3 us (49%)
  waiting for transfers between devices  43.2 us (28%)
  Pallas kernels  25.6 us (16%)
  local copies, waits for them, and re-layouts  6.49 us (4%)
  between operations  1.6 us (1%)
    all_to_all x4, starting transfers between devices, exchange(): return lax.all_to_all(array, axes, 0, 0, tiled=True)  35.3 us
    ppermute x8, starting transfers between devices, swap(): return lax.ppermute(array, axis, [(0, 1), (1, 0)])  27.2 us
    ppermute x8, waiting for transfers between devices, swap(): return lax.ppermute(array, axis, [(0, 1), (1, 0)])  22 us
    ppermute x4, starting transfers between devices, turn(): return lax.ppermute(array, 'x', [(i, (i + step) % 4) for i in range(4)])  11.7 us
    ppermute x4, waiting for transfers between devices, turn(): return lax.ppermute(array, 'x', [(i, (i + step) % 4) for i in range(4)])  10.8 us
    all_to_all x4, waiting for transfers between devices, exchange(): return lax.all_to_all(array, axes, 0, 0, tiled=True)  10.4 us
    pallas_call x2, Pallas kernels, grad(): pl.pallas_call(grad_body, out_shape=jax.ShapeDtypeStruct((32, 64), jnp.fl...  8.81 us
    pallas_call x1, Pallas kernels, attend(): pl.pallas_call(attend_body, out_shape=tuple((jax.ShapeDtypeStruct((DEC, C...  8.27 us
  transfers between devices with their start and end apart: 17, of which 6 were waited for; matrix products, arithmetic and copies ran while one was open for 2% of the time, Pallas kernels for 13%

profile of v4, /device:TPU:1, one launch (start us, length us, event | category | flops | bytes accessed | tf_op | source)
XLA Modules:
  0.0 154.5 jit_solution(8950647401390315929)
XLA Ops:
  0.7 1.0 copy-done.6
  2.6 7.8 %all-to-all-start = ((bf16[8,64,512]{2,1,0:T(8,128)(2,1)}), bf16[8,64,512]{2,1,0:T(8,128)(2,1)S(1)}, u32[]{:S(2)}, u32[]{:S(2)}) async-start(bf16[8,64,512]{2,1,0:T(8,128)(2,1)} %columns.1), calls=%async_computation | async-start | bytes 1048576 | tf_op jit(solution)/shard_map/all_to_all | solution.py:331
  11.1 1.1 copy-done.3
  12.2 2.6 %prep.1 = (bf16[432,2048]{1,0:T(8,128)(2,1)}, bf16[432,2048]{1,0:T(8,128)(2,1)}) custom-call(s32[2]{0:T(128)S(1)} %pad_add_fusion.place, s32[1]{0:T(128)} %bitcast.18.count, bf16[320,2048]{1,0:T(8,128)(2,1)S(1)} %bitcast.20, bf16[192,2048]{1,0:T(8,128)(2,1)S(1)} %bitcast.27, bf16[16,1024]{1,0:T(8,128)(2,1)S(1)} %bitcast.28), custom_call_target="tpu_custom_call" | custom-call | tf_op jit(solution)/shard_map/prep/pallas_call | solution.py:112
  14.8 4.0 %collective-permute-start.5 = (bf16[432,2048]{1,0:T(8,128)(2,1)}, bf16[432,2048]{1,0:T(8,128)(2,1)}, u32[]{:S(2)}, u32[]{:S(2)}) collective-permute-start(bf16[432,2048]{1,0:T(8,128)(2,1)} %get-tuple-element.9), channel_id=1, source_target_pairs={{0,64},{64,0},{1,65},{65,1},{2,66},{66,2},{3,67},{67,3},{4,68},{68... | collective-permute-start | bytes 5308424 | tf_op jit(solution)/shard_map/ppermute | solution.py:335
  18.8 2.4 %pack.1 = bf16[32,8,2176]{2,1,0:T(8,128)(2,1)} custom-call(s32[2,32]{1,0:T(2,128)S(1)} %bitcast.30, bf16[40,8,2048]{2,1,0:T(8,128)(2,1)} %bitcast.19), custom_call_target="tpu_custom_call" | custom-call | tf_op jit(solution)/shard_map/pack/pallas_call | solution.py:77
  21.2 4.1 %all-to-all-done = bf16[8,64,512]{2,1,0:T(8,128)(2,1)S(1)} async-done(((bf16[8,64,512]{2,1,0:T(8,128)(2,1)}), bf16[8,64,512]{2,1,0:T(8,128)(2,1)S(1)}, u32[]{:S(2)}, u32[]{:S(2)}) %all-to-all-start) | async-done | bytes 524320 | tf_op jit(solution)/shard_map/all_to_all | solution.py:331
  25.3 7.4 %all-to-all-start.1 = ((bf16[32,8,2176]{2,1,0:T(8,128)(2,1)}), bf16[32,8,2176]{2,1,0:T(8,128)(2,1)S(1)}, u32[]{:S(2)}, u32[]{:S(2)}) async-start(bf16[32,8,2176]{2,1,0:T(8,128)(2,1)} %pack.1), calls=%async_computation.1 | async-start | bytes 2228224 | tf_op jit(solution)/shard_map/all_to_all | solution.py:331
  32.7 2.7 %collective-permute-start.4 = (bf16[432,2048]{1,0:T(8,128)(2,1)}, bf16[432,2048]{1,0:T(8,128)(2,1)}, u32[]{:S(2)}, u32[]{:S(2)}) collective-permute-start(bf16[432,2048]{1,0:T(8,128)(2,1)} %get-tuple-element.8.m0), channel_id=1, source_target_pairs={{0,32},{32,0},{1,33},{33,1},{2,34},{34,2},{3,35},{35,3},{4,36},{36... | collective-permute-start | bytes 5308424 | tf_op jit(solution)/shard_map/ppermute | solution.py:335
  35.4 20.7 %collective-permute-done.5.m2.m0 = bf16[432,2048]{1,0:T(8,128)(2,1)} collective-permute-done((bf16[432,2048]{1,0:T(8,128)(2,1)}, bf16[432,2048]{1,0:T(8,128)(2,1)}, u32[]{:S(2)}, u32[]{:S(2)}) %collective-permute-start.5) | collective-permute-done | bytes 1769504 | tf_op jit(solution)/shard_map/ppermute | solution.py:335
  56.1 4.5 %collective-permute-start.6 = (bf16[432,2048]{1,0:T(8,128)(2,1)}, bf16[432,2048]{1,0:T(8,128)(2,1)}, u32[]{:S(2)}, u32[]{:S(2)}) collective-permute-start(bf16[432,2048]{1,0:T(8,128)(2,1)} %collective-permute-done.5.m2.m0), channel_id=1, source_target_pairs={{0,32},{32,0},{1,33},{33,1},{2,34},{34,2},{3,35},{35,3},{4,36},{36... | collective-permute-start | bytes 5308424 | tf_op jit(solution)/shard_map/ppermute | solution.py:335
  60.5 3.1 %collective-permute-start = (bf16[512,512]{1,0:T(8,128)(2,1)S(1)}, bf16[512,512]{1,0:T(8,128)(2,1)S(1)}, u32[]{:S(2)}, u32[]{:S(2)}) collective-permute-start(bf16[512,512]{1,0:T(8,128)(2,1)S(1)} %bitcast.21), channel_id=1, source_target_pairs={{0,8},{8,16},{16,24},{24,0},{1,9},{9,17},{17,25},{25,1},{2,10},{10... | collective-permute-start | bytes 1572872 | tf_op jit(solution)/shard_map/ppermute | solution.py:339
  63.7 3.4 %collective-permute-start.1 = (bf16[512,512]{1,0:T(8,128)(2,1)S(1)}, bf16[512,512]{1,0:T(8,128)(2,1)}, u32[]{:S(2)}, u32[]{:S(2)}) collective-permute-start(bf16[512,512]{1,0:T(8,128)(2,1)S(1)} %bitcast.22), channel_id=1, source_target_pairs={{0,24},{8,0},{16,8},{24,16},{1,25},{9,1},{17,9},{25,17},{2,26},{10... | collective-permute-start | bytes 1572872 | tf_op jit(solution)/shard_map/ppermute | solution.py:339
  68.6 3.4 %collective-permute-start.10 = (bf16[128,2048]{1,0:T(8,128)(2,1)S(1)}, bf16[128,2048]{1,0:T(8,128)(2,1)}, u32[]{:S(2)}, u32[]{:S(2)}) collective-permute-start(bf16[128,2048]{1,0:T(8,128)(2,1)S(1)} %bitcast.24), channel_id=1, source_target_pairs={{0,64},{64,0},{1,65},{65,1},{2,66},{66,2},{3,67},{67,3},{4,68},{68... | collective-permute-start | bytes 1572872 | tf_op jit(solution)/shard_map/ppermute | solution.py:335
  71.9 5.2 %collective-permute-done.left = bf16[512,512]{1,0:T(8,128)(2,1)S(1)} collective-permute-done((bf16[512,512]{1,0:T(8,128)(2,1)S(1)}, bf16[512,512]{1,0:T(8,128)(2,1)S(1)}, u32[]{:S(2)}, u32[]{:S(2)}) %collective-permute-start) | collective-permute-done | bytes 524320 | tf_op jit(solution)/shard_map/ppermute | solution.py:339
  77.1 2.0 %collective-permute-start.2 = (bf16[256,512]{1,0:T(8,128)(2,1)S(1)}, bf16[256,512]{1,0:T(8,128)(2,1)S(1)}, u32[]{:S(2)}, u32[]{:S(2)}) collective-permute-start(bf16[256,512]{1,0:T(8,128)(2,1)S(1)} %slice.12), channel_id=1, source_target_pairs={{0,8},{8,16},{16,24},{24,0},{1,9},{9,17},{17,25},{25,1},{2,10},{10... | collective-permute-start | bytes 786440 | tf_op jit(solution)/shard_map/ppermute | solution.py:339
  79.2 3.0 %collective-permute-start.12 = (bf16[128,2048]{1,0:T(8,128)(2,1)S(1)}, bf16[128,2048]{1,0:T(8,128)(2,1)}, u32[]{:S(2)}, u32[]{:S(2)}) collective-permute-start(bf16[128,2048]{1,0:T(8,128)(2,1)S(1)} %bitcast.25), channel_id=1, source_target_pairs={{0,32},{32,0},{1,33},{33,1},{2,34},{34,2},{3,35},{35,3},{4,36},{36... | collective-permute-start | bytes 1572872 | tf_op jit(solution)/shard_map/ppermute | solution.py:335
  82.1 1.3 collective-permute-done.10.h0
  83.5 3.3 %collective-permute-start.11 = (bf16[128,2048]{1,0:T(8,128)(2,1)}, bf16[128,2048]{1,0:T(8,128)(2,1)}, u32[]{:S(2)}, u32[]{:S(2)}) collective-permute-start(bf16[128,2048]{1,0:T(8,128)(2,1)} %collective-permute-done.10.h0), channel_id=1, source_target_pairs={{0,32},{32,0},{1,33},{33,1},{2,34},{34,2},{3,35},{35,3},{4,36},{36... | collective-permute-start | bytes 1572872 | tf_op jit(solution)/shard_map/ppermute | solution.py:335
  87.8 3.2 %collective-permute-start.3 = (bf16[256,512]{1,0:T(8,128)(2,1)S(1)}, bf16[256,512]{1,0:T(8,128)(2,1)S(1)}, u32[]{:S(2)}, u32[]{:S(2)}) collective-permute-start(bf16[256,512]{1,0:T(8,128)(2,1)S(1)} %slice.13), channel_id=1, source_target_pairs={{0,24},{8,0},{16,8},{24,16},{1,25},{9,1},{17,9},{25,17},{2,26},{10... | collective-permute-start | bytes 786440 | tf_op jit(solution)/shard_map/ppermute | solution.py:339
  91.0 5.6 %collective-permute-done.3.bottom = bf16[256,512]{1,0:T(8,128)(2,1)S(1)} collective-permute-done((bf16[256,512]{1,0:T(8,128)(2,1)S(1)}, bf16[256,512]{1,0:T(8,128)(2,1)S(1)}, u32[]{:S(2)}, u32[]{:S(2)}) %collective-permute-start.3) | collective-permute-done | bytes 262176 | tf_op jit(solution)/shard_map/ppermute | solution.py:339
  97.3 1.0 copy-done.2
  99.3 1.2 join_weight.1.weight
  100.5 4.1 %gain_grad.2.refs_0_ = f32[32,64]{1,0:T(8,128)S(1)} custom-call(s32[2]{0:T(128)S(1)} %pad_add_fusion.place, bf16[2048,512]{1,0:T(8,128)(2,1)S(1)} %join_weight.1.weight, bf16[432,2048]{1,0:T(8,128)(2,1)} %get-tuple-element.8.m0, bf16[432,2048]{1,0:T(8,128)(2,1)} %collective-permute-done.4.m1, bf16[128,2048]{1,0:T(8,128)(2,1)S(1)} %bitcast.26, ...), custom_call_target="tpu_custom_call" | custom-call | tf_op jit(solution)/shard_map/gain_grad/pallas_call | solution.py:237
  104.6 4.7 %gain_grad.3 = f32[32,64]{1,0:T(8,128)} custom-call(s32[2]{0:T(128)S(1)} %pad_add_fusion.place, bf16[2048,512]{1,0:T(8,128)(2,1)S(1)} %join_weight.1.weight, bf16[432,2048]{1,0:T(8,128)(2,1)} %collective-permute-done.5.m2.m0, bf16[432,2048]{1,0:T(8,128)(2,1)} %collective-permute-done.6.m3.m1, bf16[128,2048]{1,0:T(8,128)(2,1)} %collective-permute-done.10.h0, ...), custom_call_target="tpu_custom_call" | custom-call | tf_op jit(solution)/shard_map/gain_grad/pallas_call | solution.py:237
  109.3 10.2 %all-to-all-start.2 = ((f32[32,1,64]{2,1,0:T(1,128)}), f32[32,1,64]{2,1,0:T(1,128)S(1)}, u32[]{:S(2)}, u32[]{:S(2)}) async-start(f32[32,1,64]{2,1,0:T(1,128)} %bitcast.15), calls=%async_computation.2 | async-start | bytes 32768 | tf_op jit(solution)/shard_map/all_to_all | solution.py:331
  119.5 8.3 %attend.1 = (bf16[16,256]{1,0:T(8,128)(2,1)S(1)}, bf16[16,256]{1,0:T(8,128)(2,1)S(1)}, bf16[16,256]{1,0:T(8,128)(2,1)S(1)}, bf16[16,256]{1,0:T(8,128)(2,1)S(1)}) custom-call(s32[2]{0:T(128)S(1)} %pad_add_fusion.place, f32[1,2048]{1,0:T(1,128)S(1)} %bitcast.29, bf16[2048,512]{1,0:T(8,128)(2,1)S(1)} %join_weight.1.weight, ...), custom_call_target="tpu_custom_call" | custom-call | tf_op jit(solution)/shard_map/attend/pallas_call | solution.py:294
  127.8 3.1 %collective-permute-start.7 = (bf16[16,256]{1,0:T(8,128)(2,1)S(1)}, bf16[16,256]{1,0:T(8,128)(2,1)S(1)}, u32[]{:S(2)}, u32[]{:S(2)}) collective-permute-start(bf16[16,256]{1,0:T(8,128)(2,1)S(1)} %get-tuple-element.11), channel_id=1, source_target_pairs={{0,32},{32,0},{1,33},{33,1},{2,34},{34,2},{3,35},{35,3},{4,36},{36... | collective-permute-start | bytes 24584 | tf_op jit(solution)/shard_map/ppermute | solution.py:335
  130.9 3.4 %collective-permute-start.8 = (bf16[16,256]{1,0:T(8,128)(2,1)S(1)}, bf16[16,256]{1,0:T(8,128)(2,1)S(1)}, u32[]{:S(2)}, u32[]{:S(2)}) collective-permute-start(bf16[16,256]{1,0:T(8,128)(2,1)S(1)} %get-tuple-element.12), channel_id=1, source_target_pairs={{0,64},{64,0},{1,65},{65,1},{2,66},{66,2},{3,67},{67,3},{4,68},{68... | collective-permute-start | bytes 24584 | tf_op jit(solution)/shard_map/ppermute | solution.py:335
  134.3 2.1 %collective-permute-start.9 = (bf16[16,256]{1,0:T(8,128)(2,1)S(1)}, bf16[16,256]{1,0:T(8,128)(2,1)S(1)}, u32[]{:S(2)}, u32[]{:S(2)}) collective-permute-start(bf16[16,256]{1,0:T(8,128)(2,1)S(1)} %get-tuple-element.13), channel_id=1, source_target_pairs={{0,96},{32,64},{64,32},{96,0},{1,97},{33,65},{65,33},{97,1},{2,98}... | collective-permute-start | bytes 24584 | tf_op jit(solution)/shard_map/ppermute | solution.py:383
  137.1 9.9 %all-to-all-start.3 = ((f32[16,1,64]{2,1,0:T(1,128)}), f32[16,1,64]{2,1,0:T(1,128)S(1)}, u32[]{:S(2)}, u32[]{:S(2)}) async-start(f32[16,1,64]{2,1,0:T(1,128)} %broadcast_in_dim.2), calls=%async_computation.3 | async-start | bytes 16384 | tf_op jit(solution)/shard_map/all_to_all | solution.py:331
  147.6 6.4 %all-to-all-done.3 = f32[16,1,64]{2,1,0:T(1,128)S(1)} async-done(((f32[16,1,64]{2,1,0:T(1,128)}), f32[16,1,64]{2,1,0:T(1,128)S(1)}, u32[]{:S(2)}, u32[]{:S(2)}) %all-to-all-start.3) | async-done | bytes 4128 | tf_op jit(solution)/shard_map/all_to_all | solution.py:331
  (38 shorter events, 7.0 us)
Async XLA Ops:
  0.6 10.4 %copy-start = (bf16[1,1,40,8,2048]{4,3,2,1,0:T(8,128)(2,1)S(1)}, bf16[1,1,40,8,2048]{4,3,2,1,0:T(8,128)(2,1)}, u32[]{:S(2)}) copy-start(bf16[1,1,40,8,2048]{4,3,2,1,0:T(8,128)(2,1)} %param.7) | copy-start | bytes 3932164
  0.7 1.1 copy-start.6
  1.7 9.4 %copy-start.7 = (bf16[1,1,16,1024]{3,2,1,0:T(8,128)(2,1)S(1)}, bf16[1,1,16,1024]{3,2,1,0:T(8,128)(2,1)}, u32[]{:S(2)}) copy-start(bf16[1,1,16,1024]{3,2,1,0:T(8,128)(2,1)} %param.12) | copy-start | bytes 98308
  2.6 16.2 %copy-start.9 = (s32[1,1,2,32]{3,2,1,0:T(2,128)S(1)}, s32[1,1,2,32]{3,2,1,0:T(2,128)}, u32[]{:S(2)}) copy-start(s32[1,1,2,32]{3,2,1,0:T(2,128)} %param.9) | copy-start | bytes 772
  2.6 22.7 %all-to-all-start = ((bf16[8,64,512]{2,1,0:T(8,128)(2,1)}), bf16[8,64,512]{2,1,0:T(8,128)(2,1)S(1)}, u32[]{:S(2)}, u32[]{:S(2)}) async-start(bf16[8,64,512]{2,1,0:T(8,128)(2,1)} %columns.1), calls=%async_computation | async-start | bytes 1048576 | tf_op jit(solution)/shard_map/all_to_all | solution.py:331
  11.1 1.1 copy-start.3
  14.8 41.3 %collective-permute-start.5 = (bf16[432,2048]{1,0:T(8,128)(2,1)}, bf16[432,2048]{1,0:T(8,128)(2,1)}, u32[]{:S(2)}, u32[]{:S(2)}) collective-permute-start(bf16[432,2048]{1,0:T(8,128)(2,1)} %get-tuple-element.9), channel_id=1, source_target_pairs={{0,64},{64,0},{1,65},{65,1},{2,66},{66,2},{3,67},{67,3},{4,68},{68... | collective-permute-start | bytes 5308424 | tf_op jit(solution)/shard_map/ppermute | solution.py:335
  25.3 41.8 %all-to-all-start.1 = ((bf16[32,8,2176]{2,1,0:T(8,128)(2,1)}), bf16[32,8,2176]{2,1,0:T(8,128)(2,1)S(1)}, u32[]{:S(2)}, u32[]{:S(2)}) async-start(bf16[32,8,2176]{2,1,0:T(8,128)(2,1)} %pack.1), calls=%async_computation.1 | async-start | bytes 2228224 | tf_op jit(solution)/shard_map/all_to_all | solution.py:331
  32.7 67.8 %collective-permute-start.4 = (bf16[432,2048]{1,0:T(8,128)(2,1)}, bf16[432,2048]{1,0:T(8,128)(2,1)}, u32[]{:S(2)}, u32[]{:S(2)}) collective-permute-start(bf16[432,2048]{1,0:T(8,128)(2,1)} %get-tuple-element.8.m0), channel_id=1, source_target_pairs={{0,32},{32,0},{1,33},{33,1},{2,34},{34,2},{3,35},{35,3},{4,36},{36... | collective-permute-start | bytes 5308424 | tf_op jit(solution)/shard_map/ppermute | solution.py:335
  56.1 48.5 %collective-permute-start.6 = (bf16[432,2048]{1,0:T(8,128)(2,1)}, bf16[432,2048]{1,0:T(8,128)(2,1)}, u32[]{:S(2)}, u32[]{:S(2)}) collective-permute-start(bf16[432,2048]{1,0:T(8,128)(2,1)} %collective-permute-done.5.m2.m0), channel_id=1, source_target_pairs={{0,32},{32,0},{1,33},{33,1},{2,34},{34,2},{3,35},{35,3},{4,36},{36... | collective-permute-start | bytes 5308424 | tf_op jit(solution)/shard_map/ppermute | solution.py:335
  60.5 16.6 %collective-permute-start = (bf16[512,512]{1,0:T(8,128)(2,1)S(1)}, bf16[512,512]{1,0:T(8,128)(2,1)S(1)}, u32[]{:S(2)}, u32[]{:S(2)}) collective-permute-start(bf16[512,512]{1,0:T(8,128)(2,1)S(1)} %bitcast.21), channel_id=1, source_target_pairs={{0,8},{8,16},{16,24},{24,0},{1,9},{9,17},{17,25},{25,1},{2,10},{10... | collective-permute-start | bytes 1572872 | tf_op jit(solution)/shard_map/ppermute | solution.py:339
  63.7 15.5 %collective-permute-start.1 = (bf16[512,512]{1,0:T(8,128)(2,1)S(1)}, bf16[512,512]{1,0:T(8,128)(2,1)}, u32[]{:S(2)}, u32[]{:S(2)}) collective-permute-start(bf16[512,512]{1,0:T(8,128)(2,1)S(1)} %bitcast.22), channel_id=1, source_target_pairs={{0,24},{8,0},{16,8},{24,16},{1,25},{9,1},{17,9},{25,17},{2,26},{10... | collective-permute-start | bytes 1572872 | tf_op jit(solution)/shard_map/ppermute | solution.py:339
  68.6 14.9 %collective-permute-start.10 = (bf16[128,2048]{1,0:T(8,128)(2,1)S(1)}, bf16[128,2048]{1,0:T(8,128)(2,1)}, u32[]{:S(2)}, u32[]{:S(2)}) collective-permute-start(bf16[128,2048]{1,0:T(8,128)(2,1)S(1)} %bitcast.24), channel_id=1, source_target_pairs={{0,64},{64,0},{1,65},{65,1},{2,66},{66,2},{3,67},{67,3},{4,68},{68... | collective-permute-start | bytes 1572872 | tf_op jit(solution)/shard_map/ppermute | solution.py:335
  77.1 19.5 %copy-start.1 = (bf16[512,512]{1,0:T(8,128)(2,1)}, bf16[512,512]{1,0:T(8,128)(2,1)S(1)}, u32[]{:S(2)}) copy-start(bf16[512,512]{1,0:T(8,128)(2,1)S(1)} %collective-permute-done.left) | copy-start | bytes 1572868
  77.1 10.7 %collective-permute-start.2 = (bf16[256,512]{1,0:T(8,128)(2,1)S(1)}, bf16[256,512]{1,0:T(8,128)(2,1)S(1)}, u32[]{:S(2)}, u32[]{:S(2)}) collective-permute-start(bf16[256,512]{1,0:T(8,128)(2,1)S(1)} %slice.12), channel_id=1, source_target_pairs={{0,8},{8,16},{16,24},{24,0},{1,9},{9,17},{17,25},{25,1},{2,10},{10... | collective-permute-start | bytes 786440 | tf_op jit(solution)/shard_map/ppermute | solution.py:339
  79.2 21.3 %collective-permute-start.12 = (bf16[128,2048]{1,0:T(8,128)(2,1)S(1)}, bf16[128,2048]{1,0:T(8,128)(2,1)}, u32[]{:S(2)}, u32[]{:S(2)}) collective-permute-start(bf16[128,2048]{1,0:T(8,128)(2,1)S(1)} %bitcast.25), channel_id=1, source_target_pairs={{0,32},{32,0},{1,33},{33,1},{2,34},{34,2},{3,35},{35,3},{4,36},{36... | collective-permute-start | bytes 1572872 | tf_op jit(solution)/shard_map/ppermute | solution.py:335
  83.5 21.1 %collective-permute-start.11 = (bf16[128,2048]{1,0:T(8,128)(2,1)}, bf16[128,2048]{1,0:T(8,128)(2,1)}, u32[]{:S(2)}, u32[]{:S(2)}) collective-permute-start(bf16[128,2048]{1,0:T(8,128)(2,1)} %collective-permute-done.10.h0), channel_id=1, source_target_pairs={{0,32},{32,0},{1,33},{33,1},{2,34},{34,2},{3,35},{35,3},{4,36},{36... | collective-permute-start | bytes 1572872 | tf_op jit(solution)/shard_map/ppermute | solution.py:335
  87.8 8.8 %collective-permute-start.3 = (bf16[256,512]{1,0:T(8,128)(2,1)S(1)}, bf16[256,512]{1,0:T(8,128)(2,1)S(1)}, u32[]{:S(2)}, u32[]{:S(2)}) collective-permute-start(bf16[256,512]{1,0:T(8,128)(2,1)S(1)} %slice.13), channel_id=1, source_target_pairs={{0,24},{8,0},{16,8},{24,16},{1,25},{9,1},{17,9},{25,17},{2,26},{10... | collective-permute-start | bytes 786440 | tf_op jit(solution)/shard_map/ppermute | solution.py:339
  96.6 0.7 copy-start.4
  97.3 1.0 copy-start.2
  98.3 0.9 copy-start.5
  104.6 15.0 %copy-start.8 = (f32[2048]{0:T(1024)S(1)}, f32[2048]{0:T(1024)}, u32[]{:S(2)}) copy-start(f32[2048]{0:T(1024)} %param.10) | copy-start | bytes 24580
  109.3 27.0 %all-to-all-start.2 = ((f32[32,1,64]{2,1,0:T(1,128)}), f32[32,1,64]{2,1,0:T(1,128)S(1)}, u32[]{:S(2)}, u32[]{:S(2)}) async-start(f32[32,1,64]{2,1,0:T(1,128)} %bitcast.15), calls=%async_computation.2 | async-start | bytes 32768 | tf_op jit(solution)/shard_map/all_to_all | solution.py:331
  127.8 19.2 %collective-permute-start.7 = (bf16[16,256]{1,0:T(8,128)(2,1)S(1)}, bf16[16,256]{1,0:T(8,128)(2,1)S(1)}, u32[]{:S(2)}, u32[]{:S(2)}) collective-permute-start(bf16[16,256]{1,0:T(8,128)(2,1)S(1)} %get-tuple-element.11), channel_id=1, source_target_pairs={{0,32},{32,0},{1,33},{33,1},{2,34},{34,2},{3,35},{35,3},{4,36},{36... | collective-permute-start | bytes 24584 | tf_op jit(solution)/shard_map/ppermute | solution.py:335
  130.9 16.1 %collective-permute-start.8 = (bf16[16,256]{1,0:T(8,128)(2,1)S(1)}, bf16[16,256]{1,0:T(8,128)(2,1)S(1)}, u32[]{:S(2)}, u32[]{:S(2)}) collective-permute-start(bf16[16,256]{1,0:T(8,128)(2,1)S(1)} %get-tuple-element.12), channel_id=1, source_target_pairs={{0,64},{64,0},{1,65},{65,1},{2,66},{66,2},{3,67},{67,3},{4,68},{68... | collective-permute-start | bytes 24584 | tf_op jit(solution)/shard_map/ppermute | solution.py:335
  134.3 12.7 %collective-permute-start.9 = (bf16[16,256]{1,0:T(8,128)(2,1)S(1)}, bf16[16,256]{1,0:T(8,128)(2,1)S(1)}, u32[]{:S(2)}, u32[]{:S(2)}) collective-permute-start(bf16[16,256]{1,0:T(8,128)(2,1)S(1)} %get-tuple-element.13), channel_id=1, source_target_pairs={{0,96},{32,64},{64,32},{96,0},{1,97},{33,65},{65,33},{97,1},{2,98}... | collective-permute-start | bytes 24584 | tf_op jit(solution)/shard_map/ppermute | solution.py:383
  137.1 17.0 %all-to-all-start.3 = ((f32[16,1,64]{2,1,0:T(1,128)}), f32[16,1,64]{2,1,0:T(1,128)S(1)}, u32[]{:S(2)}, u32[]{:S(2)}) async-start(f32[16,1,64]{2,1,0:T(1,128)} %broadcast_in_dim.2), calls=%async_computation.3 | async-start | bytes 16384 | tf_op jit(solution)/shard_map/all_to_all | solution.py:331

commit v5 on v4

--- a/solution.py
+++ b/solution.py
@@ -1,3 +1,5 @@
+import functools
+
 import jax
 import jax.numpy as jnp
 from jax import lax
@@ -170,39 +172,50 @@
     return pl.ds(pl.multiple_of(((ring[0] + step) % 4) * BLOCK, BLOCK), BLOCK)
 
 
-def weight_body(ring, own, left, right, top, bottom, out):
-    half = BLOCK // 2
-    out[block_rows(ring, 0), :] = own[...]
-    out[block_rows(ring, 3), :] = left[...]
-    out[block_rows(ring, 1), :] = right[...]
-    far = pl.multiple_of(((ring[0] + 2) % 4) * BLOCK, BLOCK)
-    out[pl.ds(far, half), :] = top[...]
-    out[pl.ds(pl.multiple_of(far + half, half), half), :] = bottom[...]
+def weight_body(ring, own, left, right, far, out):
+    for step, piece in ((0, own), (3, left), (1, right), (2, far)):
+        out[block_rows(ring, step), :] = piece[...]
 
 
 def join_weight(ring, pieces):
     return pl.pallas_call(
         weight_body,
         out_shape=jax.ShapeDtypeStruct((D, 2 * COLS), jnp.bfloat16),
-        in_specs=[SM] + [VM] * 5,
+        in_specs=[SM] + [VM] * 4,
         out_specs=VM,
         compiler_params=params(),
         name="join_weight",
     )(ring, *pieces)
 
 
-def grad_body(place, weight, m0, m1, h0, h1, *refs):
-    *base, out, normal, tails, cots, own, row, arrivals = refs
+def scale_body(message, gain, out):
+    values = message[...].astype(jnp.float32)
+    out[...] = (values * inverse_rms(values) * gain[...]).astype(jnp.bfloat16)
+
+
+def scale(message, gain):
+    return pl.pallas_call(
+        scale_body,
+        out_shape=pltpu.HBM((TOK, D), jnp.bfloat16),
+        grid=(1,),
+        in_specs=[pl.BlockSpec((TOK, D), lambda i: (0, 0)), pl.BlockSpec((1, D), lambda i: (0, 0))],
+        out_specs=pl.BlockSpec((TOK, D), lambda i: (0, 0)),
+        compiler_params=params(),
+        name="scale",
+    )(in_hbm(message), gain)
+
+
+def grad_body(place, weight, m0, m1, m2, m3, h0, h1, h2, h3, out, normal, tails, cots, own, row, arrivals):
     size = ENC * LEN
     copies = []
-    for r, message in enumerate((m0, m1)):
+    for r, message in enumerate((m0, m1, m2, m3)):
         head = pltpu.make_async_copy(message.at[pl.ds(0, OWN)], own.at[r], arrivals.at[r, 0])
         tail = pltpu.make_async_copy(message.at[pl.ds(TOK, MROWS - TOK)], tails.at[r], arrivals.at[r, 1])
         head.start()
         tail.start()
         copies.append((head, tail))
     spot = (lax.broadcasted_iota(jnp.int32, (OWN, 1), 0) // LEN).astype(jnp.float32)
-    for r, aid in enumerate((h0, h1)):
+    for r, aid in enumerate((h0, h1, h2, h3)):
         at = r * size
         helped = aid[...].astype(jnp.float32)
         normal[at + OWN : at + size, :] = helped * inverse_rms(helped)
@@ -226,36 +239,32 @@
         )
         row[:, d : d + BLOCK] = jnp.sum(normal[:, d : d + BLOCK] * back, axis=0, keepdims=True)
     for f in range(32):
-        terms = row[:, f * 64 : (f + 1) * 64]
-        if base:
-            terms = terms + base[0][f : f + 1, :]
-        out[f : f + 1, :] = terms
-
-
-def grad(place, weight, messages, hs, base=None):
-    extra = () if base is None else (base,)
+        out[f : f + 1, :] = row[:, f * 64 : (f + 1) * 64]
+
+
+def grad(place, weight, messages, hs):
     return pl.pallas_call(
         grad_body,
         out_shape=jax.ShapeDtypeStruct((32, 64), jnp.float32),
-        in_specs=[SM, VM] + [HB] * 2 + [VM] * (2 + len(extra)),
+        in_specs=[SM, VM] + [HB] * G + [VM] * G,
         out_specs=VM,
         scratch_shapes=[
-            pltpu.VMEM((2 * ENC * LEN, D), jnp.float32),
-            pltpu.VMEM((2, MROWS - TOK, D), jnp.bfloat16),
-            pltpu.VMEM((2 * ENC * LEN, 2 * COLS), jnp.bfloat16),
-            pltpu.VMEM((2, OWN, D), jnp.bfloat16),
+            pltpu.VMEM((G * ENC * LEN, D), jnp.float32),
+            pltpu.VMEM((G, MROWS - TOK, D), jnp.bfloat16),
+            pltpu.VMEM((G * ENC * LEN, 2 * COLS), jnp.bfloat16),
+            pltpu.VMEM((G, OWN, D), jnp.bfloat16),
             pltpu.VMEM((1, D), jnp.float32),
-            pltpu.SemaphoreType.DMA((2, 2)),
+            pltpu.SemaphoreType.DMA((G, 2)),
         ],
         compiler_params=params(),
         name="gain_grad",
-    )(place, weight, *map(in_hbm, messages), *hs, *extra)
-
-
-def attend_body(place, gain, weight, m0, m1, m2, m3, o0, o1, o2, o3, tokens, asked, arrivals):
+    )(place, weight, *map(in_hbm, messages), *hs)
+
+
+def attend_body(scaled, place, gain, weight, x0, x1, m0, m1, o0, o1, tokens, asked, states, arrivals):
     copies = []
-    for r, message in enumerate((m0, m1, m2, m3)):
-        x = pltpu.make_async_copy(message.at[pl.ds(0, TOK)], tokens.at[r], arrivals.at[r, 0])
+    for r, (source, message) in enumerate(((x0, m0), (x1, m1))):
+        x = pltpu.make_async_copy(source.at[pl.ds(0, TOK)], tokens.at[r], arrivals.at[r, 0])
         q = pltpu.make_async_copy(message.at[pl.ds(QROW, DEC)], asked.at[r], arrivals.at[r, 1])
         x.start()
         q.start()
@@ -266,44 +275,53 @@
     same = row_head == col_head
     spot = (lax.broadcasted_iota(jnp.int32, (1, TOK), 1) // LEN).astype(jnp.float32)
     upper = place[1] == 1
-    for r, out in enumerate((o0, o1, o2, o3)):
+    for r in range(2):
         for copy in copies[r]:
             copy.wait()
-        values = tokens[r].astype(jnp.float32)
-        scaled = (values * inverse_rms(values) * gain[...]).astype(jnp.bfloat16)
-        states = jnp.dot(scaled, weight[...], preferred_element_type=jnp.float32).astype(jnp.bfloat16)
+        x = tokens[r]
+        if not scaled:
+            values = x.astype(jnp.float32)
+            x = (values * inverse_rms(values) * gain[...]).astype(jnp.bfloat16)
+        states[r] = jnp.dot(x, weight[...], preferred_element_type=jnp.float32).astype(jnp.bfloat16)
+    scores = []
+    for r in range(2):
         query = jnp.where(
             upper,
             asked[r, :, COLS : 2 * COLS].astype(jnp.float32),
             asked[r, :, :COLS].astype(jnp.float32),
         )
         spread = jnp.where(same, jnp.concatenate([query] * GH, axis=0), 0.0).astype(jnp.bfloat16)
-        scores = lax.dot_general(
-            spread, states[:, :COLS], (((1,), (1,)), ((), ())), preferred_element_type=jnp.float32
+        score = lax.dot_general(
+            spread, states[r, :, :COLS], (((1,), (1,)), ((), ())), preferred_element_type=jnp.float32
         ) * HEAD_DIM ** (-0.5)
         count = asked[r, :, 2 * COLS : 2 * COLS + TOK].astype(jnp.float32)[0:1, :]
-        scores = jnp.where(spot < count, scores, -jnp.inf)
-        raised = jnp.exp(scores - jnp.max(scores, axis=-1, keepdims=True))
-        weights = (raised / jnp.sum(raised, axis=-1, keepdims=True)).astype(jnp.bfloat16)
-        mixed = jnp.dot(weights, states[:, COLS:], preferred_element_type=jnp.float32)
+        scores.append(jnp.where(spot < count, score, -jnp.inf))
+    scores = jnp.concatenate(scores, axis=0)
+    raised = jnp.exp(scores - jnp.max(scores, axis=-1, keepdims=True))
+    weights = (raised / jnp.sum(raised, axis=-1, keepdims=True)).astype(jnp.bfloat16)
+    for r, out in enumerate((o0, o1)):
+        mixed = jnp.dot(
+            weights[r * rows : (r + 1) * rows, :], states[r, :, COLS:], preferred_element_type=jnp.float32
+        )
         mixed = jnp.where(same, mixed, 0.0).reshape(GH, DEC, COLS)
         out[...] = jnp.sum(mixed, axis=0).astype(jnp.bfloat16)
 
 
-def attend(place, gain, weight, messages):
-    return pl.pallas_call(
-        attend_body,
-        out_shape=tuple(jax.ShapeDtypeStruct((DEC, COLS), jnp.bfloat16) for _ in range(G)),
-        in_specs=[SM, VM, VM] + [HB] * G,
-        out_specs=(VM,) * G,
+def attend(place, gain, weight, sources, messages, scaled):
+    return pl.pallas_call(
+        functools.partial(attend_body, scaled),
+        out_shape=tuple(jax.ShapeDtypeStruct((DEC, COLS), jnp.bfloat16) for _ in range(2)),
+        in_specs=[SM, VM, VM] + [HB] * 4,
+        out_specs=(VM,) * 2,
         scratch_shapes=[
-            pltpu.VMEM((G, TOK, D), jnp.bfloat16),
-            pltpu.VMEM((G, DEC, D), jnp.bfloat16),
-            pltpu.SemaphoreType.DMA((G, 2)),
+            pltpu.VMEM((2, TOK, D), jnp.bfloat16),
+            pltpu.VMEM((2, DEC, D), jnp.bfloat16),
+            pltpu.VMEM((2, TOK, 2 * COLS), jnp.bfloat16),
+            pltpu.SemaphoreType.DMA((2, 2)),
         ],
         compiler_params=params(),
         name="attend",
-    )(place, gain, weight, *map(in_hbm, messages))
+    )(place, gain, weight, *map(in_hbm, sources), *map(in_hbm, messages))
 
 
 def assemble_body(member, p0, p1, p2, p3, out):
@@ -367,9 +385,10 @@
 
     left = turn(by_y, 1)
     right = turn(by_y, 3)
-    top = turn(left[: BLOCK // 2], 1)
-    bottom = turn(right[BLOCK // 2 :], 3)
-    weight = join_weight(ring, (by_y, left, right, top, bottom))
+    opposite = turn(left, 1)
+    weight = join_weight(ring, (by_y, left, right, opposite))
+    s_0 = scale(near, gain)
+    s_1 = scale(m_c, gain)
 
     tags = arrived[:, 0, D].astype(jnp.int32)
     h_own = unpack(tags, arrived).reshape(AID, D)
@@ -377,14 +396,14 @@
     h_c = swap(h_own, "core")
     h_cz = swap(h_z, "core")
 
-    mixed = attend(place, gain, weight, messages)
-    from_core = swap(mixed[1], "core")
-    from_z = swap(mixed[2], "zl")
-    from_both = lax.ppermute(mixed[3], GROUP, [(i, i ^ 3) for i in range(G)])
-    context_out = assemble(member, (mixed[0], from_core, from_z, from_both)).reshape(1, 1, DEC, HW)
-
-    row_terms = grad(place, weight, (near, m_c), (h_own, h_c))
-    row_terms = grad(place, weight, (m_z, m_cz), (h_z, h_cz), row_terms)
+    mixed_own, mixed_core = attend(place, gain, weight, (s_0, s_1), (near, m_c), True)
+    mixed_z, mixed_both = attend(place, gain, weight, (m_z, m_cz), (m_z, m_cz), False)
+    from_core = swap(mixed_core, "core")
+    from_z = swap(mixed_z, "zl")
+    from_both = lax.ppermute(mixed_both, GROUP, [(i, i ^ 3) for i in range(G)])
+    context_out = assemble(member, (mixed_own, from_core, from_z, from_both)).reshape(1, 1, DEC, HW)
+
+    row_terms = grad(place, weight, messages, (h_own, h_c, h_z, h_cz))
     parts = exchange(row_terms.reshape(32, 1, 64), FSDP)
     share = jnp.sum(parts, axis=0)
     gathered = exchange(jnp.broadcast_to(share[None], (16, 1, 64)), DP)

time: 156 us -> 154 us (0.987)
  starting transfers between devices: 76.3 us -> 70.9 us
  Pallas kernels: 25.6 us -> 29.8 us
    pallas_call x1 -> x4, Pallas kernels: 8.27 us -> 14.5 us  [the longest x2 8.64 us: attend(): pl.pallas_call(functools.partial(attend_body, scaled), out_shape=tuple((j...]
    ppermute x4 -> x3, starting transfers between devices: 11.7 us -> 8.5 us  [turn(): return lax.ppermute(array, 'x', [(i, (i + step) % 4) for i in range(4)])]
    all_to_all x4, starting transfers between devices: 35.3 us -> 32.4 us  [exchange(): return lax.all_to_all(array, axes, 0, 0, tiled=True)]
    pallas_call x2 -> x1, Pallas kernels: 8.81 us -> 6.69 us  [grad(): pl.pallas_call(grad_body, out_shape=jax.ShapeDtypeStruct((32, 64), jnp.fl...]
    ppermute x4 -> x3, waiting for transfers between devices: 10.8 us -> 11.2 us  [turn(): return lax.ppermute(array, 'x', [(i, (i + step) % 4) for i in range(4)])]
  transfers between devices with their start and end apart: 17 -> 16, of which waited for: 6 -> 6; matrix products, arithmetic and copies ran while one was open for 2% -> 1% of each run, Pallas kernels for 13% -> 15%
where the time goes in v5:
time: 154 us; the launch traced here: 153 us
  starting transfers between devices  70.9 us (46%)
  waiting for transfers between devices  42.9 us (28%)
  Pallas kernels  29.8 us (19%)
  local copies, waits for them, and re-layouts  6.47 us (4%)
  between operations  1.58 us (1%)
    all_to_all x4, starting transfers between devices, exchange(): return lax.all_to_all(array, axes, 0, 0, tiled=True)  32.4 us
    ppermute x8, starting transfers between devices, swap(): return lax.ppermute(array, axis, [(0, 1), (1, 0)])  27.9 us
    ppermute x8, waiting for transfers between devices, swap(): return lax.ppermute(array, axis, [(0, 1), (1, 0)])  21.3 us
    ppermute x3, waiting for transfers between devices, turn(): return lax.ppermute(array, 'x', [(i, (i + step) % 4) for i in range(4)])  11.2 us
    all_to_all x4, waiting for transfers between devices, exchange(): return lax.all_to_all(array, axes, 0, 0, tiled=True)  10.4 us
    pallas_call x2, Pallas kernels, attend(): pl.pallas_call(functools.partial(attend_body, scaled), out_shape=tuple((j...  8.64 us
    ppermute x3, starting transfers between devices, turn(): return lax.ppermute(array, 'x', [(i, (i + step) % 4) for i in range(4)])  8.5 us
    pallas_call x1, Pallas kernels, grad(): pl.pallas_call(grad_body, out_shape=jax.ShapeDtypeStruct((32, 64), jnp.fl...  6.69 us
  transfers between devices with their start and end apart: 16, of which 6 were waited for; matrix products, arithmetic and copies ran while one was open for 1% of the time, Pallas kernels for 15%

profile of v5, /device:TPU:1, one launch (start us, length us, event | category | flops | bytes accessed | tf_op | source)
XLA Modules:
  0.0 153.0 jit_solution(15859583907929367039)
XLA Ops:
  0.7 1.0 copy-done.6
  2.6 7.8 %all-to-all-start = ((bf16[8,64,512]{2,1,0:T(8,128)(2,1)}), bf16[8,64,512]{2,1,0:T(8,128)(2,1)S(1)}, u32[]{:S(2)}, u32[]{:S(2)}) async-start(bf16[8,64,512]{2,1,0:T(8,128)(2,1)} %columns.1), calls=%async_computation | async-start | bytes 1048576 | tf_op jit(solution)/shard_map/all_to_all | solution.py:349
  11.1 1.1 copy-done.1
  12.2 2.6 %prep.1 = (bf16[432,2048]{1,0:T(8,128)(2,1)}, bf16[432,2048]{1,0:T(8,128)(2,1)}) custom-call(s32[2]{0:T(128)S(1)} %pad_add_fusion.place, s32[1]{0:T(128)} %bitcast.18.count, bf16[320,2048]{1,0:T(8,128)(2,1)S(1)} %bitcast.20, bf16[192,2048]{1,0:T(8,128)(2,1)S(1)} %bitcast.27, bf16[16,1024]{1,0:T(8,128)(2,1)S(1)} %bitcast.32), custom_call_target="tpu_custom_call" | custom-call | tf_op jit(solution)/shard_map/prep/pallas_call | solution.py:114
  14.8 4.0 %collective-permute-start.5 = (bf16[432,2048]{1,0:T(8,128)(2,1)}, bf16[432,2048]{1,0:T(8,128)(2,1)}, u32[]{:S(2)}, u32[]{:S(2)}) collective-permute-start(bf16[432,2048]{1,0:T(8,128)(2,1)} %get-tuple-element.11), channel_id=1, source_target_pairs={{0,64},{64,0},{1,65},{65,1},{2,66},{66,2},{3,67},{67,3},{4,68},{68... | collective-permute-start | bytes 5308424 | tf_op jit(solution)/shard_map/ppermute | solution.py:353
  18.8 2.4 %pack.1 = bf16[32,8,2176]{2,1,0:T(8,128)(2,1)} custom-call(s32[2,32]{1,0:T(2,128)S(1)} %bitcast.33, bf16[40,8,2048]{2,1,0:T(8,128)(2,1)} %bitcast.19), custom_call_target="tpu_custom_call" | custom-call | tf_op jit(solution)/shard_map/pack/pallas_call | solution.py:79
  21.3 4.0 %all-to-all-done = bf16[8,64,512]{2,1,0:T(8,128)(2,1)S(1)} async-done(((bf16[8,64,512]{2,1,0:T(8,128)(2,1)}), bf16[8,64,512]{2,1,0:T(8,128)(2,1)S(1)}, u32[]{:S(2)}, u32[]{:S(2)}) %all-to-all-start) | async-done | bytes 524320 | tf_op jit(solution)/shard_map/all_to_all | solution.py:349
  25.3 7.4 %all-to-all-start.1 = ((bf16[32,8,2176]{2,1,0:T(8,128)(2,1)}), bf16[32,8,2176]{2,1,0:T(8,128)(2,1)S(1)}, u32[]{:S(2)}, u32[]{:S(2)}) async-start(bf16[32,8,2176]{2,1,0:T(8,128)(2,1)} %pack.1), calls=%async_computation.1 | async-start | bytes 2228224 | tf_op jit(solution)/shard_map/all_to_all | solution.py:349
  32.7 2.7 %collective-permute-start.3 = (bf16[432,2048]{1,0:T(8,128)(2,1)}, bf16[432,2048]{1,0:T(8,128)(2,1)}, u32[]{:S(2)}, u32[]{:S(2)}) collective-permute-start(bf16[432,2048]{1,0:T(8,128)(2,1)} %get-tuple-element.8.message.m0), channel_id=1, source_target_pairs={{0,32},{32,0},{1,33},{33,1},{2,34},{34,2},{3,35},{35,3},{4,36},{36... | collective-permute-start | bytes 5308424 | tf_op jit(solution)/shard_map/ppermute | solution.py:353
  35.4 20.7 %collective-permute-done.5.x0.m0.m2 = bf16[432,2048]{1,0:T(8,128)(2,1)} collective-permute-done((bf16[432,2048]{1,0:T(8,128)(2,1)}, bf16[432,2048]{1,0:T(8,128)(2,1)}, u32[]{:S(2)}, u32[]{:S(2)}) %collective-permute-start.5) | collective-permute-done | bytes 1769504 | tf_op jit(solution)/shard_map/ppermute | solution.py:353
  56.1 4.5 %collective-permute-start.6 = (bf16[432,2048]{1,0:T(8,128)(2,1)}, bf16[432,2048]{1,0:T(8,128)(2,1)}, u32[]{:S(2)}, u32[]{:S(2)}) collective-permute-start(bf16[432,2048]{1,0:T(8,128)(2,1)} %collective-permute-done.5.x0.m0.m2), channel_id=1, source_target_pairs={{0,32},{32,0},{1,33},{33,1},{2,34},{34,2},{3,35},{35,3},{4,36},{36... | collective-permute-start | bytes 5308424 | tf_op jit(solution)/shard_map/ppermute | solution.py:353
  60.6 3.1 %collective-permute-start = (bf16[512,512]{1,0:T(8,128)(2,1)S(1)}, bf16[512,512]{1,0:T(8,128)(2,1)S(1)}, u32[]{:S(2)}, u32[]{:S(2)}) collective-permute-start(bf16[512,512]{1,0:T(8,128)(2,1)S(1)} %bitcast.21), channel_id=1, source_target_pairs={{0,8},{8,16},{16,24},{24,0},{1,9},{9,17},{17,25},{25,1},{2,10},{10... | collective-permute-start | bytes 1572872 | tf_op jit(solution)/shard_map/ppermute | solution.py:357
  63.7 3.4 %collective-permute-start.1 = (bf16[512,512]{1,0:T(8,128)(2,1)S(1)}, bf16[512,512]{1,0:T(8,128)(2,1)}, u32[]{:S(2)}, u32[]{:S(2)}) collective-permute-start(bf16[512,512]{1,0:T(8,128)(2,1)S(1)} %bitcast.22), channel_id=1, source_target_pairs={{0,24},{8,0},{16,8},{24,16},{1,25},{9,1},{17,9},{25,17},{2,26},{10... | collective-permute-start | bytes 1572872 | tf_op jit(solution)/shard_map/ppermute | solution.py:357
  68.6 3.4 %collective-permute-start.10 = (bf16[128,2048]{1,0:T(8,128)(2,1)S(1)}, bf16[128,2048]{1,0:T(8,128)(2,1)}, u32[]{:S(2)}, u32[]{:S(2)}) collective-permute-start(bf16[128,2048]{1,0:T(8,128)(2,1)S(1)} %bitcast.24), channel_id=1, source_target_pairs={{0,64},{64,0},{1,65},{65,1},{2,66},{66,2},{3,67},{67,3},{4,68},{68... | collective-permute-start | bytes 1572872 | tf_op jit(solution)/shard_map/ppermute | solution.py:353
  72.0 5.2 %collective-permute-done.left = bf16[512,512]{1,0:T(8,128)(2,1)S(1)} collective-permute-done((bf16[512,512]{1,0:T(8,128)(2,1)S(1)}, bf16[512,512]{1,0:T(8,128)(2,1)S(1)}, u32[]{:S(2)}, u32[]{:S(2)}) %collective-permute-start) | collective-permute-done | bytes 524320 | tf_op jit(solution)/shard_map/ppermute | solution.py:357
  77.2 2.0 %collective-permute-start.2 = (bf16[512,512]{1,0:T(8,128)(2,1)S(1)}, bf16[512,512]{1,0:T(8,128)(2,1)S(1)}, u32[]{:S(2)}, u32[]{:S(2)}) collective-permute-start(bf16[512,512]{1,0:T(8,128)(2,1)S(1)} %collective-permute-done.left), channel_id=1, source_target_pairs={{0,8},{8,16},{16,24},{24,0},{1,9},{9,17},{17,25},{25,1},{2,10},{10... | collective-permute-start | bytes 1572872 | tf_op jit(solution)/shard_map/ppermute | solution.py:357
  80.0 2.9 %collective-permute-start.9 = (bf16[128,2048]{1,0:T(8,128)(2,1)S(1)}, bf16[128,2048]{1,0:T(8,128)(2,1)}, u32[]{:S(2)}, u32[]{:S(2)}) collective-permute-start(bf16[128,2048]{1,0:T(8,128)(2,1)S(1)} %bitcast.25), channel_id=1, source_target_pairs={{0,32},{32,0},{1,33},{33,1},{2,34},{34,2},{3,35},{35,3},{4,36},{36... | collective-permute-start | bytes 1572872 | tf_op jit(solution)/shard_map/ppermute | solution.py:353
  83.5 3.3 %collective-permute-start.11 = (bf16[128,2048]{1,0:T(8,128)(2,1)}, bf16[128,2048]{1,0:T(8,128)(2,1)}, u32[]{:S(2)}, u32[]{:S(2)}) collective-permute-start(bf16[128,2048]{1,0:T(8,128)(2,1)} %collective-permute-done.10.h2), channel_id=1, source_target_pairs={{0,32},{32,0},{1,33},{33,1},{2,34},{34,2},{3,35},{35,3},{4,36},{36... | collective-permute-start | bytes 1572872 | tf_op jit(solution)/shard_map/ppermute | solution.py:353
  86.9 6.0 %collective-permute-done.2.far = bf16[512,512]{1,0:T(8,128)(2,1)S(1)} collective-permute-done((bf16[512,512]{1,0:T(8,128)(2,1)S(1)}, bf16[512,512]{1,0:T(8,128)(2,1)S(1)}, u32[]{:S(2)}, u32[]{:S(2)}) %collective-permute-start.2) | collective-permute-done | bytes 524320 | tf_op jit(solution)/shard_map/ppermute | solution.py:357
  93.7 1.0 copy-done.3
  95.7 1.2 join_weight.1.weight
  97.0 6.7 %gain_grad.1 = f32[32,64]{1,0:T(8,128)} custom-call(s32[2]{0:T(128)S(1)} %pad_add_fusion.place, bf16[2048,512]{1,0:T(8,128)(2,1)S(1)} %join_weight.1.weight, bf16[432,2048]{1,0:T(8,128)(2,1)} %get-tuple-element.8.message.m0, bf16[432,2048]{1,0:T(8,128)(2,1)} %collective-permute-done.3.message.m1, bf16[432,2048]{1,0:T(8,128)(2,1)} %collective-permute-done.5.x0.m0.m2, ...), custom_call_target="tpu_custom_call" | custom-call | tf_op jit(solution)/shard_map/gain_grad/pallas_call | solution.py:246
  103.7 7.3 %all-to-all-start.2 = ((f32[32,1,64]{2,1,0:T(1,128)}), f32[32,1,64]{2,1,0:T(1,128)S(1)}, u32[]{:S(2)}, u32[]{:S(2)}) async-start(f32[32,1,64]{2,1,0:T(1,128)} %bitcast.15), calls=%async_computation.2 | async-start | bytes 32768 | tf_op jit(solution)/shard_map/all_to_all | solution.py:349
  111.0 3.0 %scale.2.x0 = bf16[320,2048]{1,0:T(8,128)(2,1)} custom-call(bf16[432,2048]{1,0:T(8,128)(2,1)} %get-tuple-element.8.message.m0, f32[1,2048]{1,0:T(1,128)S(1)} %bitcast.28), custom_call_target="tpu_custom_call" | custom-call | tf_op jit(solution)/shard_map/scale/pallas_call | solution.py:197
  114.0 2.9 %scale.3.x1 = bf16[320,2048]{1,0:T(8,128)(2,1)} custom-call(bf16[432,2048]{1,0:T(8,128)(2,1)} %collective-permute-done.3.message.m1, f32[1,2048]{1,0:T(1,128)S(1)} %bitcast.29), custom_call_target="tpu_custom_call" | custom-call | tf_op jit(solution)/shard_map/scale/pallas_call | solution.py:197
  116.9 4.1 %attend.2 = (bf16[16,256]{1,0:T(8,128)(2,1)S(1)}, bf16[16,256]{1,0:T(8,128)(2,1)S(1)}) custom-call(s32[2]{0:T(128)S(1)} %pad_add_fusion.place, f32[1,2048]{1,0:T(1,128)S(1)} %bitcast.30, bf16[2048,512]{1,0:T(8,128)(2,1)S(1)} %join_weight.1.weight, bf16[320,2048]{1,0:T(8,128)(2,1)} %scale.2.x0, bf16[320,2048]{1,0:T(8,128)(2,1)} %scale.3.x1, ...), custom_call_target="tpu_custom_call" | custom-call | tf_op jit(solution)/shard_map/attend/pallas_call | solution.py:311
  121.0 3.8 %collective-permute-start.4 = (bf16[16,256]{1,0:T(8,128)(2,1)S(1)}, bf16[16,256]{1,0:T(8,128)(2,1)S(1)}, u32[]{:S(2)}, u32[]{:S(2)}) collective-permute-start(bf16[16,256]{1,0:T(8,128)(2,1)S(1)} %get-tuple-element.10), channel_id=1, source_target_pairs={{0,32},{32,0},{1,33},{33,1},{2,34},{34,2},{3,35},{35,3},{4,36},{36... | collective-permute-start | bytes 24584 | tf_op jit(solution)/shard_map/ppermute | solution.py:353
  124.8 4.6 %attend.3 = (bf16[16,256]{1,0:T(8,128)(2,1)S(1)}, bf16[16,256]{1,0:T(8,128)(2,1)S(1)}) custom-call(s32[2]{0:T(128)S(1)} %pad_add_fusion.place, f32[1,2048]{1,0:T(1,128)S(1)} %bitcast.31, bf16[2048,512]{1,0:T(8,128)(2,1)S(1)} %join_weight.1.weight, bf16[432,2048]{1,0:T(8,128)(2,1)} %collective-permute-done.5.x0.m0.m2, ...), custom_call_target="tpu_custom_call" | custom-call | tf_op jit(solution)/shard_map/attend/pallas_call | solution.py:311
  129.4 3.4 %collective-permute-start.7 = (bf16[16,256]{1,0:T(8,128)(2,1)S(1)}, bf16[16,256]{1,0:T(8,128)(2,1)S(1)}, u32[]{:S(2)}, u32[]{:S(2)}) collective-permute-start(bf16[16,256]{1,0:T(8,128)(2,1)S(1)} %get-tuple-element.12), channel_id=1, source_target_pairs={{0,64},{64,0},{1,65},{65,1},{2,66},{66,2},{3,67},{67,3},{4,68},{68... | collective-permute-start | bytes 24584 | tf_op jit(solution)/shard_map/ppermute | solution.py:353
  132.7 2.1 %collective-permute-start.8 = (bf16[16,256]{1,0:T(8,128)(2,1)S(1)}, bf16[16,256]{1,0:T(8,128)(2,1)S(1)}, u32[]{:S(2)}, u32[]{:S(2)}) collective-permute-start(bf16[16,256]{1,0:T(8,128)(2,1)S(1)} %get-tuple-element.13), channel_id=1, source_target_pairs={{0,96},{32,64},{64,32},{96,0},{1,97},{33,65},{65,33},{97,1},{2,98}... | collective-permute-start | bytes 24584 | tf_op jit(solution)/shard_map/ppermute | solution.py:403
  135.5 9.9 %all-to-all-start.3 = ((f32[16,1,64]{2,1,0:T(1,128)}), f32[16,1,64]{2,1,0:T(1,128)S(1)}, u32[]{:S(2)}, u32[]{:S(2)}) async-start(f32[16,1,64]{2,1,0:T(1,128)} %broadcast_in_dim.2), calls=%async_computation.3 | async-start | bytes 16384 | tf_op jit(solution)/shard_map/all_to_all | solution.py:349
  146.1 6.4 %all-to-all-done.3 = f32[16,1,64]{2,1,0:T(1,128)S(1)} async-done(((f32[16,1,64]{2,1,0:T(1,128)}), f32[16,1,64]{2,1,0:T(1,128)S(1)}, u32[]{:S(2)}, u32[]{:S(2)}) %all-to-all-start.3) | async-done | bytes 4128 | tf_op jit(solution)/shard_map/all_to_all | solution.py:349
  (36 shorter events, 7.5 us)
Async XLA Ops:
  0.6 10.4 %copy-start = (bf16[1,1,40,8,2048]{4,3,2,1,0:T(8,128)(2,1)S(1)}, bf16[1,1,40,8,2048]{4,3,2,1,0:T(8,128)(2,1)}, u32[]{:S(2)}) copy-start(bf16[1,1,40,8,2048]{4,3,2,1,0:T(8,128)(2,1)} %param.7) | copy-start | bytes 3932164
  0.7 1.1 copy-start.6
  1.7 9.4 %copy-start.8 = (bf16[1,1,16,1024]{3,2,1,0:T(8,128)(2,1)S(1)}, bf16[1,1,16,1024]{3,2,1,0:T(8,128)(2,1)}, u32[]{:S(2)}) copy-start(bf16[1,1,16,1024]{3,2,1,0:T(8,128)(2,1)} %param.12) | copy-start | bytes 98308
  2.6 16.3 %copy-start.9 = (s32[1,1,2,32]{3,2,1,0:T(2,128)S(1)}, s32[1,1,2,32]{3,2,1,0:T(2,128)}, u32[]{:S(2)}) copy-start(s32[1,1,2,32]{3,2,1,0:T(2,128)} %param.9) | copy-start | bytes 772
  2.6 22.7 %all-to-all-start = ((bf16[8,64,512]{2,1,0:T(8,128)(2,1)}), bf16[8,64,512]{2,1,0:T(8,128)(2,1)S(1)}, u32[]{:S(2)}, u32[]{:S(2)}) async-start(bf16[8,64,512]{2,1,0:T(8,128)(2,1)} %columns.1), calls=%async_computation | async-start | bytes 1048576 | tf_op jit(solution)/shard_map/all_to_all | solution.py:349
  11.1 1.1 copy-start.1
  14.8 41.3 %collective-permute-start.5 = (bf16[432,2048]{1,0:T(8,128)(2,1)}, bf16[432,2048]{1,0:T(8,128)(2,1)}, u32[]{:S(2)}, u32[]{:S(2)}) collective-permute-start(bf16[432,2048]{1,0:T(8,128)(2,1)} %get-tuple-element.11), channel_id=1, source_target_pairs={{0,64},{64,0},{1,65},{65,1},{2,66},{66,2},{3,67},{67,3},{4,68},{68... | collective-permute-start | bytes 5308424 | tf_op jit(solution)/shard_map/ppermute | solution.py:353
  25.3 41.8 %all-to-all-start.1 = ((bf16[32,8,2176]{2,1,0:T(8,128)(2,1)}), bf16[32,8,2176]{2,1,0:T(8,128)(2,1)S(1)}, u32[]{:S(2)}, u32[]{:S(2)}) async-start(bf16[32,8,2176]{2,1,0:T(8,128)(2,1)} %pack.1), calls=%async_computation.1 | async-start | bytes 2228224 | tf_op jit(solution)/shard_map/all_to_all | solution.py:349
  32.7 64.2 %collective-permute-start.3 = (bf16[432,2048]{1,0:T(8,128)(2,1)}, bf16[432,2048]{1,0:T(8,128)(2,1)}, u32[]{:S(2)}, u32[]{:S(2)}) collective-permute-start(bf16[432,2048]{1,0:T(8,128)(2,1)} %get-tuple-element.8.message.m0), channel_id=1, source_target_pairs={{0,32},{32,0},{1,33},{33,1},{2,34},{34,2},{3,35},{35,3},{4,36},{36... | collective-permute-start | bytes 5308424 | tf_op jit(solution)/shard_map/ppermute | solution.py:353
  56.1 40.8 %collective-permute-start.6 = (bf16[432,2048]{1,0:T(8,128)(2,1)}, bf16[432,2048]{1,0:T(8,128)(2,1)}, u32[]{:S(2)}, u32[]{:S(2)}) collective-permute-start(bf16[432,2048]{1,0:T(8,128)(2,1)} %collective-permute-done.5.x0.m0.m2), channel_id=1, source_target_pairs={{0,32},{32,0},{1,33},{33,1},{2,34},{34,2},{3,35},{35,3},{4,36},{36... | collective-permute-start | bytes 5308424 | tf_op jit(solution)/shard_map/ppermute | solution.py:353
  60.6 16.6 %collective-permute-start = (bf16[512,512]{1,0:T(8,128)(2,1)S(1)}, bf16[512,512]{1,0:T(8,128)(2,1)S(1)}, u32[]{:S(2)}, u32[]{:S(2)}) collective-permute-start(bf16[512,512]{1,0:T(8,128)(2,1)S(1)} %bitcast.21), channel_id=1, source_target_pairs={{0,8},{8,16},{16,24},{24,0},{1,9},{9,17},{17,25},{25,1},{2,10},{10... | collective-permute-start | bytes 1572872 | tf_op jit(solution)/shard_map/ppermute | solution.py:357
  63.7 16.3 %collective-permute-start.1 = (bf16[512,512]{1,0:T(8,128)(2,1)S(1)}, bf16[512,512]{1,0:T(8,128)(2,1)}, u32[]{:S(2)}, u32[]{:S(2)}) collective-permute-start(bf16[512,512]{1,0:T(8,128)(2,1)S(1)} %bitcast.22), channel_id=1, source_target_pairs={{0,24},{8,0},{16,8},{24,16},{1,25},{9,1},{17,9},{25,17},{2,26},{10... | collective-permute-start | bytes 1572872 | tf_op jit(solution)/shard_map/ppermute | solution.py:357
  68.6 14.9 %collective-permute-start.10 = (bf16[128,2048]{1,0:T(8,128)(2,1)S(1)}, bf16[128,2048]{1,0:T(8,128)(2,1)}, u32[]{:S(2)}, u32[]{:S(2)}) collective-permute-start(bf16[128,2048]{1,0:T(8,128)(2,1)S(1)} %bitcast.24), channel_id=1, source_target_pairs={{0,64},{64,0},{1,65},{65,1},{2,66},{66,2},{3,67},{67,3},{4,68},{68... | collective-permute-start | bytes 1572872 | tf_op jit(solution)/shard_map/ppermute | solution.py:353
  77.2 15.7 %collective-permute-start.2 = (bf16[512,512]{1,0:T(8,128)(2,1)S(1)}, bf16[512,512]{1,0:T(8,128)(2,1)S(1)}, u32[]{:S(2)}, u32[]{:S(2)}) collective-permute-start(bf16[512,512]{1,0:T(8,128)(2,1)S(1)} %collective-permute-done.left), channel_id=1, source_target_pairs={{0,8},{8,16},{16,24},{24,0},{1,9},{9,17},{17,25},{25,1},{2,10},{10... | collective-permute-start | bytes 1572872 | tf_op jit(solution)/shard_map/ppermute | solution.py:357
  79.2 0.8 copy-start.2
  80.0 17.0 %collective-permute-start.9 = (bf16[128,2048]{1,0:T(8,128)(2,1)S(1)}, bf16[128,2048]{1,0:T(8,128)(2,1)}, u32[]{:S(2)}, u32[]{:S(2)}) collective-permute-start(bf16[128,2048]{1,0:T(8,128)(2,1)S(1)} %bitcast.25), channel_id=1, source_target_pairs={{0,32},{32,0},{1,33},{33,1},{2,34},{34,2},{3,35},{35,3},{4,36},{36... | collective-permute-start | bytes 1572872 | tf_op jit(solution)/shard_map/ppermute | solution.py:353
  83.5 13.4 %collective-permute-start.11 = (bf16[128,2048]{1,0:T(8,128)(2,1)}, bf16[128,2048]{1,0:T(8,128)(2,1)}, u32[]{:S(2)}, u32[]{:S(2)}) collective-permute-start(bf16[128,2048]{1,0:T(8,128)(2,1)} %collective-permute-done.10.h2), channel_id=1, source_target_pairs={{0,32},{32,0},{1,33},{33,1},{2,34},{34,2},{3,35},{35,3},{4,36},{36... | collective-permute-start | bytes 1572872 | tf_op jit(solution)/shard_map/ppermute | solution.py:353
  92.9 0.8 copy-start.4
  93.7 1.0 copy-start.3
  94.7 1.0 copy-start.5
  96.9 14.1 %copy-start.7 = (f32[2048]{0:T(1024)S(1)}, f32[2048]{0:T(1024)}, u32[]{:S(2)}) copy-start(f32[2048]{0:T(1024)} %param.10) | copy-start | bytes 24580
  103.7 31.2 %all-to-all-start.2 = ((f32[32,1,64]{2,1,0:T(1,128)}), f32[32,1,64]{2,1,0:T(1,128)S(1)}, u32[]{:S(2)}, u32[]{:S(2)}) async-start(f32[32,1,64]{2,1,0:T(1,128)} %bitcast.15), calls=%async_computation.2 | async-start | bytes 32768 | tf_op jit(solution)/shard_map/all_to_all | solution.py:349
  121.0 24.5 %collective-permute-start.4 = (bf16[16,256]{1,0:T(8,128)(2,1)S(1)}, bf16[16,256]{1,0:T(8,128)(2,1)S(1)}, u32[]{:S(2)}, u32[]{:S(2)}) collective-permute-start(bf16[16,256]{1,0:T(8,128)(2,1)S(1)} %get-tuple-element.10), channel_id=1, source_target_pairs={{0,32},{32,0},{1,33},{33,1},{2,34},{34,2},{3,35},{35,3},{4,36},{36... | collective-permute-start | bytes 24584 | tf_op jit(solution)/shard_map/ppermute | solution.py:353
  129.4 16.1 %collective-permute-start.7 = (bf16[16,256]{1,0:T(8,128)(2,1)S(1)}, bf16[16,256]{1,0:T(8,128)(2,1)S(1)}, u32[]{:S(2)}, u32[]{:S(2)}) collective-permute-start(bf16[16,256]{1,0:T(8,128)(2,1)S(1)} %get-tuple-element.12), channel_id=1, source_target_pairs={{0,64},{64,0},{1,65},{65,1},{2,66},{66,2},{3,67},{67,3},{4,68},{68... | collective-permute-start | bytes 24584 | tf_op jit(solution)/shard_map/ppermute | solution.py:353
  132.7 12.7 %collective-permute-start.8 = (bf16[16,256]{1,0:T(8,128)(2,1)S(1)}, bf16[16,256]{1,0:T(8,128)(2,1)S(1)}, u32[]{:S(2)}, u32[]{:S(2)}) collective-permute-start(bf16[16,256]{1,0:T(8,128)(2,1)S(1)} %get-tuple-element.13), channel_id=1, source_target_pairs={{0,96},{32,64},{64,32},{96,0},{1,97},{33,65},{65,33},{97,1},{2,98}... | collective-permute-start | bytes 24584 | tf_op jit(solution)/shard_map/ppermute | solution.py:403
  135.5 16.9 %all-to-all-start.3 = ((f32[16,1,64]{2,1,0:T(1,128)}), f32[16,1,64]{2,1,0:T(1,128)S(1)}, u32[]{:S(2)}, u32[]{:S(2)}) async-start(f32[16,1,64]{2,1,0:T(1,128)} %broadcast_in_dim.2), calls=%async_computation.3 | async-start | bytes 16384 | tf_op jit(solution)/shard_map/all_to_all | solution.py:349

commit v6 on v5

--- a/solution.py
+++ b/solution.py
@@ -385,7 +385,10 @@
 
     left = turn(by_y, 1)
     right = turn(by_y, 3)
-    opposite = turn(left, 1)
+    onward = jnp.where(core == 0, left, right)
+    opposite = lax.ppermute(
+        onward, ("core", "x"), [(c * 4 + i, c * 4 + (i + (1, 3)[c]) % 4) for c in range(2) for i in range(4)]
+    )
     weight = join_weight(ring, (by_y, left, right, opposite))
     s_0 = scale(near, gain)
     s_1 = scale(m_c, gain)

time: 154 us -> 153 us (level)
  waiting for transfers between devices: 42.9 us -> 39.8 us
  starting transfers between devices: 70.9 us -> 72.7 us
    ppermute x0 -> x1, starting transfers between devices: none -> 4.58 us  [forward(): lax.ppermute(onward, ('core', 'x'), [(c * 4 + i, c * 4 + (i + (1, 3)[c])...]
    ppermute x3 -> x2, waiting for transfers between devices: 11.2 us -> 6.91 us  [turn(): return lax.ppermute(array, 'x', [(i, (i + step) % 4) for i in range(4)])]
    ppermute x8, starting transfers between devices: 27.9 us -> 24.4 us  [swap(): return lax.ppermute(array, axis, [(0, 1), (1, 0)])]
    all_to_all x4, starting transfers between devices: 32.4 us -> 34.9 us  [exchange(): return lax.all_to_all(array, axes, 0, 0, tiled=True)]
    ppermute x3 -> x2, starting transfers between devices: 8.5 us -> 6.49 us  [turn(): return lax.ppermute(array, 'x', [(i, (i + step) % 4) for i in range(4)])]
    ppermute x0 -> x1, waiting for transfers between devices: none -> 1.74 us  [forward(): lax.ppermute(onward, ('core', 'x'), [(c * 4 + i, c * 4 + (i + (1, 3)[c])...]
  transfers between devices with their start and end apart: 16 -> 16, of which waited for: 6 -> 6; matrix products, arithmetic and copies ran while one was open for 1% -> 2% of each run, Pallas kernels for 15% -> 15%
where the time goes in v6:
time: 153 us; the launch traced here: 152 us
  starting transfers between devices  72.7 us (48%)
  waiting for transfers between devices  39.8 us (26%)
  Pallas kernels  29.8 us (19%)
  local copies, waits for them, and re-layouts  5.68 us (4%)
  other arithmetic  2.42 us (2%)
  between operations  1.59 us (1%)
    all_to_all x4, starting transfers between devices, exchange(): return lax.all_to_all(array, axes, 0, 0, tiled=True)  34.9 us
    ppermute x8, starting transfers between devices, swap(): return lax.ppermute(array, axis, [(0, 1), (1, 0)])  24.4 us
    ppermute x8, waiting for transfers between devices, swap(): return lax.ppermute(array, axis, [(0, 1), (1, 0)])  20.7 us
    all_to_all x4, waiting for transfers between devices, exchange(): return lax.all_to_all(array, axes, 0, 0, tiled=True)  10.4 us
    pallas_call x2, Pallas kernels, attend(): pl.pallas_call(functools.partial(attend_body, scaled), out_shape=tuple((j...  8.64 us
    ppermute x2, waiting for transfers between devices, turn(): return lax.ppermute(array, 'x', [(i, (i + step) % 4) for i in range(4)])  6.91 us
    pallas_call x1, Pallas kernels, grad(): pl.pallas_call(grad_body, out_shape=jax.ShapeDtypeStruct((32, 64), jnp.fl...  6.69 us
    ppermute x2, starting transfers between devices, turn(): return lax.ppermute(array, 'x', [(i, (i + step) % 4) for i in range(4)])  6.49 us
  transfers between devices with their start and end apart: 16, of which 6 were waited for; matrix products, arithmetic and copies ran while one was open for 2% of the time, Pallas kernels for 15%

profile of v6, /device:TPU:1, one launch (start us, length us, event | category | flops | bytes accessed | tf_op | source)
XLA Modules:
  0.0 151.9 jit_solution(6663513965027543436)
XLA Ops:
  2.6 7.8 %all-to-all-start = ((bf16[8,64,512]{2,1,0:T(8,128)(2,1)}), bf16[8,64,512]{2,1,0:T(8,128)(2,1)S(1)}, u32[]{:S(2)}, u32[]{:S(2)}) async-start(bf16[8,64,512]{2,1,0:T(8,128)(2,1)} %columns.1), calls=%async_computation | async-start | bytes 1048576 | tf_op jit(solution)/shard_map/all_to_all | solution.py:349
  11.1 1.1 copy-done.3
  12.2 2.6 %prep.1 = (bf16[432,2048]{1,0:T(8,128)(2,1)}, bf16[432,2048]{1,0:T(8,128)(2,1)}) custom-call(s32[2]{0:T(128)S(1)} %pad_add_fusion.place, s32[1]{0:T(128)} %bitcast.18.count, bf16[320,2048]{1,0:T(8,128)(2,1)S(1)} %bitcast.20, bf16[192,2048]{1,0:T(8,128)(2,1)S(1)} %bitcast.27, bf16[16,1024]{1,0:T(8,128)(2,1)S(1)} %bitcast.32), custom_call_target="tpu_custom_call" | custom-call | tf_op jit(solution)/shard_map/prep/pallas_call | solution.py:114
  14.8 4.0 %collective-permute-start.5 = (bf16[432,2048]{1,0:T(8,128)(2,1)}, bf16[432,2048]{1,0:T(8,128)(2,1)}, u32[]{:S(2)}, u32[]{:S(2)}) collective-permute-start(bf16[432,2048]{1,0:T(8,128)(2,1)} %get-tuple-element.11), channel_id=1, source_target_pairs={{0,64},{64,0},{1,65},{65,1},{2,66},{66,2},{3,67},{67,3},{4,68},{68... | collective-permute-start | bytes 5308424 | tf_op jit(solution)/shard_map/ppermute | solution.py:353
  18.8 2.4 %pack.1 = bf16[32,8,2176]{2,1,0:T(8,128)(2,1)} custom-call(s32[2,32]{1,0:T(2,128)S(1)} %bitcast.33, bf16[40,8,2048]{2,1,0:T(8,128)(2,1)} %bitcast.19), custom_call_target="tpu_custom_call" | custom-call | tf_op jit(solution)/shard_map/pack/pallas_call | solution.py:79
  21.3 4.0 %all-to-all-done = bf16[8,64,512]{2,1,0:T(8,128)(2,1)S(1)} async-done(((bf16[8,64,512]{2,1,0:T(8,128)(2,1)}), bf16[8,64,512]{2,1,0:T(8,128)(2,1)S(1)}, u32[]{:S(2)}, u32[]{:S(2)}) %all-to-all-start) | async-done | bytes 524320 | tf_op jit(solution)/shard_map/all_to_all | solution.py:349
  25.3 7.4 %all-to-all-start.1 = ((bf16[32,8,2176]{2,1,0:T(8,128)(2,1)}), bf16[32,8,2176]{2,1,0:T(8,128)(2,1)S(1)}, u32[]{:S(2)}, u32[]{:S(2)}) async-start(bf16[32,8,2176]{2,1,0:T(8,128)(2,1)} %pack.1), calls=%async_computation.1 | async-start | bytes 2228224 | tf_op jit(solution)/shard_map/all_to_all | solution.py:349
  32.7 2.7 %collective-permute-start.3 = (bf16[432,2048]{1,0:T(8,128)(2,1)}, bf16[432,2048]{1,0:T(8,128)(2,1)}, u32[]{:S(2)}, u32[]{:S(2)}) collective-permute-start(bf16[432,2048]{1,0:T(8,128)(2,1)} %get-tuple-element.8.message.m0), channel_id=1, source_target_pairs={{0,32},{32,0},{1,33},{33,1},{2,34},{34,2},{3,35},{35,3},{4,36},{36... | collective-permute-start | bytes 5308424 | tf_op jit(solution)/shard_map/ppermute | solution.py:353
  35.4 20.7 %collective-permute-done.5.x0.m0.m2 = bf16[432,2048]{1,0:T(8,128)(2,1)} collective-permute-done((bf16[432,2048]{1,0:T(8,128)(2,1)}, bf16[432,2048]{1,0:T(8,128)(2,1)}, u32[]{:S(2)}, u32[]{:S(2)}) %collective-permute-start.5) | collective-permute-done | bytes 1769504 | tf_op jit(solution)/shard_map/ppermute | solution.py:353
  56.1 4.5 %collective-permute-start.6 = (bf16[432,2048]{1,0:T(8,128)(2,1)}, bf16[432,2048]{1,0:T(8,128)(2,1)}, u32[]{:S(2)}, u32[]{:S(2)}) collective-permute-start(bf16[432,2048]{1,0:T(8,128)(2,1)} %collective-permute-done.5.x0.m0.m2), channel_id=1, source_target_pairs={{0,32},{32,0},{1,33},{33,1},{2,34},{34,2},{3,35},{35,3},{4,36},{36... | collective-permute-start | bytes 5308424 | tf_op jit(solution)/shard_map/ppermute | solution.py:353
  60.6 3.1 %collective-permute-start = (bf16[512,512]{1,0:T(8,128)(2,1)S(1)}, bf16[512,512]{1,0:T(8,128)(2,1)S(1)}, u32[]{:S(2)}, u32[]{:S(2)}) collective-permute-start(bf16[512,512]{1,0:T(8,128)(2,1)S(1)} %bitcast.21), channel_id=1, source_target_pairs={{0,8},{8,16},{16,24},{24,0},{1,9},{9,17},{17,25},{25,1},{2,10},{10... | collective-permute-start | bytes 1572872 | tf_op jit(solution)/shard_map/ppermute | solution.py:357
  63.7 3.4 %collective-permute-start.1 = (bf16[512,512]{1,0:T(8,128)(2,1)S(1)}, bf16[512,512]{1,0:T(8,128)(2,1)}, u32[]{:S(2)}, u32[]{:S(2)}) collective-permute-start(bf16[512,512]{1,0:T(8,128)(2,1)S(1)} %bitcast.22), channel_id=1, source_target_pairs={{0,24},{8,0},{16,8},{24,16},{1,25},{9,1},{17,9},{25,17},{2,26},{10... | collective-permute-start | bytes 1572872 | tf_op jit(solution)/shard_map/ppermute | solution.py:357
  68.6 3.4 %collective-permute-start.10 = (bf16[128,2048]{1,0:T(8,128)(2,1)S(1)}, bf16[128,2048]{1,0:T(8,128)(2,1)}, u32[]{:S(2)}, u32[]{:S(2)}) collective-permute-start(bf16[128,2048]{1,0:T(8,128)(2,1)S(1)} %bitcast.24), channel_id=1, source_target_pairs={{0,64},{64,0},{1,65},{65,1},{2,66},{66,2},{3,67},{67,3},{4,68},{68... | collective-permute-start | bytes 1572872 | tf_op jit(solution)/shard_map/ppermute | solution.py:353
  72.0 5.2 %collective-permute-done.left = bf16[512,512]{1,0:T(8,128)(2,1)S(1)} collective-permute-done((bf16[512,512]{1,0:T(8,128)(2,1)S(1)}, bf16[512,512]{1,0:T(8,128)(2,1)S(1)}, u32[]{:S(2)}, u32[]{:S(2)}) %collective-permute-start) | collective-permute-done | bytes 524320 | tf_op jit(solution)/shard_map/ppermute | solution.py:357
  77.2 1.7 %collective-permute-done.1.right = bf16[512,512]{1,0:T(8,128)(2,1)} collective-permute-done((bf16[512,512]{1,0:T(8,128)(2,1)S(1)}, bf16[512,512]{1,0:T(8,128)(2,1)}, u32[]{:S(2)}, u32[]{:S(2)}) %collective-permute-start.1) | collective-permute-done | bytes 524320 | tf_op jit(solution)/shard_map/ppermute | solution.py:357
  78.9 1.1 broadcast_select_fusion
  80.0 4.6 %collective-permute-start.2 = (bf16[512,512]{1,0:T(8,128)(2,1)S(1)}, bf16[512,512]{1,0:T(8,128)(2,1)S(1)}, u32[]{:S(2)}, u32[]{:S(2)}) collective-permute-start(bf16[512,512]{1,0:T(8,128)(2,1)S(1)} %broadcast_select_fusion), channel_id=1, source_target_pairs={{0,8},{8,16},{16,24},{24,0},{32,56},{40,32},{48,40},{56,48},{1,9},... | collective-permute-start | bytes 1572872 | tf_op jit(solution)/shard_map/ppermute | solution.py:389
  84.6 1.9 %collective-permute-start.9 = (bf16[128,2048]{1,0:T(8,128)(2,1)S(1)}, bf16[128,2048]{1,0:T(8,128)(2,1)}, u32[]{:S(2)}, u32[]{:S(2)}) collective-permute-start(bf16[128,2048]{1,0:T(8,128)(2,1)S(1)} %bitcast.25), channel_id=1, source_target_pairs={{0,32},{32,0},{1,33},{33,1},{2,34},{34,2},{3,35},{35,3},{4,36},{36... | collective-permute-start | bytes 1572872 | tf_op jit(solution)/shard_map/ppermute | solution.py:353
  86.5 2.4 %collective-permute-start.11 = (bf16[128,2048]{1,0:T(8,128)(2,1)}, bf16[128,2048]{1,0:T(8,128)(2,1)}, u32[]{:S(2)}, u32[]{:S(2)}) collective-permute-start(bf16[128,2048]{1,0:T(8,128)(2,1)} %collective-permute-done.10.h2), channel_id=1, source_target_pairs={{0,32},{32,0},{1,33},{33,1},{2,34},{34,2},{3,35},{35,3},{4,36},{36... | collective-permute-start | bytes 1572872 | tf_op jit(solution)/shard_map/ppermute | solution.py:353
  89.0 1.7 %collective-permute-done.2.far = bf16[512,512]{1,0:T(8,128)(2,1)S(1)} collective-permute-done((bf16[512,512]{1,0:T(8,128)(2,1)S(1)}, bf16[512,512]{1,0:T(8,128)(2,1)S(1)}, u32[]{:S(2)}, u32[]{:S(2)}) %collective-permute-start.2) | collective-permute-done | bytes 524320 | tf_op jit(solution)/shard_map/ppermute | solution.py:389
  93.6 1.2 join_weight.1.weight
  94.8 6.7 %gain_grad.1 = f32[32,64]{1,0:T(8,128)} custom-call(s32[2]{0:T(128)S(1)} %pad_add_fusion.place, bf16[2048,512]{1,0:T(8,128)(2,1)S(1)} %join_weight.1.weight, bf16[432,2048]{1,0:T(8,128)(2,1)} %get-tuple-element.8.message.m0, bf16[432,2048]{1,0:T(8,128)(2,1)} %collective-permute-done.3.message.m1, bf16[432,2048]{1,0:T(8,128)(2,1)} %collective-permute-done.5.x0.m0.m2, ...), custom_call_target="tpu_custom_call" | custom-call | tf_op jit(solution)/shard_map/gain_grad/pallas_call | solution.py:246
  101.5 9.9 %all-to-all-start.2 = ((f32[32,1,64]{2,1,0:T(1,128)}), f32[32,1,64]{2,1,0:T(1,128)S(1)}, u32[]{:S(2)}, u32[]{:S(2)}) async-start(f32[32,1,64]{2,1,0:T(1,128)} %bitcast.15), calls=%async_computation.2 | async-start | bytes 32768 | tf_op jit(solution)/shard_map/all_to_all | solution.py:349
  111.4 3.0 %scale.2.x0 = bf16[320,2048]{1,0:T(8,128)(2,1)} custom-call(bf16[432,2048]{1,0:T(8,128)(2,1)} %get-tuple-element.8.message.m0, f32[1,2048]{1,0:T(1,128)S(1)} %bitcast.28), custom_call_target="tpu_custom_call" | custom-call | tf_op jit(solution)/shard_map/scale/pallas_call | solution.py:197
  114.4 2.9 %scale.3.x1 = bf16[320,2048]{1,0:T(8,128)(2,1)} custom-call(bf16[432,2048]{1,0:T(8,128)(2,1)} %collective-permute-done.3.message.m1, f32[1,2048]{1,0:T(1,128)S(1)} %bitcast.29), custom_call_target="tpu_custom_call" | custom-call | tf_op jit(solution)/shard_map/scale/pallas_call | solution.py:197
  117.3 4.1 %attend.2 = (bf16[16,256]{1,0:T(8,128)(2,1)S(1)}, bf16[16,256]{1,0:T(8,128)(2,1)S(1)}) custom-call(s32[2]{0:T(128)S(1)} %pad_add_fusion.place, f32[1,2048]{1,0:T(1,128)S(1)} %bitcast.30, bf16[2048,512]{1,0:T(8,128)(2,1)S(1)} %join_weight.1.weight, bf16[320,2048]{1,0:T(8,128)(2,1)} %scale.2.x0, bf16[320,2048]{1,0:T(8,128)(2,1)} %scale.3.x1, ...), custom_call_target="tpu_custom_call" | custom-call | tf_op jit(solution)/shard_map/attend/pallas_call | solution.py:311
  121.4 2.2 %collective-permute-start.4 = (bf16[16,256]{1,0:T(8,128)(2,1)S(1)}, bf16[16,256]{1,0:T(8,128)(2,1)S(1)}, u32[]{:S(2)}, u32[]{:S(2)}) collective-permute-start(bf16[16,256]{1,0:T(8,128)(2,1)S(1)} %get-tuple-element.10), channel_id=1, source_target_pairs={{0,32},{32,0},{1,33},{33,1},{2,34},{34,2},{3,35},{35,3},{4,36},{36... | collective-permute-start | bytes 24584 | tf_op jit(solution)/shard_map/ppermute | solution.py:353
  123.6 4.6 %attend.3 = (bf16[16,256]{1,0:T(8,128)(2,1)S(1)}, bf16[16,256]{1,0:T(8,128)(2,1)S(1)}) custom-call(s32[2]{0:T(128)S(1)} %pad_add_fusion.place, f32[1,2048]{1,0:T(1,128)S(1)} %bitcast.31, bf16[2048,512]{1,0:T(8,128)(2,1)S(1)} %join_weight.1.weight, bf16[432,2048]{1,0:T(8,128)(2,1)} %collective-permute-done.5.x0.m0.m2, ...), custom_call_target="tpu_custom_call" | custom-call | tf_op jit(solution)/shard_map/attend/pallas_call | solution.py:311
  128.2 3.4 %collective-permute-start.7 = (bf16[16,256]{1,0:T(8,128)(2,1)S(1)}, bf16[16,256]{1,0:T(8,128)(2,1)S(1)}, u32[]{:S(2)}, u32[]{:S(2)}) collective-permute-start(bf16[16,256]{1,0:T(8,128)(2,1)S(1)} %get-tuple-element.12), channel_id=1, source_target_pairs={{0,64},{64,0},{1,65},{65,1},{2,66},{66,2},{3,67},{67,3},{4,68},{68... | collective-permute-start | bytes 24584 | tf_op jit(solution)/shard_map/ppermute | solution.py:353
  131.6 2.3 %collective-permute-start.8 = (bf16[16,256]{1,0:T(8,128)(2,1)S(1)}, bf16[16,256]{1,0:T(8,128)(2,1)S(1)}, u32[]{:S(2)}, u32[]{:S(2)}) collective-permute-start(bf16[16,256]{1,0:T(8,128)(2,1)S(1)} %get-tuple-element.13), channel_id=1, source_target_pairs={{0,96},{32,64},{64,32},{96,0},{1,97},{33,65},{65,33},{97,1},{2,98}... | collective-permute-start | bytes 24584 | tf_op jit(solution)/shard_map/ppermute | solution.py:406
  134.5 9.8 %all-to-all-start.3 = ((f32[16,1,64]{2,1,0:T(1,128)}), f32[16,1,64]{2,1,0:T(1,128)S(1)}, u32[]{:S(2)}, u32[]{:S(2)}) async-start(f32[16,1,64]{2,1,0:T(1,128)} %broadcast_in_dim.2), calls=%async_computation.3 | async-start | bytes 16384 | tf_op jit(solution)/shard_map/all_to_all | solution.py:349
  145.0 6.4 %all-to-all-done.3 = f32[16,1,64]{2,1,0:T(1,128)S(1)} async-done(((f32[16,1,64]{2,1,0:T(1,128)}), f32[16,1,64]{2,1,0:T(1,128)S(1)}, u32[]{:S(2)}, u32[]{:S(2)}) %all-to-all-start.3) | async-done | bytes 4128 | tf_op jit(solution)/shard_map/all_to_all | solution.py:349
  (37 shorter events, 8.2 us)
Async XLA Ops:
  0.6 10.4 %copy-start = (bf16[1,1,40,8,2048]{4,3,2,1,0:T(8,128)(2,1)S(1)}, bf16[1,1,40,8,2048]{4,3,2,1,0:T(8,128)(2,1)}, u32[]{:S(2)}) copy-start(bf16[1,1,40,8,2048]{4,3,2,1,0:T(8,128)(2,1)} %param.7) | copy-start | bytes 3932164
  0.7 1.1 copy-start.6
  1.7 9.4 %copy-start.8 = (bf16[1,1,16,1024]{3,2,1,0:T(8,128)(2,1)S(1)}, bf16[1,1,16,1024]{3,2,1,0:T(8,128)(2,1)}, u32[]{:S(2)}) copy-start(bf16[1,1,16,1024]{3,2,1,0:T(8,128)(2,1)} %param.12) | copy-start | bytes 98308
  2.6 16.3 %copy-start.9 = (s32[1,1,2,32]{3,2,1,0:T(2,128)S(1)}, s32[1,1,2,32]{3,2,1,0:T(2,128)}, u32[]{:S(2)}) copy-start(s32[1,1,2,32]{3,2,1,0:T(2,128)} %param.9) | copy-start | bytes 772
  2.6 22.7 %all-to-all-start = ((bf16[8,64,512]{2,1,0:T(8,128)(2,1)}), bf16[8,64,512]{2,1,0:T(8,128)(2,1)S(1)}, u32[]{:S(2)}, u32[]{:S(2)}) async-start(bf16[8,64,512]{2,1,0:T(8,128)(2,1)} %columns.1), calls=%async_computation | async-start | bytes 1048576 | tf_op jit(solution)/shard_map/all_to_all | solution.py:349
  11.1 1.1 copy-start.3
  14.8 41.3 %collective-permute-start.5 = (bf16[432,2048]{1,0:T(8,128)(2,1)}, bf16[432,2048]{1,0:T(8,128)(2,1)}, u32[]{:S(2)}, u32[]{:S(2)}) collective-permute-start(bf16[432,2048]{1,0:T(8,128)(2,1)} %get-tuple-element.11), channel_id=1, source_target_pairs={{0,64},{64,0},{1,65},{65,1},{2,66},{66,2},{3,67},{67,3},{4,68},{68... | collective-permute-start | bytes 5308424 | tf_op jit(solution)/shard_map/ppermute | solution.py:353
  25.3 41.8 %all-to-all-start.1 = ((bf16[32,8,2176]{2,1,0:T(8,128)(2,1)}), bf16[32,8,2176]{2,1,0:T(8,128)(2,1)S(1)}, u32[]{:S(2)}, u32[]{:S(2)}) async-start(bf16[32,8,2176]{2,1,0:T(8,128)(2,1)} %pack.1), calls=%async_computation.1 | async-start | bytes 2228224 | tf_op jit(solution)/shard_map/all_to_all | solution.py:349
  32.7 62.1 %collective-permute-start.3 = (bf16[432,2048]{1,0:T(8,128)(2,1)}, bf16[432,2048]{1,0:T(8,128)(2,1)}, u32[]{:S(2)}, u32[]{:S(2)}) collective-permute-start(bf16[432,2048]{1,0:T(8,128)(2,1)} %get-tuple-element.8.message.m0), channel_id=1, source_target_pairs={{0,32},{32,0},{1,33},{33,1},{2,34},{34,2},{3,35},{35,3},{4,36},{36... | collective-permute-start | bytes 5308424 | tf_op jit(solution)/shard_map/ppermute | solution.py:353
  56.1 38.7 %collective-permute-start.6 = (bf16[432,2048]{1,0:T(8,128)(2,1)}, bf16[432,2048]{1,0:T(8,128)(2,1)}, u32[]{:S(2)}, u32[]{:S(2)}) collective-permute-start(bf16[432,2048]{1,0:T(8,128)(2,1)} %collective-permute-done.5.x0.m0.m2), channel_id=1, source_target_pairs={{0,32},{32,0},{1,33},{33,1},{2,34},{34,2},{3,35},{35,3},{4,36},{36... | collective-permute-start | bytes 5308424 | tf_op jit(solution)/shard_map/ppermute | solution.py:353
  60.6 16.6 %collective-permute-start = (bf16[512,512]{1,0:T(8,128)(2,1)S(1)}, bf16[512,512]{1,0:T(8,128)(2,1)S(1)}, u32[]{:S(2)}, u32[]{:S(2)}) collective-permute-start(bf16[512,512]{1,0:T(8,128)(2,1)S(1)} %bitcast.21), channel_id=1, source_target_pairs={{0,8},{8,16},{16,24},{24,0},{1,9},{9,17},{17,25},{25,1},{2,10},{10... | collective-permute-start | bytes 1572872 | tf_op jit(solution)/shard_map/ppermute | solution.py:357
  63.7 15.2 %collective-permute-start.1 = (bf16[512,512]{1,0:T(8,128)(2,1)S(1)}, bf16[512,512]{1,0:T(8,128)(2,1)}, u32[]{:S(2)}, u32[]{:S(2)}) collective-permute-start(bf16[512,512]{1,0:T(8,128)(2,1)S(1)} %bitcast.22), channel_id=1, source_target_pairs={{0,24},{8,0},{16,8},{24,16},{1,25},{9,1},{17,9},{25,17},{2,26},{10... | collective-permute-start | bytes 1572872 | tf_op jit(solution)/shard_map/ppermute | solution.py:357
  68.6 17.9 %collective-permute-start.10 = (bf16[128,2048]{1,0:T(8,128)(2,1)S(1)}, bf16[128,2048]{1,0:T(8,128)(2,1)}, u32[]{:S(2)}, u32[]{:S(2)}) collective-permute-start(bf16[128,2048]{1,0:T(8,128)(2,1)S(1)} %bitcast.24), channel_id=1, source_target_pairs={{0,64},{64,0},{1,65},{65,1},{2,66},{66,2},{3,67},{67,3},{4,68},{68... | collective-permute-start | bytes 1572872 | tf_op jit(solution)/shard_map/ppermute | solution.py:353
  77.2 13.5 %copy-start.1 = (bf16[512,512]{1,0:T(8,128)(2,1)}, bf16[512,512]{1,0:T(8,128)(2,1)S(1)}, u32[]{:S(2)}) copy-start(bf16[512,512]{1,0:T(8,128)(2,1)S(1)} %collective-permute-done.left) | copy-start | bytes 1572868
  80.0 10.7 %collective-permute-start.2 = (bf16[512,512]{1,0:T(8,128)(2,1)S(1)}, bf16[512,512]{1,0:T(8,128)(2,1)S(1)}, u32[]{:S(2)}, u32[]{:S(2)}) collective-permute-start(bf16[512,512]{1,0:T(8,128)(2,1)S(1)} %broadcast_select_fusion), channel_id=1, source_target_pairs={{0,8},{8,16},{16,24},{24,0},{32,56},{40,32},{48,40},{56,48},{1,9},... | collective-permute-start | bytes 1572872 | tf_op jit(solution)/shard_map/ppermute | solution.py:389
  84.6 10.2 %collective-permute-start.9 = (bf16[128,2048]{1,0:T(8,128)(2,1)S(1)}, bf16[128,2048]{1,0:T(8,128)(2,1)}, u32[]{:S(2)}, u32[]{:S(2)}) collective-permute-start(bf16[128,2048]{1,0:T(8,128)(2,1)S(1)} %bitcast.25), channel_id=1, source_target_pairs={{0,32},{32,0},{1,33},{33,1},{2,34},{34,2},{3,35},{35,3},{4,36},{36... | collective-permute-start | bytes 1572872 | tf_op jit(solution)/shard_map/ppermute | solution.py:353
  86.5 8.3 %collective-permute-start.11 = (bf16[128,2048]{1,0:T(8,128)(2,1)}, bf16[128,2048]{1,0:T(8,128)(2,1)}, u32[]{:S(2)}, u32[]{:S(2)}) collective-permute-start(bf16[128,2048]{1,0:T(8,128)(2,1)} %collective-permute-done.10.h2), channel_id=1, source_target_pairs={{0,32},{32,0},{1,33},{33,1},{2,34},{34,2},{3,35},{35,3},{4,36},{36... | collective-permute-start | bytes 1572872 | tf_op jit(solution)/shard_map/ppermute | solution.py:353
  90.7 0.8 copy-start.4
  91.5 1.0 copy-start.2
  92.5 1.0 copy-start.5
  94.8 16.6 %copy-start.7 = (f32[2048]{0:T(1024)S(1)}, f32[2048]{0:T(1024)}, u32[]{:S(2)}) copy-start(f32[2048]{0:T(1024)} %param.10) | copy-start | bytes 24580
  101.5 32.4 %all-to-all-start.2 = ((f32[32,1,64]{2,1,0:T(1,128)}), f32[32,1,64]{2,1,0:T(1,128)S(1)}, u32[]{:S(2)}, u32[]{:S(2)}) async-start(f32[32,1,64]{2,1,0:T(1,128)} %bitcast.15), calls=%async_computation.2 | async-start | bytes 32768 | tf_op jit(solution)/shard_map/all_to_all | solution.py:349
  121.4 23.0 %collective-permute-start.4 = (bf16[16,256]{1,0:T(8,128)(2,1)S(1)}, bf16[16,256]{1,0:T(8,128)(2,1)S(1)}, u32[]{:S(2)}, u32[]{:S(2)}) collective-permute-start(bf16[16,256]{1,0:T(8,128)(2,1)S(1)} %get-tuple-element.10), channel_id=1, source_target_pairs={{0,32},{32,0},{1,33},{33,1},{2,34},{34,2},{3,35},{35,3},{4,36},{36... | collective-permute-start | bytes 24584 | tf_op jit(solution)/shard_map/ppermute | solution.py:353
  128.2 16.1 %collective-permute-start.7 = (bf16[16,256]{1,0:T(8,128)(2,1)S(1)}, bf16[16,256]{1,0:T(8,128)(2,1)S(1)}, u32[]{:S(2)}, u32[]{:S(2)}) collective-permute-start(bf16[16,256]{1,0:T(8,128)(2,1)S(1)} %get-tuple-element.12), channel_id=1, source_target_pairs={{0,64},{64,0},{1,65},{65,1},{2,66},{66,2},{3,67},{67,3},{4,68},{68... | collective-permute-start | bytes 24584 | tf_op jit(solution)/shard_map/ppermute | solution.py:353
  131.6 12.8 %collective-permute-start.8 = (bf16[16,256]{1,0:T(8,128)(2,1)S(1)}, bf16[16,256]{1,0:T(8,128)(2,1)S(1)}, u32[]{:S(2)}, u32[]{:S(2)}) collective-permute-start(bf16[16,256]{1,0:T(8,128)(2,1)S(1)} %get-tuple-element.13), channel_id=1, source_target_pairs={{0,96},{32,64},{64,32},{96,0},{1,97},{33,65},{65,33},{97,1},{2,98}... | collective-permute-start | bytes 24584 | tf_op jit(solution)/shard_map/ppermute | solution.py:406
  134.5 16.9 %all-to-all-start.3 = ((f32[16,1,64]{2,1,0:T(1,128)}), f32[16,1,64]{2,1,0:T(1,128)S(1)}, u32[]{:S(2)}, u32[]{:S(2)}) async-start(f32[16,1,64]{2,1,0:T(1,128)} %broadcast_in_dim.2), calls=%async_computation.3 | async-start | bytes 16384 | tf_op jit(solution)/shard_map/all_to_all | solution.py:349
